TPU v7x, 8 devices: a whole 2x2x1 slice. The times are simulated.
8 devices in a mesh: dp: 1 (over z), pz: 2 (over y), py: 2 (over x), px: 2 (over core).
Axes of the slice: x: 2, y: 2, z: 1, core: 2. Of those that a mesh axis runs over, the one named last changes fastest.
Arguments:
- volumes: bfloat16 [2, 32, 128, 128, 128], P('dp', None, 'px', 'py', 'pz')
- filter_taps: float32 [3, 3, 25], replicated
- mix_weight: bfloat16 [3, 32, 32], replicated
- mix_bias: float32 [3, 32], replicated
Outputs:
- output: bfloat16 [2, 32, 128, 128, 128], P('dp', None, 'px', 'py', 'pz')
All inputs are finite; a program needn't handle non-finite values.
Results may differ from a plain program's by a relative error of at most 0.00543444.
Values are sent between devices in bfloat16 or wider.
A program may use at most 1 GiB of HBM per device.

v0:
```python
import jax
import jax.numpy as jnp
from jax import lax
from jax.sharding import PartitionSpec as P

PASS_FORMS = ('vcsyz,si->vciyz', 'vcxsz,si->vcxiz', 'vcxys,si->vcxyi')
GRID_AXES = ((2, 'px'), (3, 'py'), (4, 'pz'))


def band_matrix(tap_row, out_len):
    tap_count = tap_row.shape[0]
    tap_index = jnp.arange(out_len + tap_count - 1)[:, None] - jnp.arange(out_len)[None, :]
    inside = (tap_index >= 0) & (tap_index < tap_count)
    picked = tap_row[jnp.clip(tap_index, 0, tap_count - 1)]
    return jnp.where(inside, picked, 0.0).astype(jnp.bfloat16)


def neighbour_planes(block, plane_count, axis_dim, axis_name, axis_size):
    if axis_size == 1:
        zero_shape = block.shape[:axis_dim] + (plane_count,) + block.shape[axis_dim + 1:]
        zero_planes = jnp.zeros(zero_shape, block.dtype)
        return zero_planes, zero_planes
    extent = block.shape[axis_dim]
    low_planes = lax.slice_in_dim(block, 0, plane_count, axis=axis_dim)
    high_planes = lax.slice_in_dim(block, extent - plane_count, extent, axis=axis_dim)
    upward = [(source, source + 1) for source in range(axis_size - 1)]
    downward = [(source + 1, source) for source in range(axis_size - 1)]
    from_lower = lax.ppermute(high_planes, axis_name, upward)
    from_upper = lax.ppermute(low_planes, axis_name, downward)
    return from_lower, from_upper


def solution(mesh):
    axis_sizes = {'px': mesh.shape['px'], 'py': mesh.shape['py'], 'pz': mesh.shape['pz']}
    vol_spec = P('dp', None, 'px', 'py', 'pz')

    def local_layers(vol_block, filter_taps, mix_weight, mix_bias):
        half_width = (filter_taps.shape[2] - 1) // 2
        vol_state = vol_block
        for layer_idx in range(filter_taps.shape[0]):
            current = vol_state
            for pass_idx in range(3):
                axis_dim, axis_name = GRID_AXES[pass_idx]
                from_lower, from_upper = neighbour_planes(current, half_width, axis_dim, axis_name, axis_sizes[axis_name])
                padded = jnp.concatenate([from_lower, current, from_upper], axis=axis_dim)
                matrix = band_matrix(filter_taps[layer_idx, pass_idx], current.shape[axis_dim])
                current = jnp.einsum(PASS_FORMS[pass_idx], padded, matrix, preferred_element_type=jnp.float32).astype(jnp.bfloat16)
            mix_out = jnp.einsum('cd,vcxyz->vdxyz', mix_weight[layer_idx], current, preferred_element_type=jnp.float32)
            activated = jax.nn.gelu(mix_out + mix_bias[layer_idx][None, :, None, None, None], approximate=True)
            vol_state = (vol_state.astype(jnp.float32) + activated).astype(jnp.bfloat16)
        return vol_state

    return jax.shard_map(local_layers, mesh=mesh, in_specs=(vol_spec, P(), P(), P()), out_specs=vol_spec, check_vma=False)
```

profile of v0, /device:TPU:1, one launch (start us, length us, event | category | flops | bytes accessed | tf_op | source)
XLA Modules:
  0.0 3990.2 jit_solution(2783473951208736300)
XLA Ops:
  35.0 93.0 %copy.78 = bf16[2,32,64,64,64]{2,4,3,1,0:T(8,128)(2,1)} copy(bf16[2,32,64,64,64]{4,3,2,1,0:T(8,128)(2,1)} %param.4) | data formatting | bytes 67108864 | tf_op args[0]
  160.5 54.1 %copy.77 = bf16[2,32,12,64,64]{2,4,3,1,0:T(8,128)(2,1)} copy(bf16[2,32,12,64,64]{4,3,2,1,0:T(8,128)(2,1)} %collective-permute-done) | data formatting | bytes 12582912 | tf_op jit(solution)/shard_map/ppermute | solution.py:28
  214.7 53.9 %copy.79 = bf16[2,32,12,64,64]{2,4,3,1,0:T(8,128)(2,1)} copy(bf16[2,32,12,64,64]{4,3,2,1,0:T(8,128)(2,1)} %collective-permute-done.1) | data formatting | bytes 12582912 | tf_op jit(solution)/shard_map/ppermute | solution.py:29
  268.6 99.8 %convert_bitcast_fusion.5 = bf16[2,32,64,64,64]{4,2,3,1,0:T(8,128)(2,1)} fusion(bf16[2,32,12,64,64]{2,4,3,1,0:T(8,128)(2,1)} %copy.79, bf16[2,32,64,64,64]{2,4,3,1,0:T(8,128)(2,1)} %copy.78, bf16[2,32,12,64,64]{2,4,3,1,0:T(8,128)(2,1)} %copy.77, bf16[88,64]{0,1:T(8,128)(2,1)S(1)} %copy.76), kind=kOutput, calls=%fused_computation.74 | convolution fusion | flops 3108007424 | bytes 79703040 | tf_op jit(solution)/shard_map/vcsyz,si->vciyz/dot_general | solution.py:47
  400.0 31.6 gather_fusion
  431.7 227.7 %collective-permute-done.2 = bf16[2,32,64,12,64]{4,2,3,1,0:T(8,128)(2,1)} collective-permute-done((bf16[2,32,64,12,64]{4,2,3,1,0:T(8,128)(2,1)}, bf16[2,32,64,12,64]{4,2,3,1,0:T(8,128)(2,1)}, u32[]{:S(2)}, u32[]{:S(2)}) %collective-permute-start.2) | collective-permute-done | bytes 6291488 | tf_op jit(solution)/shard_map/ppermute | solution.py:28
  668.0 61.4 %pad_maximum_fusion = bf16[2,32,64,88,64]{4,2,3,1,0:T(8,128)(2,1)} fusion(bf16[2,32,64,12,64]{4,2,3,1,0:T(8,128)(2,1)} %collective-permute-done.3, bf16[2,32,64,64,64]{4,2,3,1,0:T(8,128)(2,1)} %convert_bitcast_fusion.5, bf16[2,32,64,12,64]{4,2,3,1,0:T(8,128)(2,1)} %collective-permute-done.2), kind=kLoop, calls=%fused_computation.39 | loop fusion | flops 46137344 | bytes 92274688 | tf_op jit(solution)/shard_map/concatenate | solution.py:45
  729.4 86.6 %convert_bitcast_fusion.4 = bf16[2,32,64,64,64]{3,4,2,1,0:T(8,128)(2,1)} fusion(bf16[2,32,64,88,64]{4,2,3,1,0:T(8,128)(2,1)} %pad_maximum_fusion, bf16[88,64]{0,1:T(8,128)(2,1)S(1)} %copy.75), kind=kOutput, calls=%fused_computation.73 | convolution fusion | flops 2969595392 | bytes 79703040 | tf_op jit(solution)/shard_map/vcxsz,si->vcxiz/dot_general | solution.py:47
  900.4 219.7 %collective-permute-done.4 = bf16[2,32,64,64,12]{3,2,4,1,0:T(8,128)(2,1)} collective-permute-done((bf16[2,32,64,64,12]{3,2,4,1,0:T(8,128)(2,1)}, bf16[2,32,64,64,12]{3,2,4,1,0:T(8,128)(2,1)}, u32[]{:S(2)}, u32[]{:S(2)}) %collective-permute-start.4) | collective-permute-done | bytes 6291488 | tf_op jit(solution)/shard_map/ppermute | solution.py:28
  1153.0 63.2 %pad_maximum_fusion.1 = bf16[2,32,64,64,88]{3,4,2,1,0:T(8,128)(2,1)} fusion(bf16[2,32,64,64,12]{3,4,2,1,0:T(8,128)(2,1)} %copy.84, bf16[2,32,64,64,64]{3,4,2,1,0:T(8,128)(2,1)} %convert_bitcast_fusion.4, bf16[2,32,64,64,12]{3,4,2,1,0:T(8,128)(2,1)} %copy.83), kind=kLoop, calls=%fused_computation.40 | loop fusion | flops 138412032 | bytes 92274688 | tf_op jit(solution)/shard_map/concatenate | solution.py:45
  1216.3 100.3 %copy.86 = bf16[2,32,64,64,88]{4,1,3,2,0:T(8,128)(2,1)} copy(bf16[2,32,64,64,88]{3,4,2,1,0:T(8,128)(2,1)} %pad_maximum_fusion.1) | data formatting | bytes 92274688 | tf_op jit(solution)/shard_map/concatenate | solution.py:45
  1316.6 88.0 %fusion.8 = bf16[2,32,64,64,64]{4,1,3,2,0:T(8,128)(2,1)} fusion(bf16[2,32,64,64,64]{4,3,2,1,0:T(8,128)(2,1)} %param.4, f32[32]{0:T(128)S(1)} %get-tuple-element.33, bf16[2,32,64,64,88]{4,1,3,2,0:T(8,128)(2,1)} %copy.86, bf16[88,64]{0,1:T(8,128)(2,1)S(1)} %copy.85, bf16[3,32,32]{2,1,0:T(8,128)(2,1)} %param.6), kind=kOutput, calls=%fused_computation.20 | convolution fusion | flops 4244663808 | bytes 167791744 | tf_op jit(solution)/shard_map/cd,vcxyz->vdxyz/dot_general | solution.py:48
  1468.3 62.2 %pad_maximum_fusion.2 = bf16[2,32,88,64,64]{4,1,3,2,0:T(8,128)(2,1)} fusion(bf16[2,32,12,64,64]{4,1,3,2,0:T(8,128)(2,1)} %collective-permute-done.7, bf16[2,32,64,64,64]{4,1,3,2,0:T(8,128)(2,1)} %fusion.8, bf16[2,32,12,64,64]{4,1,3,2,0:T(8,128)(2,1)} %collective-permute-done.6), kind=kLoop, calls=%fused_computation.41 | loop fusion | flops 46137344 | bytes 92274688 | tf_op jit(solution)/shard_map/concatenate | solution.py:45
  1530.5 121.5 %convert_bitcast_fusion.3 = bf16[2,32,64,64,64]{4,2,3,1,0:T(8,128)(2,1)} fusion(bf16[2,32,88,64,64]{4,1,3,2,0:T(8,128)(2,1)} %pad_maximum_fusion.2, bf16[88,64]{0,1:T(8,128)(2,1)S(1)} %copy.89), kind=kOutput, calls=%fused_computation.70 | convolution fusion | flops 2969595392 | bytes 79703040 | tf_op jit(solution)/shard_map/vcsyz,si->vciyz/dot_general | solution.py:47
  1712.6 227.7 %collective-permute-done.8 = bf16[2,32,64,12,64]{4,2,3,1,0:T(8,128)(2,1)} collective-permute-done((bf16[2,32,64,12,64]{4,2,3,1,0:T(8,128)(2,1)}, bf16[2,32,64,12,64]{4,2,3,1,0:T(8,128)(2,1)}, u32[]{:S(2)}, u32[]{:S(2)}) %collective-permute-start.8) | collective-permute-done | bytes 6291488 | tf_op jit(solution)/shard_map/ppermute | solution.py:28
  1948.9 61.4 %pad_maximum_fusion.3 = bf16[2,32,64,88,64]{4,2,3,1,0:T(8,128)(2,1)} fusion(bf16[2,32,64,12,64]{4,2,3,1,0:T(8,128)(2,1)} %collective-permute-done.9, bf16[2,32,64,64,64]{4,2,3,1,0:T(8,128)(2,1)} %convert_bitcast_fusion.3, bf16[2,32,64,12,64]{4,2,3,1,0:T(8,128)(2,1)} %collective-permute-done.8), kind=kLoop, calls=%fused_computation.42 | loop fusion | flops 46137344 | bytes 92274688 | tf_op jit(solution)/shard_map/concatenate | solution.py:45
  2010.3 86.6 %convert_bitcast_fusion.2 = bf16[2,32,64,64,64]{3,4,2,1,0:T(8,128)(2,1)} fusion(bf16[2,32,64,88,64]{4,2,3,1,0:T(8,128)(2,1)} %pad_maximum_fusion.3, bf16[88,64]{0,1:T(8,128)(2,1)S(1)} %copy.88), kind=kOutput, calls=%fused_computation.69 | convolution fusion | flops 2969595392 | bytes 79703040 | tf_op jit(solution)/shard_map/vcxsz,si->vcxiz/dot_general | solution.py:47
  2147.3 31.6 gather_fusion.5
  2179.0 220.1 %collective-permute-done.10 = bf16[2,32,64,64,12]{3,2,4,1,0:T(8,128)(2,1)} collective-permute-done((bf16[2,32,64,64,12]{3,2,4,1,0:T(8,128)(2,1)}, bf16[2,32,64,64,12]{3,2,4,1,0:T(8,128)(2,1)}, u32[]{:S(2)}, u32[]{:S(2)}) %collective-permute-start.10) | collective-permute-done | bytes 6291488 | tf_op jit(solution)/shard_map/ppermute | solution.py:28
  2432.0 63.2 %pad_maximum_fusion.4 = bf16[2,32,64,64,88]{3,4,2,1,0:T(8,128)(2,1)} fusion(bf16[2,32,64,64,12]{3,4,2,1,0:T(8,128)(2,1)} %copy.95, bf16[2,32,64,64,64]{3,4,2,1,0:T(8,128)(2,1)} %convert_bitcast_fusion.2, bf16[2,32,64,64,12]{3,4,2,1,0:T(8,128)(2,1)} %copy.94), kind=kLoop, calls=%fused_computation.43 | loop fusion | flops 138412032 | bytes 92274688 | tf_op jit(solution)/shard_map/concatenate | solution.py:45
  2495.3 100.3 %copy.97 = bf16[2,32,64,64,88]{4,1,3,2,0:T(8,128)(2,1)} copy(bf16[2,32,64,64,88]{3,4,2,1,0:T(8,128)(2,1)} %pad_maximum_fusion.4) | data formatting | bytes 92274688 | tf_op jit(solution)/shard_map/concatenate | solution.py:45
  2595.6 79.0 %fusion.17 = bf16[2,32,64,64,64]{4,1,3,2,0:T(8,128)(2,1)} fusion(bf16[2,32,64,64,64]{4,1,3,2,0:T(8,128)(2,1)} %fusion.8, f32[32]{0:T(128)S(1)} %copy-done.13, bf16[2,32,64,64,88]{4,1,3,2,0:T(8,128)(2,1)} %copy.97, bf16[88,64]{0,1:T(8,128)(2,1)S(1)} %copy.96, bf16[3,32,32]{2,1,0:T(8,128)(2,1)} %param.6), kind=kOutput, calls=%fused_computation.29 | convolution fusion | flops 4244663808 | bytes 167791744 | tf_op jit(solution)/shard_map/cd,vcxyz->vdxyz/dot_general | solution.py:48
  2738.3 62.2 %pad_maximum_fusion.5 = bf16[2,32,88,64,64]{4,1,3,2,0:T(8,128)(2,1)} fusion(bf16[2,32,12,64,64]{4,1,3,2,0:T(8,128)(2,1)} %collective-permute-done.13, bf16[2,32,64,64,64]{4,1,3,2,0:T(8,128)(2,1)} %fusion.17, bf16[2,32,12,64,64]{4,1,3,2,0:T(8,128)(2,1)} %collective-permute-done.12), kind=kLoop, calls=%fused_computation.44 | loop fusion | flops 46137344 | bytes 92274688 | tf_op jit(solution)/shard_map/concatenate | solution.py:45
  2800.4 121.5 %convert_bitcast_fusion.1 = bf16[2,32,64,64,64]{4,2,3,1,0:T(8,128)(2,1)} fusion(bf16[2,32,88,64,64]{4,1,3,2,0:T(8,128)(2,1)} %pad_maximum_fusion.5, bf16[88,64]{0,1:T(8,128)(2,1)S(1)} %copy.100), kind=kOutput, calls=%fused_computation.66 | convolution fusion | flops 2969595392 | bytes 79703040 | tf_op jit(solution)/shard_map/vcsyz,si->vciyz/dot_general | solution.py:47
  2982.6 227.7 %collective-permute-done.14 = bf16[2,32,64,12,64]{4,2,3,1,0:T(8,128)(2,1)} collective-permute-done((bf16[2,32,64,12,64]{4,2,3,1,0:T(8,128)(2,1)}, bf16[2,32,64,12,64]{4,2,3,1,0:T(8,128)(2,1)}, u32[]{:S(2)}, u32[]{:S(2)}) %collective-permute-start.14) | collective-permute-done | bytes 6291488 | tf_op jit(solution)/shard_map/ppermute | solution.py:28
  3218.9 61.4 %pad_maximum_fusion.6 = bf16[2,32,64,88,64]{4,2,3,1,0:T(8,128)(2,1)} fusion(bf16[2,32,64,12,64]{4,2,3,1,0:T(8,128)(2,1)} %collective-permute-done.15, bf16[2,32,64,64,64]{4,2,3,1,0:T(8,128)(2,1)} %convert_bitcast_fusion.1, bf16[2,32,64,12,64]{4,2,3,1,0:T(8,128)(2,1)} %collective-permute-done.14), kind=kLoop, calls=%fused_computation.45 | loop fusion | flops 46137344 | bytes 92274688 | tf_op jit(solution)/shard_map/concatenate | solution.py:45
  3280.3 86.6 %convert_bitcast_fusion = bf16[2,32,64,64,64]{3,4,2,1,0:T(8,128)(2,1)} fusion(bf16[2,32,64,88,64]{4,2,3,1,0:T(8,128)(2,1)} %pad_maximum_fusion.6, bf16[88,64]{0,1:T(8,128)(2,1)S(1)} %copy.99), kind=kOutput, calls=%fused_computation.65 | convolution fusion | flops 2969595392 | bytes 79703040 | tf_op jit(solution)/shard_map/vcxsz,si->vcxiz/dot_general | solution.py:47
  3448.9 220.3 %collective-permute-done.16 = bf16[2,32,64,64,12]{3,2,4,1,0:T(8,128)(2,1)} collective-permute-done((bf16[2,32,64,64,12]{3,2,4,1,0:T(8,128)(2,1)}, bf16[2,32,64,64,12]{3,2,4,1,0:T(8,128)(2,1)}, u32[]{:S(2)}, u32[]{:S(2)}) %collective-permute-start.16) | collective-permute-done | bytes 6291488 | tf_op jit(solution)/shard_map/ppermute | solution.py:28
  3702.0 63.2 %pad_maximum_fusion.7 = bf16[2,32,64,64,88]{3,4,2,1,0:T(8,128)(2,1)} fusion(bf16[2,32,64,64,12]{3,4,2,1,0:T(8,128)(2,1)} %copy.106, bf16[2,32,64,64,64]{3,4,2,1,0:T(8,128)(2,1)} %convert_bitcast_fusion, bf16[2,32,64,64,12]{3,4,2,1,0:T(8,128)(2,1)} %copy.105), kind=kLoop, calls=%fused_computation.46 | loop fusion | flops 138412032 | bytes 92274688 | tf_op jit(solution)/shard_map/concatenate | solution.py:45
  3765.2 100.3 %copy.108 = bf16[2,32,64,64,88]{4,1,3,2,0:T(8,128)(2,1)} copy(bf16[2,32,64,64,88]{3,4,2,1,0:T(8,128)(2,1)} %pad_maximum_fusion.7) | data formatting | bytes 92274688 | tf_op jit(solution)/shard_map/concatenate | solution.py:45
  3865.5 79.0 %fusion.26 = bf16[2,32,64,64,64]{4,1,3,2,0:T(8,128)(2,1)} fusion(bf16[2,32,64,64,64]{4,1,3,2,0:T(8,128)(2,1)} %fusion.17, f32[32]{0:T(128)S(1)} %copy-done.12, bf16[2,32,64,64,88]{4,1,3,2,0:T(8,128)(2,1)} %copy.108, bf16[88,64]{0,1:T(8,128)(2,1)S(1)} %copy.107, bf16[3,32,32]{2,1,0:T(8,128)(2,1)} %param.6), kind=kOutput, calls=%fused_computation.38 | convolution fusion | flops 4244663808 | bytes 167791744 | tf_op jit(solution)/shard_map/cd,vcxyz->vdxyz/dot_general | solution.py:48
  3944.5 45.2 %copy.110 = bf16[2,32,64,64,64]{4,3,2,1,0:T(8,128)(2,1)} copy(bf16[2,32,64,64,64]{4,1,3,2,0:T(8,128)(2,1)} %fusion.26) | data formatting | bytes 67108864 | tf_op jit(solution)/shard_map/convert_element_type | solution.py:50
  (109 shorter events, 688.9 us)
Async XLA Ops:
  21.6 139.0 %collective-permute-start = (bf16[2,32,12,64,64]{4,3,2,1,0:T(8,128)(2,1)}, bf16[2,32,12,64,64]{4,3,2,1,0:T(8,128)(2,1)}, u32[]{:S(2)}, u32[]{:S(2)}) collective-permute-start(bf16[2,32,12,64,64]{4,3,2,1,0:T(8,128)(2,1)} %get-tuple-element.21), channel_id=1, source_target_pairs={{0,1},{2,3},{4,5},{6,7}} | collective-permute-start | bytes 18874376 | tf_op jit(solution)/shard_map/ppermute | solution.py:28
  22.9 105.3 %copy-start.10 = (f32[3,3,25]{2,1,0:T(4,128)S(1)}, f32[3,3,25]{2,1,0:T(4,128)}, u32[]{:S(2)}) copy-start(f32[3,3,25]{2,1,0:T(4,128)} %param.5) | copy-start | bytes 2704
  22.9 191.8 %collective-permute-start.1 = (bf16[2,32,12,64,64]{4,3,2,1,0:T(8,128)(2,1)}, bf16[2,32,12,64,64]{4,3,2,1,0:T(8,128)(2,1)}, u32[]{:S(2)}, u32[]{:S(2)}) collective-permute-start(bf16[2,32,12,64,64]{4,3,2,1,0:T(8,128)(2,1)} %get-tuple-element.22), channel_id=1, source_target_pairs={{1,0},{3,2},{5,4},{7,6}} | collective-permute-start | bytes 18874376 | tf_op jit(solution)/shard_map/ppermute | solution.py:29
  128.2 739.9 %copy-start.7 = (s32[6144]{0:T(1024)}, s32[6144]{0:T(1024)S(1)}, u32[]{:S(2)}) copy-start(s32[6144]{0:T(1024)S(1)} %pad_clamp_fusion) | copy-start | bytes 73732
  390.0 269.4 %collective-permute-start.2 = (bf16[2,32,64,12,64]{4,2,3,1,0:T(8,128)(2,1)}, bf16[2,32,64,12,64]{4,2,3,1,0:T(8,128)(2,1)}, u32[]{:S(2)}, u32[]{:S(2)}) collective-permute-start(bf16[2,32,64,12,64]{4,2,3,1,0:T(8,128)(2,1)} %get-tuple-element.19), channel_id=1, source_target_pairs={{0,2},{1,3},{4,6},{5,7}} | collective-permute-start | bytes 18874376 | tf_op jit(solution)/shard_map/ppermute | solution.py:28
  398.5 269.6 %collective-permute-start.3 = (bf16[2,32,64,12,64]{4,2,3,1,0:T(8,128)(2,1)}, bf16[2,32,64,12,64]{4,2,3,1,0:T(8,128)(2,1)}, u32[]{:S(2)}, u32[]{:S(2)}) collective-permute-start(bf16[2,32,64,12,64]{4,2,3,1,0:T(8,128)(2,1)} %get-tuple-element.20), channel_id=1, source_target_pairs={{2,0},{3,1},{6,4},{7,5}} | collective-permute-start | bytes 18874376 | tf_op jit(solution)/shard_map/ppermute | solution.py:29
  816.0 52.0 %copy-start.6 = (bf16[25]{0:T(256)(128)(2,1)S(1)}, bf16[25]{0:T(256)(128)(2,1)}, u32[]{:S(2)}) copy-start(bf16[25]{0:T(256)(128)(2,1)} %get-tuple-element.28) | copy-start | bytes 154
  816.0 83.8 %copy-start.11 = (f32[3,32]{1,0:T(4,128)S(1)}, f32[3,32]{1,0:T(4,128)}, u32[]{:S(2)}) copy-start(f32[3,32]{1,0:T(4,128)} %param.7) | copy-start | bytes 1156
  850.1 270.0 %collective-permute-start.4 = (bf16[2,32,64,64,12]{3,2,4,1,0:T(8,128)(2,1)}, bf16[2,32,64,64,12]{3,2,4,1,0:T(8,128)(2,1)}, u32[]{:S(2)}, u32[]{:S(2)}) collective-permute-start(bf16[2,32,64,64,12]{3,2,4,1,0:T(8,128)(2,1)} %copy.81), channel_id=1, source_target_pairs={{0,4},{1,5},{2,6},{3,7}} | collective-permute-start | bytes 18874376 | tf_op jit(solution)/shard_map/ppermute | solution.py:28
  866.3 271.4 %collective-permute-start.5 = (bf16[2,32,64,64,12]{3,2,4,1,0:T(8,128)(2,1)}, bf16[2,32,64,64,12]{3,2,4,1,0:T(8,128)(2,1)}, u32[]{:S(2)}, u32[]{:S(2)}) collective-permute-start(bf16[2,32,64,64,12]{3,2,4,1,0:T(8,128)(2,1)} %copy.82), channel_id=1, source_target_pairs={{4,0},{5,1},{6,2},{7,3}} | collective-permute-start | bytes 18874376 | tf_op jit(solution)/shard_map/ppermute | solution.py:29
  1316.6 119.9 %copy-start.5 = (bf16[25]{0:T(256)(128)(2,1)S(1)}, bf16[25]{0:T(256)(128)(2,1)}, u32[]{:S(2)}) copy-start(bf16[25]{0:T(256)(128)(2,1)} %get-tuple-element.26) | copy-start | bytes 154
  1316.6 119.9 %copy-start.8 = (s32[6144]{0:T(1024)S(1)}, s32[6144]{0:T(1024)}, u32[]{:S(2)}) copy-start(s32[6144]{0:T(1024)} %copy-done.7) | copy-start | bytes 73732
  1422.9 45.4 %collective-permute-start.6 = (bf16[2,32,12,64,64]{4,1,3,2,0:T(8,128)(2,1)}, bf16[2,32,12,64,64]{4,1,3,2,0:T(8,128)(2,1)}, u32[]{:S(2)}, u32[]{:S(2)}) collective-permute-start(bf16[2,32,12,64,64]{4,1,3,2,0:T(8,128)(2,1)} %get-tuple-element.15), channel_id=1, source_target_pairs={{0,1},{2,3},{4,5},{6,7}} | collective-permute-start | bytes 18874376 | tf_op jit(solution)/shard_map/ppermute | solution.py:28
  1424.2 44.1 %collective-permute-start.7 = (bf16[2,32,12,64,64]{4,1,3,2,0:T(8,128)(2,1)}, bf16[2,32,12,64,64]{4,1,3,2,0:T(8,128)(2,1)}, u32[]{:S(2)}, u32[]{:S(2)}) collective-permute-start(bf16[2,32,12,64,64]{4,1,3,2,0:T(8,128)(2,1)} %get-tuple-element.16), channel_id=1, source_target_pairs={{1,0},{3,2},{5,4},{7,6}} | collective-permute-start | bytes 18874376 | tf_op jit(solution)/shard_map/ppermute | solution.py:29
  1530.5 150.4 %copy-start.4 = (bf16[25]{0:T(256)(128)(2,1)S(1)}, bf16[25]{0:T(256)(128)(2,1)}, u32[]{:S(2)}) copy-start(bf16[25]{0:T(256)(128)(2,1)} %get-tuple-element.27) | copy-start | bytes 154
  1673.8 266.5 %collective-permute-start.8 = (bf16[2,32,64,12,64]{4,2,3,1,0:T(8,128)(2,1)}, bf16[2,32,64,12,64]{4,2,3,1,0:T(8,128)(2,1)}, u32[]{:S(2)}, u32[]{:S(2)}) collective-permute-start(bf16[2,32,64,12,64]{4,2,3,1,0:T(8,128)(2,1)} %get-tuple-element.13), channel_id=1, source_target_pairs={{0,2},{1,3},{4,6},{5,7}} | collective-permute-start | bytes 18874376 | tf_op jit(solution)/shard_map/ppermute | solution.py:28
  1679.6 269.3 %collective-permute-start.9 = (bf16[2,32,64,12,64]{4,2,3,1,0:T(8,128)(2,1)}, bf16[2,32,64,12,64]{4,2,3,1,0:T(8,128)(2,1)}, u32[]{:S(2)}, u32[]{:S(2)}) collective-permute-start(bf16[2,32,64,12,64]{4,2,3,1,0:T(8,128)(2,1)} %get-tuple-element.14), channel_id=1, source_target_pairs={{2,0},{3,1},{6,4},{7,5}} | collective-permute-start | bytes 18874376 | tf_op jit(solution)/shard_map/ppermute | solution.py:29
  2096.9 50.3 %copy-start.3 = (bf16[25]{0:T(256)(128)(2,1)S(1)}, bf16[25]{0:T(256)(128)(2,1)}, u32[]{:S(2)}) copy-start(bf16[25]{0:T(256)(128)(2,1)} %get-tuple-element.25) | copy-start | bytes 154
  2131.0 268.1 %collective-permute-start.10 = (bf16[2,32,64,64,12]{3,2,4,1,0:T(8,128)(2,1)}, bf16[2,32,64,64,12]{3,2,4,1,0:T(8,128)(2,1)}, u32[]{:S(2)}, u32[]{:S(2)}) collective-permute-start(bf16[2,32,64,64,12]{3,2,4,1,0:T(8,128)(2,1)} %copy.92), channel_id=1, source_target_pairs={{0,4},{1,5},{2,6},{3,7}} | collective-permute-start | bytes 18874376 | tf_op jit(solution)/shard_map/ppermute | solution.py:28
  2146.0 270.7 %collective-permute-start.11 = (bf16[2,32,64,64,12]{3,2,4,1,0:T(8,128)(2,1)}, bf16[2,32,64,64,12]{3,2,4,1,0:T(8,128)(2,1)}, u32[]{:S(2)}, u32[]{:S(2)}) collective-permute-start(bf16[2,32,64,64,12]{3,2,4,1,0:T(8,128)(2,1)} %copy.93), channel_id=1, source_target_pairs={{4,0},{5,1},{6,2},{7,3}} | collective-permute-start | bytes 18874376 | tf_op jit(solution)/shard_map/ppermute | solution.py:29
  2495.3 100.3 %copy-start.13 = (f32[32]{0:T(128)S(1)}, f32[32]{0:T(128)}, u32[]{:S(2)}) copy-start(f32[32]{0:T(128)} %get-tuple-element.34) | copy-start | bytes 388
  2595.6 110.9 %copy-start.2 = (bf16[25]{0:T(256)(128)(2,1)S(1)}, bf16[25]{0:T(256)(128)(2,1)}, u32[]{:S(2)}) copy-start(bf16[25]{0:T(256)(128)(2,1)} %get-tuple-element.31) | copy-start | bytes 154
  2595.6 110.9 %copy-start.9 = (s32[6144]{0:T(1024)S(1)}, s32[6144]{0:T(1024)}, u32[]{:S(2)}) copy-start(s32[6144]{0:T(1024)} %copy-done.7) | copy-start | bytes 73732
  2692.9 45.4 %collective-permute-start.12 = (bf16[2,32,12,64,64]{4,1,3,2,0:T(8,128)(2,1)}, bf16[2,32,12,64,64]{4,1,3,2,0:T(8,128)(2,1)}, u32[]{:S(2)}, u32[]{:S(2)}) collective-permute-start(bf16[2,32,12,64,64]{4,1,3,2,0:T(8,128)(2,1)} %get-tuple-element.9), channel_id=1, source_target_pairs={{0,1},{2,3},{4,5},{6,7}} | collective-permute-start | bytes 18874376 | tf_op jit(solution)/shard_map/ppermute | solution.py:28
  2694.2 44.1 %collective-permute-start.13 = (bf16[2,32,12,64,64]{4,1,3,2,0:T(8,128)(2,1)}, bf16[2,32,12,64,64]{4,1,3,2,0:T(8,128)(2,1)}, u32[]{:S(2)}, u32[]{:S(2)}) collective-permute-start(bf16[2,32,12,64,64]{4,1,3,2,0:T(8,128)(2,1)} %get-tuple-element.10), channel_id=1, source_target_pairs={{1,0},{3,2},{5,4},{7,6}} | collective-permute-start | bytes 18874376 | tf_op jit(solution)/shard_map/ppermute | solution.py:29
  2800.4 150.4 %copy-start.1 = (bf16[25]{0:T(256)(128)(2,1)S(1)}, bf16[25]{0:T(256)(128)(2,1)}, u32[]{:S(2)}) copy-start(bf16[25]{0:T(256)(128)(2,1)} %get-tuple-element.24) | copy-start | bytes 154
  2943.8 266.5 %collective-permute-start.14 = (bf16[2,32,64,12,64]{4,2,3,1,0:T(8,128)(2,1)}, bf16[2,32,64,12,64]{4,2,3,1,0:T(8,128)(2,1)}, u32[]{:S(2)}, u32[]{:S(2)}) collective-permute-start(bf16[2,32,64,12,64]{4,2,3,1,0:T(8,128)(2,1)} %get-tuple-element.7), channel_id=1, source_target_pairs={{0,2},{1,3},{4,6},{5,7}} | collective-permute-start | bytes 18874376 | tf_op jit(solution)/shard_map/ppermute | solution.py:28
  2949.5 269.3 %collective-permute-start.15 = (bf16[2,32,64,12,64]{4,2,3,1,0:T(8,128)(2,1)}, bf16[2,32,64,12,64]{4,2,3,1,0:T(8,128)(2,1)}, u32[]{:S(2)}, u32[]{:S(2)}) collective-permute-start(bf16[2,32,64,12,64]{4,2,3,1,0:T(8,128)(2,1)} %get-tuple-element.8), channel_id=1, source_target_pairs={{2,0},{3,1},{6,4},{7,5}} | collective-permute-start | bytes 18874376 | tf_op jit(solution)/shard_map/ppermute | solution.py:29
  3366.9 50.2 %copy-start = (bf16[25]{0:T(256)(128)(2,1)S(1)}, bf16[25]{0:T(256)(128)(2,1)}, u32[]{:S(2)}) copy-start(bf16[25]{0:T(256)(128)(2,1)} %get-tuple-element.23) | copy-start | bytes 154
  3400.9 268.2 %collective-permute-start.16 = (bf16[2,32,64,64,12]{3,2,4,1,0:T(8,128)(2,1)}, bf16[2,32,64,64,12]{3,2,4,1,0:T(8,128)(2,1)}, u32[]{:S(2)}, u32[]{:S(2)}) collective-permute-start(bf16[2,32,64,64,12]{3,2,4,1,0:T(8,128)(2,1)} %copy.103), channel_id=1, source_target_pairs={{0,4},{1,5},{2,6},{3,7}} | collective-permute-start | bytes 18874376 | tf_op jit(solution)/shard_map/ppermute | solution.py:28
  3415.9 270.8 %collective-permute-start.17 = (bf16[2,32,64,64,12]{3,2,4,1,0:T(8,128)(2,1)}, bf16[2,32,64,64,12]{3,2,4,1,0:T(8,128)(2,1)}, u32[]{:S(2)}, u32[]{:S(2)}) collective-permute-start(bf16[2,32,64,64,12]{3,2,4,1,0:T(8,128)(2,1)} %copy.104), channel_id=1, source_target_pairs={{4,0},{5,1},{6,2},{7,3}} | collective-permute-start | bytes 18874376 | tf_op jit(solution)/shard_map/ppermute | solution.py:29
  3765.2 100.3 %copy-start.12 = (f32[32]{0:T(128)S(1)}, f32[32]{0:T(128)}, u32[]{:S(2)}) copy-start(f32[32]{0:T(128)} %get-tuple-element.32) | copy-start | bytes 388
where the time goes:
time: 4010 us; the launch traced here: 3990 us
  waiting for transfers between devices  1380 us (34%)
  local copies, waits for them, and re-layouts  1180 us (29%)
  matrix products  849 us (21%)
  other arithmetic  498 us (12%)
  starting transfers between devices  89.2 us (2%)
    ppermute x9, waiting for transfers between devices, neighbour_planes(): from_lower = lax.ppermute(high_planes, axis_name, upward)  1340 us
    dot_general x6, matrix products, local_layers(): jnp.einsum(PASS_FORMS[pass_idx], padded, matrix, preferred_element_type=j...  603 us
    concatenate x8, other arithmetic, local_layers(): padded = jnp.concatenate([from_lower, current, from_upper], axis=axis_dim)  498 us
    concatenate x3, local copies, waits for them, and re-layouts, local_layers(): padded = jnp.concatenate([from_lower, current, from_upper], axis=axis_dim)  301 us
    gather x27, local copies, waits for them, and re-layouts, band_matrix(): picked = tap_row[jnp.clip(tap_index, 0, tap_count - 1)]  286 us
    dot_general x3, matrix products, local_layers(): jnp.einsum('cd,vcxyz->vdxyz', mix_weight[layer_idx], current, preferred_e...  246 us
    slice x12, local copies, waits for them, and re-layouts, neighbour_planes(): lax.slice_in_dim(block, extent - plane_count, extent, axis=axis_dim)  226 us
    ppermute x4, local copies, waits for them, and re-layouts, neighbour_planes(): from_lower = lax.ppermute(high_planes, axis_name, upward)  100 us
  transfers between devices with their start and end apart: 18, of which 12 were waited for; matrix products, arithmetic and copies ran while one was open for 13% of the time, Pallas kernels for 0%

commit v1 on v0

v1 whole, which is shorter than its diff:
```python
import functools

import jax
import jax.numpy as jnp
from jax import lax
from jax.experimental import pallas as pl
from jax.experimental.pallas import tpu as pltpu
from jax.sharding import PartitionSpec as P


BF = jnp.bfloat16
F32 = jnp.float32
SUB = 4
ROWS = SUB * SUB
PITCH = 40


def shape_of(*dims, dtype=BF):
    return jax.ShapeDtypeStruct(dims, dtype)


def grid2(rows, cols):
    return lax.broadcasted_iota(jnp.int32, (rows, cols), 0), lax.broadcasted_iota(jnp.int32, (rows, cols), 1)


def interleave(first, second):
    return jnp.concatenate([first, second], axis=1)


def bands_kernel(taps_ref, iband_ref, jband_ref, kband_ref, khalo_ref):
    layer = pl.program_id(0)
    at_end = lax.axis_index('pz') == 0
    half = (taps_ref.shape[2] - 1) // 2

    def toeplitz(ref, axis, out_pos, in_pos, keep):
        tap = jnp.where(keep, in_pos - out_pos + half, -1)
        total = jnp.zeros(tap.shape, F32)
        for t in range(2 * half + 1):
            total = jnp.where(tap == t, taps_ref[layer, axis, t], total)
        ref[0] = total.astype(BF)

    def rows_cols(ref):
        dims = ref.shape[1:]
        return lax.broadcasted_iota(jnp.int32, dims, 0), lax.broadcasted_iota(jnp.int32, dims, 1)

    lanes = iband_ref.shape[1] // 2
    o, n = rows_cols(iband_ref)
    toeplitz(iband_ref, 0, n % lanes, o % lanes, o // lanes == n // lanes)
    o, n = rows_cols(jband_ref)
    toeplitz(jband_ref, 1, o // SUB, n // SUB - half, o % SUB == n % SUB)
    groups = kband_ref.shape[1] // ROWS
    edge = khalo_ref.shape[1] // ROWS

    def k_of(row):
        turned = row // ROWS + jnp.where(at_end, groups - edge, 0)
        return jnp.where(turned >= groups, turned - groups, turned) * SUB + row % SUB

    def same_j(o, n):
        return (o % ROWS) // SUB == (n % ROWS) // SUB

    o, n = rows_cols(kband_ref)
    toeplitz(kband_ref, 2, k_of(o), k_of(n), same_j(o, n))
    o, n = rows_cols(khalo_ref)
    far = jnp.where(at_end, groups * SUB, -half) + (n // ROWS) * SUB + n % SUB
    toeplitz(khalo_ref, 2, k_of(o), far, same_j(o, n))


def bands(taps, lanes, j_len, kg, hg):
    layers, _, count = taps.shape
    sizes = [(2 * lanes, 2 * lanes), (j_len * SUB, (j_len + count - 1) * SUB), (kg * ROWS,) * 2, (hg * ROWS,) * 2]
    return pl.pallas_call(
        bands_kernel,
        out_shape=[shape_of(layers, *s) for s in sizes],
        grid=(layers,),
        in_specs=[pl.BlockSpec(memory_space=pltpu.SMEM)],
        out_specs=[pl.BlockSpec((1,) + s, lambda l: (l, 0, 0)) for s in sizes],
        compiler_params=pltpu.CompilerParams(dimension_semantics=("arbitrary",)),
        name='bands',
    )(taps)


def enter_kernel(half_ref, own_ref, other_ref, perm_ref, band_ref, *refs):
    vol_ref, filt_ref, upn_ref, upd_ref, dnn_ref, dnd_ref, scratch = refs[-7:]
    side, j_len, k_len = own_ref.shape[2], own_ref.shape[3], own_ref.shape[4]
    lanes = 2 * side
    first = half_ref[0] * side

    def fill(n, _):
        for base, ref in ((first, own_ref), (side - first, other_ref)):
            pair = interleave(ref[0, 0, n], ref[0, 1, n]).astype(F32)
            scratch[pl.ds(pl.multiple_of((base + n) * PITCH, 8), j_len), :] = pair
        return 0

    lax.fori_loop(0, side, fill, 0, unroll=8)

    def group(g, _):
        tiles = [scratch[pl.ds(g * SUB + j, lanes, stride=PITCH), :].T.astype(BF) for j in range(SUB)]
        columns = interleave(
            jnp.concatenate([t[:k_len] for t in tiles], axis=0),
            jnp.concatenate([t[k_len:] for t in tiles], axis=0),
        )
        mixed = jnp.dot(perm_ref[...], columns, preferred_element_type=F32).astype(BF)
        filtered = jnp.dot(mixed, band_ref[...], preferred_element_type=F32).astype(BF)
        for m in range(2):
            vol_ref[g, :, m] = mixed[:, m * lanes:(m + 1) * lanes].reshape(-1, ROWS, lanes)
            filt_ref[g, :, m] = filtered[:, m * lanes:(m + 1) * lanes].reshape(-1, ROWS, lanes)
        return 0

    groups = j_len // SUB
    lax.fori_loop(0, groups, group, 0, unroll=4)
    hg = upn_ref.shape[0]
    upn_ref[...] = filt_ref[groups - hg:, :hg]
    upd_ref[...] = filt_ref[groups - hg:, hg:]
    dnn_ref[...] = filt_ref[:hg, :hg]
    dnd_ref[...] = filt_ref[:hg, hg:]


def enter(volumes, vol_idx, other, chan_at, before, half, perm, band, hg):
    _, chans, side, j_all, k_len = volumes.shape
    j_len = j_all // 2
    jg, kg = j_len // SUB, k_len // SUB
    at = chan_at // 2
    sizes = [(jg, kg), (jg, kg), (hg, hg), (hg, kg - hg), (hg, hg), (hg, kg - hg)]
    before = before or []
    return pl.pallas_call(
        enter_kernel,
        out_shape=[shape_of(*s, chans, ROWS, 2 * side) for s in sizes],
        grid_spec=pltpu.PrefetchScalarGridSpec(
            num_scalar_prefetch=1,
            grid=(other.shape[1] // 2,),
            in_specs=[
                pl.BlockSpec((1, 2, side, j_len, k_len), lambda c, h: (vol_idx, c + at, 0, h[0], 0)),
                pl.BlockSpec((1, 2, side, j_len, k_len), lambda c, h: (0, c, 0, 0, 0)),
                pl.BlockSpec(perm.shape, lambda c, h: (0, 0)),
                pl.BlockSpec((None,) + band.shape[1:], lambda c, h: (0, 0, 0)),
            ] + [pl.BlockSpec(memory_space=pl.ANY)] * len(before),
            out_specs=[pl.BlockSpec(s + (2, ROWS, 2 * side), lambda c, h: (0, 0, c + at, 0, 0)) for s in sizes],
            scratch_shapes=[pltpu.VMEM((2 * side * PITCH, 2 * k_len), F32)],
        ),
        input_output_aliases={5 + n: n for n in range(len(before))},
        compiler_params=pltpu.CompilerParams(dimension_semantics=("arbitrary",)),
        cost_estimate=pl.CostEstimate(flops=other.shape[1] * 1_000_000_000, bytes_accessed=other.shape[1] * 2_500_000, transcendentals=0),
    )(half, volumes, other, perm, band, *before)


def leave_kernel(half_ref, own_ref, other_ref, perm_ref, *refs):
    raw_ref, scratch = refs[-2:]
    side, j_all, k_len = raw_ref.shape[2], raw_ref.shape[3], raw_ref.shape[4]
    lanes = own_ref.shape[4]
    j_len = j_all // 2
    half = half_ref[0]
    left = lax.broadcasted_iota(jnp.int32, (own_ref.shape[1] * ROWS, lanes), 1) < side

    def group(g, _):
        chan = []
        for m in range(2):
            a, b = own_ref[g, :, m].reshape(-1, lanes), other_ref[g, :, m].reshape(-1, lanes)
            chan.append(jnp.concatenate([
                interleave(a[:, :side], b[:, :side]), interleave(a[:, side:], b[:, side:])], axis=0))
        rows = jnp.dot(perm_ref[...], interleave(*chan), preferred_element_type=F32)
        for j in range(SUB):
            part = rows[j * k_len:(j + 1) * k_len]
            tile = jnp.concatenate([part[:, :lanes], part[:, lanes:]], axis=0)
            scratch[pl.ds(g * SUB + j, lanes, stride=PITCH), :] = tile.T
        return 0

    lax.fori_loop(0, j_len // SUB, group, 0, unroll=4)

    def drain(n, _):
        for base, where in ((0, half), (side, 1 - half)):
            pair = scratch[pl.ds(pl.multiple_of((base + n) * PITCH, 8), j_len), :].astype(BF)
            at = pl.ds(pl.multiple_of(where * j_len, j_len), j_len)
            raw_ref[0, 0, n, at] = pair[:, :k_len]
            raw_ref[0, 1, n, at] = pair[:, k_len:]
        return 0

    lax.fori_loop(0, side, drain, 0, unroll=8)


def leave(own, other, vol_idx, result, half, perm, full_shape):
    _, chans, side, j_all, k_len = full_shape
    jg, kp = own.shape[:2]
    operands = [half, own, other, perm]
    spec = pl.BlockSpec((jg, kp, 2, ROWS, 2 * side), lambda c, h: (0, 0, c, 0, 0))
    in_specs = [spec, spec, pl.BlockSpec(perm.shape, lambda c, h: (0, 0))]
    aliases = {}
    if result is not None:
        operands.append(result)
        in_specs.append(pl.BlockSpec(memory_space=pl.ANY))
        aliases = {4: 0}
    return pl.pallas_call(
        leave_kernel,
        out_shape=shape_of(*full_shape),
        grid_spec=pltpu.PrefetchScalarGridSpec(
            num_scalar_prefetch=1,
            grid=(chans // 2,),
            in_specs=in_specs,
            out_specs=pl.BlockSpec((1, 2, side, j_all, k_len), lambda c, h: (vol_idx, c, 0, 0, 0)),
            scratch_shapes=[pltpu.VMEM((2 * side * PITCH, 2 * k_len), F32)],
        ),
        input_output_aliases=aliases,
        compiler_params=pltpu.CompilerParams(dimension_semantics=("arbitrary",)),
        cost_estimate=pl.CostEstimate(flops=30_000_000_000, bytes_accessed=50_000_000, transcendentals=0),
    )(*operands)


def along_j_kernel(field_ref, low_ref, high_ref, band_ref, out_ref):
    chans, lanes = field_ref.shape[2], field_ref.shape[4]

    def pair(n, _):
        halves = []
        for m in range(2):
            c = 2 * n + m
            halves.append(jnp.concatenate(
                [ref[:, 0, c].reshape(-1, lanes) for ref in (low_ref, field_ref, high_ref)], axis=0))
        total = jnp.dot(band_ref[...], interleave(*halves), preferred_element_type=F32).astype(BF)
        for m in range(2):
            out_ref[:, 0, 2 * n + m] = total[:, m * lanes:(m + 1) * lanes].reshape(-1, ROWS, lanes)
        return 0

    lax.fori_loop(0, chans // 2, pair, 0, unroll=4)


def along_j(field, low, high, band, layer, first):
    jg, _, chans, rows, lanes = field.shape
    halo, count = low.shape[:2]
    return pl.pallas_call(
        along_j_kernel,
        out_shape=shape_of(jg, count, chans, rows, lanes),
        grid=(count,),
        in_specs=[
            pl.BlockSpec((jg, 1, chans, rows, lanes), lambda g: (0, g + first, 0, 0, 0)),
            pl.BlockSpec((halo, 1, chans, rows, lanes), lambda g: (0, g, 0, 0, 0)),
            pl.BlockSpec((halo, 1, chans, rows, lanes), lambda g: (0, g, 0, 0, 0)),
            pl.BlockSpec((None,) + band.shape[1:], lambda g: (layer, 0, 0)),
        ],
        out_specs=pl.BlockSpec((jg, 1, chans, rows, lanes), lambda g: (0, g, 0, 0, 0)),
        compiler_params=pltpu.CompilerParams(dimension_semantics=("arbitrary",)),
        cost_estimate=pl.CostEstimate(flops=count * 1_000_000_000, bytes_accessed=count * 2_900_000, transcendentals=0),
    )(field, low, high, band)


GELU_A = 0.7978845608028654
GELU_B = GELU_A * 0.044715


def finish_kernel(last, edge_ref, rest_ref, halo_ref, vol_ref, band_ref, halo_band_ref, mix_ref, bias_ref, *refs):
    unit = refs[-1]
    edge = edge_ref.shape[1]
    groups, chans, lanes = vol_ref.shape[1], vol_ref.shape[2], vol_ref.shape[4]
    edge_rows = edge * ROWS

    def channel_pair(n, _):
        own, far = [], []
        for m in range(2):
            c = 2 * n + m
            own.append(jnp.concatenate(
                [edge_ref[0, :, c].reshape(-1, lanes), rest_ref[0, :, c].reshape(-1, lanes)], axis=0))
            far.append(halo_ref[0, :, c].reshape(-1, lanes))
        total = jnp.dot(band_ref[...], interleave(*own), preferred_element_type=F32)
        extra = jnp.dot(halo_band_ref[...], interleave(*far), preferred_element_type=F32)
        head = (total[:edge_rows] + extra).astype(BF)
        tail = total[edge_rows:].astype(BF)
        for m in range(2):
            cut = slice(m * lanes, (m + 1) * lanes)
            unit[:edge, 2 * n + m] = head[:, cut].reshape(-1, ROWS, lanes)
            unit[edge:, 2 * n + m] = tail[:, cut].reshape(-1, ROWS, lanes)
        return 0

    lax.fori_loop(0, chans // 2, channel_pair, 0, unroll=4)

    def group_pair(n, _):
        k0, k1 = (n, n + groups // 2) if last else (2 * n, 2 * n + 1)
        both = lambda ref, lead: interleave(
            ref[lead + (k0,)].reshape(-1, lanes), ref[lead + (k1,)].reshape(-1, lanes))
        x = jnp.dot(mix_ref[...], both(unit, ()), preferred_element_type=F32) + interleave(bias_ref[...], bias_ref[...])
        half_x = 0.5 * x
        act = half_x * jnp.tanh(x * (GELU_A + GELU_B * (x * x))) + half_x
        new = (both(vol_ref, (0,)).astype(F32) + act).astype(BF)
        shaped = lambda a: a.reshape(chans, ROWS, lanes)
        if last:
            own_ref, other_ref = refs[:2]
            side = lanes // 2
            low = interleave(new[:, :side], new[:, lanes:lanes + side])
            high = interleave(new[:, side:lanes], new[:, lanes + side:])
            is_low = lax.axis_index('px') == 0
            own_ref[0, n] = shaped(jnp.where(is_low, low, high))
            other_ref[0, n] = shaped(jnp.where(is_low, high, low))
        else:
            iband_ref, new_ref, filt_ref = refs[:3]
            new_ref[0, k0], new_ref[0, k1] = shaped(new[:, :lanes]), shaped(new[:, lanes:])
            filt = jnp.dot(new, iband_ref[...], preferred_element_type=F32).astype(BF)
            filt_ref[0, k0], filt_ref[0, k1] = shaped(filt[:, :lanes]), shaped(filt[:, lanes:])
        return 0

    lax.fori_loop(0, groups // 2, group_pair, 0, unroll=4)

    if not last:
        filt_ref, upn_ref, upd_ref, dnn_ref, dnd_ref = refs[2:7]
        g = pl.program_id(0)

        @pl.when(g < edge)
        def _():
            dnn_ref[0] = filt_ref[0, :edge]
            dnd_ref[0] = filt_ref[0, edge:]

        @pl.when(g >= pl.num_programs(0) - edge)
        def _():
            upn_ref[0] = filt_ref[0, :edge]
            upd_ref[0] = filt_ref[0, edge:]


def finish(edge, rest, halo, vol, layer, band, halo_band, mix, bias, iband):
    jg, kg, chans, rows, lanes = vol.shape
    hg = edge.shape[1]
    last = iband is None
    block = lambda a: pl.BlockSpec((1,) + a.shape[1:], lambda g: (g, 0, 0, 0, 0))
    of_layer = lambda a, l: pl.BlockSpec((None,) + a.shape[1:], lambda g: (l, 0, 0))
    in_specs = [block(edge), block(rest), block(halo), block(vol)]
    in_specs += [of_layer(a, layer) for a in (band, halo_band, mix, bias)]
    operands = [edge, rest, halo, vol, band, halo_band, mix, bias]
    if last:
        packed = shape_of(jg, kg // 2, chans, rows, lanes)
        out_shape, out_specs = [packed] * 2, [block(packed)] * 2
    else:
        operands.append(iband)
        in_specs.append(of_layer(iband, layer + 1))
        out_shape = [shape_of(*vol.shape)] * 2
        out_specs = [block(vol)] * 2
        up = lambda g: (jnp.maximum(g - (jg - hg), 0), 0, 0, 0, 0)
        down = lambda g: (jnp.minimum(g, hg - 1), 0, 0, 0, 0)
        for index in (up, down):
            for size in (hg, kg - hg):
                out_shape.append(shape_of(hg, size, chans, rows, lanes))
                out_specs.append(pl.BlockSpec((1, size, chans, rows, lanes), index))
    return pl.pallas_call(
        functools.partial(finish_kernel, last),
        out_shape=out_shape,
        grid=(jg,),
        in_specs=in_specs,
        out_specs=out_specs,
        scratch_shapes=[pltpu.VMEM((kg, chans, rows, lanes), BF)],
        compiler_params=pltpu.CompilerParams(dimension_semantics=("arbitrary",)),
        cost_estimate=pl.CostEstimate(flops=40_000_000_000, bytes_accessed=75_000_000, transcendentals=8_400_000),
    )(*operands)


def solution(mesh):
    sizes = {a: mesh.shape[a] for a in ('px', 'py', 'pz')}
    vol_spec = P('dp', None, 'px', 'py', 'pz')

    def local_layers(volumes, filter_taps, mix_weight, mix_bias):
        count, chans, side, j_all, k_len = volumes.shape
        layers, _, taps = filter_taps.shape
        half = (taps - 1) // 2
        j_len = j_all // 2
        kg, hg = k_len // SUB, half // SUB
        px, pz = lax.axis_index('px'), lax.axis_index('pz')
        half_idx = px.astype(jnp.int32).reshape(1)
        iband, jband, kband, khalo = bands(filter_taps.astype(BF).astype(F32), 2 * side, j_len, kg, hg)

        o, n = grid2(chans * ROWS, chans * ROWS)
        spread = jnp.repeat(jnp.repeat(mix_weight.swapaxes(1, 2), ROWS, axis=1), ROWS, axis=2)
        mix = jnp.where(o % ROWS == n % ROWS, spread, jnp.zeros((), BF))
        bias = jnp.broadcast_to(jnp.repeat(mix_bias, ROWS, axis=1)[:, :, None], (layers, chans * ROWS, 2 * side))

        o, n = grid2(kg * ROWS, SUB * k_len)
        k_row = jnp.where(pz == 0, (o // ROWS + kg - hg) % kg, o // ROWS) * SUB + o % SUB
        perm = jnp.where(n == ((o % ROWS) // SUB) * k_len + k_row, 1.0, 0.0).astype(BF)

        swap = [(0, 1), (1, 0)]
        line = sizes['py'] * sizes['px']
        upward = [(s, s + 1) for s in range(line - 1)]
        downward = [(s + 1, s) for s in range(line - 1)]
        up = lambda a: lax.ppermute(a, ('py', 'px'), upward)
        down = lambda a: lax.ppermute(a, ('py', 'px'), downward)

        states = []
        for v in range(count):
            pieces = 2 if v == 0 else 1
            width = chans // pieces
            outs = None
            for p in range(pieces):
                sent = lax.dynamic_slice(
                    volumes, (v, p * width, 0, (1 - px) * j_len, 0), (1, width, side, j_len, k_len))
                other = lax.ppermute(sent, 'px', swap)
                outs = enter(volumes, v, other, p * width, outs, half_idx, perm, iband, hg)
            states.append(outs)
        result = None

        def send_j(v):
            _, _, up_near, up_deep, down_near, down_deep = states[v]
            moved = []
            for move, part in ((up, up_near), (down, down_near),
                                     (up, up_deep), (down, down_deep)):
                moved.append(move(part))
            return moved

        def edge_of(l, v, after):
            filt = states[v][1]
            if after is not None:
                filt, after = lax.optimization_barrier((filt, after))
            edge = along_j(filt, *halos[v][:2], jband, l, 0)
            return edge, lax.ppermute(edge, 'pz', swap), after

        halos = [send_j(v) for v in range(count)]
        edges = [edge_of(0, 0, None)] + [None] * (count - 1)
        rests = [None] * count
        rests[0] = along_j(states[0][1], *halos[0][2:], jband, 0, hg)
        for step in range(count * layers):
            l, v = divmod(step, count)
            nl, nv = divmod(step + 1, count)
            if nl < layers and edges[nv] is None:
                edges[nv] = edge_of(nl, nv, rests[v])
                rests[v] = edges[nv][2]
            edge, halo, _ = edges[v]
            states[v] = finish(edge, rests[v], halo, states[v][0], l, kband, khalo, mix, bias,
                               iband if l + 1 < layers else None)
            edges[v] = rests[v] = None
            if l + 1 < layers:
                halos[v] = send_j(v)
            if nl < layers:
                rests[nv] = along_j(states[nv][1], *halos[nv][2:], jband, nl, hg)
        for v in range(count):
            own, other = states[v]
            other = lax.ppermute(other, 'px', swap)
            result = leave(own, other, v, result, half_idx, perm.T, volumes.shape)
        return result

    return jax.shard_map(local_layers, mesh=mesh, in_specs=(vol_spec, P(), P(), P()), out_specs=vol_spec, check_vma=False)
```

time: 4010 us -> 935 us (0.23)
  waiting for transfers between devices: 1380 us -> 202 us
  local copies, waits for them, and re-layouts: 1180 us -> 38.5 us
  matrix products: 849 us -> 0 us
  Pallas kernels: 0 us -> 613 us
  other arithmetic: 498 us -> 3.52 us
    ppermute x18 -> x35, waiting for transfers between devices: 1380 us -> 202 us  [the longest x12 175 us: local_layers(): up = lambda a: lax.ppermute(a, ('py', 'px'), upward)]
    dot_general x9 -> x0, matrix products: 849 us -> none  [the longest x6 603 us: local_layers(): jnp.einsum(PASS_FORMS[pass_idx], padded, matrix, preferred_element_type=j...]
    pallas_call x0 -> x24, Pallas kernels: none -> 613 us  [the longest x6 284 us: finish(): pl.pallas_call(functools.partial(finish_kernel, last), out_shape=out_shap...]
    concatenate x8 -> x0, other arithmetic: 498 us -> none  [local_layers(): padded = jnp.concatenate([from_lower, current, from_upper], axis=axis_dim)]
    concatenate x3 -> x0, local copies, waits for them, and re-layouts: 301 us -> none  [local_layers(): padded = jnp.concatenate([from_lower, current, from_upper], axis=axis_dim)]
    gather x27 -> x0, local copies, waits for them, and re-layouts: 286 us -> none  [band_matrix(): picked = tap_row[jnp.clip(tap_index, 0, tap_count - 1)]]
    slice x15 -> x0, local copies, waits for them, and re-layouts: 251 us -> none  [the longest x12 226 us: neighbour_planes(): lax.slice_in_dim(block, extent - plane_count, extent, axis=axis_dim)]
    ppermute x8 -> x0, local copies, waits for them, and re-layouts: 200 us -> none  [the longest x4 100 us: neighbour_planes(): from_lower = lax.ppermute(high_planes, axis_name, upward)]
  transfers between devices with their start and end apart: 18 -> 35, of which waited for: 12 -> 9; matrix products, arithmetic and copies ran while one was open for 13% -> 2% of each run, Pallas kernels for 0% -> 62%
where the time goes in v1:
time: 935 us; the launch traced here: 930 us
  Pallas kernels  613 us (66%)
  waiting for transfers between devices  202 us (22%)
  starting transfers between devices  72.6 us (8%)
  local copies, waits for them, and re-layouts  38.5 us (4%)
    pallas_call x6, Pallas kernels, finish(): pl.pallas_call(functools.partial(finish_kernel, last), out_shape=out_shap...  284 us
    ppermute x12, waiting for transfers between devices, local_layers(): up = lambda a: lax.ppermute(a, ('py', 'px'), upward)  175 us
    pallas_call x12, Pallas kernels, along_j(): pl.pallas_call(along_j_kernel, out_shape=shape_of(jg, count, chans, rows,...  157 us
    pallas_call x3, Pallas kernels, enter(): pl.pallas_call(enter_kernel, out_shape=[shape_of(*s, chans, ROWS, 2 * sid...  85.4 us
    pallas_call x2, Pallas kernels, leave(): pl.pallas_call(leave_kernel, out_shape=shape_of(*full_shape), grid_spec=p...  81.3 us
    ppermute x12, starting transfers between devices, local_layers(): down = lambda a: lax.ppermute(a, ('py', 'px'), downward)  36.6 us
    ppermute x12, starting transfers between devices, local_layers(): up = lambda a: lax.ppermute(a, ('py', 'px'), upward)  30.5 us
    dynamic_slice x2, local copies, waits for them, and re-layouts, local_layers(): lax.dynamic_slice(volumes, (v, p * width, 0, (1 - px) * j_len, 0), (1, wi...  27.2 us
  transfers between devices with their start and end apart: 35, of which 9 were waited for; matrix products, arithmetic and copies ran while one was open for 2% of the time, Pallas kernels for 62%

profile of v1, /device:TPU:1, one launch (start us, length us, event | category | flops | bytes accessed | tf_op | source)
XLA Modules:
  0.0 929.9 jit_solution(1190016344369674376)
XLA Ops:
  0.0 12.2 %constant_dynamic-slice_fusion = (bf16[1,16,64,32,64]{4,3,2,1,0:T(8,128)(2,1)}, bf16[1,16,64,32,64]{4,3,2,1,0:T(8,128)(2,1)}) fusion(bf16[2,32,64,64,64]{4,3,2,1,0:T(8,128)(2,1)} %own_ref.5, s32[]{:T(128)S(6)} %select_n.80), kind=kLoop, calls=%fused_computation.67 | loop fusion | bytes 16777220 | tf_op jit(solution)/shard_map/dynamic_slice | solution.py:384
  12.2 15.0 %constant_dynamic-slice_fusion.2 = bf16[1,32,64,32,64]{4,3,2,1,0:T(8,128)(2,1)} fusion(bf16[2,32,64,64,64]{4,3,2,1,0:T(8,128)(2,1)} %own_ref.5, s32[]{:T(128)S(6)} %select_n.80), kind=kLoop, calls=%fused_computation.69 | loop fusion | bytes 16777220 | tf_op jit(solution)/shard_map/dynamic_slice | solution.py:384
  28.3 5.1 bands.1
  34.7 22.0 %shard_map.47 = (bf16[8,16,32,16,128]{4,3,2,1,0:T(8,128)(2,1)}, bf16[8,16,32,16,128]{4,3,2,1,0:T(8,128)(2,1)}, bf16[3,3,32,16,128]{4,3,2,1,0:T(8,128)(2,1)}, bf1...) custom-call(s32[1]{0:T(128)} %bitcast.half_ref, ...), custom_call_target="tpu_custom_call" | custom-call | flops 16000000000 | bytes 40000000 | tf_op jit(solution)/shard_map/pallas_call | solution.py:125
  56.7 8.1 collective-permute-done.1.other_ref
  64.9 22.0 %shard_map.48 = (bf16[8,16,32,16,128]{4,3,2,1,0:T(8,128)(2,1)}, bf16[8,16,32,16,128]{4,3,2,1,0:T(8,128)(2,1)}, bf16[3,3,32,16,128]{4,3,2,1,0:T(8,128)(2,1)}, bf1...) custom-call(s32[1]{0:T(128)} %bitcast.half_ref, ...), custom_call_target="tpu_custom_call", output_to_operand_aliasing={{0}: (5, {}), {1}: (6, {}), {2}: (7, {}), {3}: (8, {}), {4}... | custom-call | flops 16000000000 | bytes 40000000 | tf_op jit(solution)/shard_map/pallas_call | solution.py:125
  102.0 57.6 %collective-permute-done.7.low_ref = bf16[3,3,32,16,128]{4,3,2,1,0:T(8,128)(2,1)} collective-permute-done((bf16[3,3,32,16,128]{4,3,2,1,0:T(8,128)(2,1)}, bf16[3,3,32,16,128]{4,3,2,1,0:T(8,128)(2,1)}, u32[]{:S(2)}, u32[]{:S(2)}) %collective-permute-start.7) | collective-permute-done | bytes 1179680 | tf_op jit(solution)/shard_map/ppermute | solution.py:375
  164.0 6.0 shard_map.51.edge_ref
  171.3 41.3 %shard_map.46 = (bf16[8,16,32,16,128]{4,3,2,1,0:T(8,128)(2,1)}, bf16[8,16,32,16,128]{4,3,2,1,0:T(8,128)(2,1)}, bf16[3,3,32,16,128]{4,3,2,1,0:T(8,128)(2,1)}, bf1...) custom-call(s32[1]{0:T(128)} %bitcast.half_ref, ...), custom_call_target="tpu_custom_call" | custom-call | flops 32000000000 | bytes 80000000 | tf_op jit(solution)/shard_map/pallas_call | solution.py:125
  223.6 20.1 %shard_map.49.rest_ref = bf16[8,13,32,16,128]{4,3,2,1,0:T(8,128)(2,1)} custom-call(bf16[8,16,32,16,128]{4,3,2,1,0:T(8,128)(2,1)} %get-tuple-element.73.field_ref, bf16[3,13,32,16,128]{4,3,2,1,0:T(8,128)(2,1)} %collective-permute-done.3.low_ref, bf16[3,13,32,16,128]{4,3,2,1,0:T(8,128)(2,1)} %collective-permute-done.4.high_ref, ...), custom_call_target="tpu_custom_call" | custom-call | flops 12999999488 | bytes 37700000 | tf_op jit(solution)/shard_map/pallas_call | solution.py:227
  243.8 39.1 %collective-permute-done.5.low_ref = bf16[3,3,32,16,128]{4,3,2,1,0:T(8,128)(2,1)S(1)} collective-permute-done((bf16[3,3,32,16,128]{4,3,2,1,0:T(8,128)(2,1)}, bf16[3,3,32,16,128]{4,3,2,1,0:T(8,128)(2,1)S(1)}, u32[]{:S(2)}, u32[]{:S(2)}) %collective-permute-start.5) | collective-permute-done | bytes 1179680 | tf_op jit(solution)/shard_map/ppermute | solution.py:375
  282.8 4.7 collective-permute-done.6.high_ref
  288.6 6.1 shard_map.50.edge_ref
  296.0 51.7 %shard_map.52 = (bf16[8,16,32,16,128]{4,3,2,1,0:T(8,128)(2,1)}, bf16[8,16,32,16,128]{4,3,2,1,0:T(8,128)(2,1)}, bf16[3,3,32,16,128]{4,3,2,1,0:T(8,128)(2,1)}, bf1...) custom-call(bf16[8,3,32,16,128]{4,3,2,1,0:T(8,128)(2,1)} %shard_map.5, ...), custom_call_target="tpu_custom_call" | custom-call | flops 40000000000 | bytes 75000000 | tf_op jit(solution)/shard_map/pallas_call | solution.py:336
  358.9 20.2 %shard_map.53.rest_ref = bf16[8,13,32,16,128]{4,3,2,1,0:T(8,128)(2,1)} custom-call(bf16[8,16,32,16,128]{4,3,2,1,0:T(8,128)(2,1)} %get-tuple-element.77.field_ref, bf16[3,13,32,16,128]{4,3,2,1,0:T(8,128)(2,1)} %collective-permute-done.10.low_ref, bf16[3,13,32,16,128]{4,3,2,1,0:T(8,128)(2,1)} %collective-permute-done.11.high_ref, ...), custom_call_target="tpu_custom_call" | custom-call | flops 12999999488 | bytes 37700000 | tf_op jit(solution)/shard_map/pallas_call | solution.py:227
  381.1 6.1 shard_map.57.edge_ref
  388.4 51.8 %shard_map.54 = (bf16[8,16,32,16,128]{4,3,2,1,0:T(8,128)(2,1)}, bf16[8,16,32,16,128]{4,3,2,1,0:T(8,128)(2,1)}, bf16[3,3,32,16,128]{4,3,2,1,0:T(8,128)(2,1)}, bf1...) custom-call(bf16[8,3,32,16,128]{4,3,2,1,0:T(8,128)(2,1)} %shard_map.5, ...), custom_call_target="tpu_custom_call" | custom-call | flops 40000000000 | bytes 75000000 | tf_op jit(solution)/shard_map/pallas_call | solution.py:336
  451.2 20.2 %shard_map.55.rest_ref = bf16[8,13,32,16,128]{4,3,2,1,0:T(8,128)(2,1)} custom-call(bf16[8,16,32,16,128]{4,3,2,1,0:T(8,128)(2,1)} %get-tuple-element.97.field_ref, bf16[3,13,32,16,128]{4,3,2,1,0:T(8,128)(2,1)} %collective-permute-done.13.low_ref, bf16[3,13,32,16,128]{4,3,2,1,0:T(8,128)(2,1)} %collective-permute-done.14.high_ref, ...), custom_call_target="tpu_custom_call" | custom-call | flops 12999999488 | bytes 37700000 | tf_op jit(solution)/shard_map/pallas_call | solution.py:227
  471.4 39.4 %collective-permute-done.15.low_ref = bf16[3,3,32,16,128]{4,3,2,1,0:T(8,128)(2,1)S(1)} collective-permute-done((bf16[3,3,32,16,128]{4,3,2,1,0:T(8,128)(2,1)}, bf16[3,3,32,16,128]{4,3,2,1,0:T(8,128)(2,1)S(1)}, u32[]{:S(2)}, u32[]{:S(2)}) %collective-permute-start.15) | collective-permute-done | bytes 1179680 | tf_op jit(solution)/shard_map/ppermute | solution.py:375
  516.5 6.1 shard_map.56.edge_ref
  522.9 51.5 %shard_map.58 = (bf16[8,16,32,16,128]{4,3,2,1,0:T(8,128)(2,1)}, bf16[8,16,32,16,128]{4,3,2,1,0:T(8,128)(2,1)}, bf16[3,3,32,16,128]{4,3,2,1,0:T(8,128)(2,1)}, bf1...) custom-call(bf16[8,3,32,16,128]{4,3,2,1,0:T(8,128)(2,1)} %shard_map.5, ...), custom_call_target="tpu_custom_call" | custom-call | flops 40000000000 | bytes 75000000 | tf_op jit(solution)/shard_map/pallas_call | solution.py:336
  585.4 20.2 %shard_map.59.rest_ref = bf16[8,13,32,16,128]{4,3,2,1,0:T(8,128)(2,1)} custom-call(bf16[8,16,32,16,128]{4,3,2,1,0:T(8,128)(2,1)} %get-tuple-element.94.field_ref, bf16[3,13,32,16,128]{4,3,2,1,0:T(8,128)(2,1)} %collective-permute-done.20.low_ref, bf16[3,13,32,16,128]{4,3,2,1,0:T(8,128)(2,1)} %collective-permute-done.21.high_ref, ...), custom_call_target="tpu_custom_call" | custom-call | flops 12999999488 | bytes 37700000 | tf_op jit(solution)/shard_map/pallas_call | solution.py:227
  607.6 6.1 shard_map.65.edge_ref
  614.9 51.6 %shard_map.60 = (bf16[8,16,32,16,128]{4,3,2,1,0:T(8,128)(2,1)}, bf16[8,16,32,16,128]{4,3,2,1,0:T(8,128)(2,1)}, bf16[3,3,32,16,128]{4,3,2,1,0:T(8,128)(2,1)}, bf1...) custom-call(bf16[8,3,32,16,128]{4,3,2,1,0:T(8,128)(2,1)} %shard_map.5, ...), custom_call_target="tpu_custom_call" | custom-call | flops 40000000000 | bytes 75000000 | tf_op jit(solution)/shard_map/pallas_call | solution.py:336
  677.7 20.2 %shard_map.61.rest_ref = bf16[8,13,32,16,128]{4,3,2,1,0:T(8,128)(2,1)} custom-call(bf16[8,16,32,16,128]{4,3,2,1,0:T(8,128)(2,1)} %get-tuple-element.118.field_ref, bf16[3,13,32,16,128]{4,3,2,1,0:T(8,128)(2,1)} %collective-permute-done.23.low_ref, bf16[3,13,32,16,128]{4,3,2,1,0:T(8,128)(2,1)} %collective-permute-done.24.high_ref, ...), custom_call_target="tpu_custom_call" | custom-call | flops 12999999488 | bytes 37700000 | tf_op jit(solution)/shard_map/pallas_call | solution.py:227
  697.9 39.2 %collective-permute-done.25.low_ref = bf16[3,3,32,16,128]{4,3,2,1,0:T(8,128)(2,1)S(1)} collective-permute-done((bf16[3,3,32,16,128]{4,3,2,1,0:T(8,128)(2,1)}, bf16[3,3,32,16,128]{4,3,2,1,0:T(8,128)(2,1)S(1)}, u32[]{:S(2)}, u32[]{:S(2)}) %collective-permute-start.25) | collective-permute-done | bytes 1179680 | tf_op jit(solution)/shard_map/ppermute | solution.py:375
  742.7 6.1 shard_map.62.edge_ref
  749.0 38.6 %shard_map.66 = (bf16[8,8,32,16,128]{4,3,2,1,0:T(8,128)(2,1)}, bf16[8,8,32,16,128]{4,3,2,1,0:T(8,128)(2,1)}) custom-call(bf16[8,3,32,16,128]{4,3,2,1,0:T(8,128)(2,1)} %shard_map.65.edge_ref, bf16[8,13,32,16,128]{4,3,2,1,0:T(8,128)(2,1)} %shard_map.61.rest_ref, bf16[8,3,32,16,128]{4,3,2,1,0:T(8,128)(2,1)} %collective-permute-done.33.halo_ref, ...), custom_call_target="tpu_custom_call" | custom-call | flops 40000000000 | bytes 75000000 | tf_op jit(solution)/shard_map/pallas_call | solution.py:336
  787.6 20.2 %shard_map.63.rest_ref = bf16[8,13,32,16,128]{4,3,2,1,0:T(8,128)(2,1)} custom-call(bf16[8,16,32,16,128]{4,3,2,1,0:T(8,128)(2,1)} %get-tuple-element.110.field_ref, bf16[3,13,32,16,128]{4,3,2,1,0:T(8,128)(2,1)} %collective-permute-done.27.low_ref, bf16[3,13,32,16,128]{4,3,2,1,0:T(8,128)(2,1)} %collective-permute-done.28.high_ref, ...), custom_call_target="tpu_custom_call" | custom-call | flops 12999999488 | bytes 37700000 | tf_op jit(solution)/shard_map/pallas_call | solution.py:227
  809.5 38.7 %shard_map.64 = (bf16[8,8,32,16,128]{4,3,2,1,0:T(8,128)(2,1)}, bf16[8,8,32,16,128]{4,3,2,1,0:T(8,128)(2,1)}) custom-call(bf16[8,3,32,16,128]{4,3,2,1,0:T(8,128)(2,1)} %shard_map.62.edge_ref, bf16[8,13,32,16,128]{4,3,2,1,0:T(8,128)(2,1)} %shard_map.63.rest_ref, bf16[8,3,32,16,128]{4,3,2,1,0:T(8,128)(2,1)} %copy-done.13, ...), custom_call_target="tpu_custom_call" | custom-call | flops 40000000000 | bytes 75000000 | tf_op jit(solution)/shard_map/pallas_call | solution.py:336
  848.6 40.6 %shard_map.67.refs_0_ = bf16[2,32,64,64,64]{4,3,2,1,0:T(8,128)(2,1)} custom-call(s32[1]{0:T(128)} %bitcast.half_ref, bf16[8,8,32,16,128]{4,3,2,1,0:T(8,128)(2,1)} %get-tuple-element.123.own_ref, bf16[8,8,32,16,128]{4,3,2,1,0:T(8,128)(2,1)} %collective-permute-done.34.other_ref, bf16[256,256]{1,0:T(8,128)(2,1)} %get-tuple-element.127.perm_ref), custom_call_target="tpu_custom_call" | custom-call | flops 30000001024 | bytes 50000000 | tf_op jit(solution)/shard_map/pallas_call | solution.py:191
  889.3 40.7 %shard_map.68 = bf16[2,32,64,64,64]{4,3,2,1,0:T(8,128)(2,1)} custom-call(s32[1]{0:T(128)} %bitcast.half_ref, bf16[8,8,32,16,128]{4,3,2,1,0:T(8,128)(2,1)} %get-tuple-element.116.own_ref, bf16[8,8,32,16,128]{4,3,2,1,0:T(8,128)(2,1)} %collective-permute-done.30.other_ref, ...), custom_call_target="tpu_custom_call", output_to_operand_aliasing={{}: (4, {})} | custom-call | flops 30000001024 | bytes 50000000 | tf_op jit(solution)/shard_map/pallas_call | solution.py:191
  (111 shorter events, 101.1 us)
Async XLA Ops:
  27.2 144.1 %collective-permute-start = (bf16[1,32,64,32,64]{4,3,2,1,0:T(8,128)(2,1)}, bf16[1,32,64,32,64]{4,3,2,1,0:T(8,128)(2,1)}, u32[]{:S(2)}, u32[]{:S(2)}) collective-permute-start(bf16[1,32,64,32,64]{4,3,2,1,0:T(8,128)(2,1)} %constant_dynamic-slice_fusion.2), channel_id=1, source_target_pairs={{0,1},{1,0},{2,3},{3,2},{4,5},{5,4},{6,7},{7,6}} | collective-permute-start | bytes 25165832 | tf_op jit(solution)/shard_map/ppermute | solution.py:386
  27.7 37.1 %collective-permute-start.1 = (bf16[1,16,64,32,64]{4,3,2,1,0:T(8,128)(2,1)}, bf16[1,16,64,32,64]{4,3,2,1,0:T(8,128)(2,1)}, u32[]{:S(2)}, u32[]{:S(2)}) collective-permute-start(bf16[1,16,64,32,64]{4,3,2,1,0:T(8,128)(2,1)} %get-tuple-element.126), channel_id=1, source_target_pairs={{0,1},{1,0},{2,3},{3,2},{4,5},{5,4},{6,7},{7,6}} | collective-permute-start | bytes 12582920 | tf_op jit(solution)/shard_map/ppermute | solution.py:386
  86.9 132.3 %collective-permute-start.3 = (bf16[3,13,32,16,128]{4,3,2,1,0:T(8,128)(2,1)}, bf16[3,13,32,16,128]{4,3,2,1,0:T(8,128)(2,1)}, u32[]{:S(2)}, u32[]{:S(2)}) collective-permute-start(bf16[3,13,32,16,128]{4,3,2,1,0:T(8,128)(2,1)} %get-tuple-element.74), channel_id=1, source_target_pairs={{0,1},{1,2},{2,3},{4,5},{5,6},{6,7}} | collective-permute-start | bytes 15335432 | tf_op jit(solution)/shard_map/ppermute | solution.py:375
  91.4 129.7 %collective-permute-start.4 = (bf16[3,13,32,16,128]{4,3,2,1,0:T(8,128)(2,1)}, bf16[3,13,32,16,128]{4,3,2,1,0:T(8,128)(2,1)}, u32[]{:S(2)}, u32[]{:S(2)}) collective-permute-start(bf16[3,13,32,16,128]{4,3,2,1,0:T(8,128)(2,1)} %get-tuple-element.75), channel_id=1, source_target_pairs={{1,0},{2,1},{3,2},{5,4},{6,5},{7,6}} | collective-permute-start | bytes 15335432 | tf_op jit(solution)/shard_map/ppermute | solution.py:376
  93.5 66.1 %collective-permute-start.7 = (bf16[3,3,32,16,128]{4,3,2,1,0:T(8,128)(2,1)}, bf16[3,3,32,16,128]{4,3,2,1,0:T(8,128)(2,1)}, u32[]{:S(2)}, u32[]{:S(2)}) collective-permute-start(bf16[3,3,32,16,128]{4,3,2,1,0:T(8,128)(2,1)} %get-tuple-element.80), channel_id=1, source_target_pairs={{0,1},{1,2},{2,3},{4,5},{5,6},{6,7}} | collective-permute-start | bytes 3538952 | tf_op jit(solution)/shard_map/ppermute | solution.py:375
  97.0 67.0 %collective-permute-start.8 = (bf16[3,3,32,16,128]{4,3,2,1,0:T(8,128)(2,1)}, bf16[3,3,32,16,128]{4,3,2,1,0:T(8,128)(2,1)}, u32[]{:S(2)}, u32[]{:S(2)}) collective-permute-start(bf16[3,3,32,16,128]{4,3,2,1,0:T(8,128)(2,1)} %get-tuple-element.81), channel_id=1, source_target_pairs={{1,0},{2,1},{3,2},{5,4},{6,5},{7,6}} | collective-permute-start | bytes 3538952 | tf_op jit(solution)/shard_map/ppermute | solution.py:376
  170.1 124.8 %collective-permute-start.9 = (bf16[8,3,32,16,128]{4,3,2,1,0:T(8,128)(2,1)}, bf16[8,3,32,16,128]{4,3,2,1,0:T(8,128)(2,1)}, u32[]{:S(2)}, u32[]{:S(2)}) collective-permute-start(bf16[8,3,32,16,128]{4,3,2,1,0:T(8,128)(2,1)} %shard_map.51.edge_ref), channel_id=1, source_target_pairs={{0,4},{4,0},{1,5},{5,1},{2,6},{6,2},{3,7},{7,3}} | collective-permute-start | bytes 9437192 | tf_op jit(solution)/shard_map/ppermute | solution.py:404
  212.6 139.5 %collective-permute-start.10 = (bf16[3,13,32,16,128]{4,3,2,1,0:T(8,128)(2,1)}, bf16[3,13,32,16,128]{4,3,2,1,0:T(8,128)(2,1)}, u32[]{:S(2)}, u32[]{:S(2)}) collective-permute-start(bf16[3,13,32,16,128]{4,3,2,1,0:T(8,128)(2,1)} %get-tuple-element.87), channel_id=1, source_target_pairs={{0,1},{1,2},{2,3},{4,5},{5,6},{6,7}} | collective-permute-start | bytes 15335432 | tf_op jit(solution)/shard_map/ppermute | solution.py:375
  214.6 140.6 %collective-permute-start.11 = (bf16[3,13,32,16,128]{4,3,2,1,0:T(8,128)(2,1)}, bf16[3,13,32,16,128]{4,3,2,1,0:T(8,128)(2,1)}, u32[]{:S(2)}, u32[]{:S(2)}) collective-permute-start(bf16[3,13,32,16,128]{4,3,2,1,0:T(8,128)(2,1)} %get-tuple-element.88), channel_id=1, source_target_pairs={{1,0},{2,1},{3,2},{5,4},{6,5},{7,6}} | collective-permute-start | bytes 15335432 | tf_op jit(solution)/shard_map/ppermute | solution.py:376
  219.2 63.7 %collective-permute-start.5 = (bf16[3,3,32,16,128]{4,3,2,1,0:T(8,128)(2,1)}, bf16[3,3,32,16,128]{4,3,2,1,0:T(8,128)(2,1)S(1)}, u32[]{:S(2)}, u32[]{:S(2)}) collective-permute-start(bf16[3,3,32,16,128]{4,3,2,1,0:T(8,128)(2,1)} %get-tuple-element.78), channel_id=1, source_target_pairs={{0,1},{1,2},{2,3},{4,5},{5,6},{6,7}} | collective-permute-start | bytes 3538952 | tf_op jit(solution)/shard_map/ppermute | solution.py:375
  221.1 66.4 %collective-permute-start.6 = (bf16[3,3,32,16,128]{4,3,2,1,0:T(8,128)(2,1)}, bf16[3,3,32,16,128]{4,3,2,1,0:T(8,128)(2,1)S(1)}, u32[]{:S(2)}, u32[]{:S(2)}) collective-permute-start(bf16[3,3,32,16,128]{4,3,2,1,0:T(8,128)(2,1)} %get-tuple-element.79), channel_id=1, source_target_pairs={{1,0},{2,1},{3,2},{5,4},{6,5},{7,6}} | collective-permute-start | bytes 3538952 | tf_op jit(solution)/shard_map/ppermute | solution.py:376
  294.6 93.8 %collective-permute-start.12 = (bf16[8,3,32,16,128]{4,3,2,1,0:T(8,128)(2,1)}, bf16[8,3,32,16,128]{4,3,2,1,0:T(8,128)(2,1)}, u32[]{:S(2)}, u32[]{:S(2)}) collective-permute-start(bf16[8,3,32,16,128]{4,3,2,1,0:T(8,128)(2,1)} %shard_map.50.edge_ref), channel_id=1, source_target_pairs={{0,4},{4,0},{1,5},{5,1},{2,6},{6,2},{3,7},{7,3}} | collective-permute-start | bytes 9437192 | tf_op jit(solution)/shard_map/ppermute | solution.py:404
  347.7 31.3 %collective-permute-start.17 = (bf16[3,3,32,16,128]{4,3,2,1,0:T(8,128)(2,1)}, bf16[3,3,32,16,128]{4,3,2,1,0:T(8,128)(2,1)S(1)}, u32[]{:S(2)}, u32[]{:S(2)}) collective-permute-start(bf16[3,3,32,16,128]{4,3,2,1,0:T(8,128)(2,1)} %get-tuple-element.98), channel_id=1, source_target_pairs={{0,1},{1,2},{2,3},{4,5},{5,6},{6,7}} | collective-permute-start | bytes 3538952 | tf_op jit(solution)/shard_map/ppermute | solution.py:375
  352.2 94.6 %collective-permute-start.13 = (bf16[3,13,32,16,128]{4,3,2,1,0:T(8,128)(2,1)}, bf16[3,13,32,16,128]{4,3,2,1,0:T(8,128)(2,1)}, u32[]{:S(2)}, u32[]{:S(2)}) collective-permute-start(bf16[3,13,32,16,128]{4,3,2,1,0:T(8,128)(2,1)} %get-tuple-element.92), channel_id=1, source_target_pairs={{0,1},{1,2},{2,3},{4,5},{5,6},{6,7}} | collective-permute-start | bytes 15335432 | tf_op jit(solution)/shard_map/ppermute | solution.py:375
  355.3 93.5 %collective-permute-start.14 = (bf16[3,13,32,16,128]{4,3,2,1,0:T(8,128)(2,1)}, bf16[3,13,32,16,128]{4,3,2,1,0:T(8,128)(2,1)}, u32[]{:S(2)}, u32[]{:S(2)}) collective-permute-start(bf16[3,13,32,16,128]{4,3,2,1,0:T(8,128)(2,1)} %get-tuple-element.93), channel_id=1, source_target_pairs={{1,0},{2,1},{3,2},{5,4},{6,5},{7,6}} | collective-permute-start | bytes 15335432 | tf_op jit(solution)/shard_map/ppermute | solution.py:376
  387.2 135.7 %collective-permute-start.19 = (bf16[8,3,32,16,128]{4,3,2,1,0:T(8,128)(2,1)}, bf16[8,3,32,16,128]{4,3,2,1,0:T(8,128)(2,1)}, u32[]{:S(2)}, u32[]{:S(2)}) collective-permute-start(bf16[8,3,32,16,128]{4,3,2,1,0:T(8,128)(2,1)} %shard_map.57.edge_ref), channel_id=1, source_target_pairs={{0,4},{4,0},{1,5},{5,1},{2,6},{6,2},{3,7},{7,3}} | collective-permute-start | bytes 9437192 | tf_op jit(solution)/shard_map/ppermute | solution.py:404
  440.2 138.6 %collective-permute-start.20 = (bf16[3,13,32,16,128]{4,3,2,1,0:T(8,128)(2,1)}, bf16[3,13,32,16,128]{4,3,2,1,0:T(8,128)(2,1)}, u32[]{:S(2)}, u32[]{:S(2)}) collective-permute-start(bf16[3,13,32,16,128]{4,3,2,1,0:T(8,128)(2,1)} %get-tuple-element.103), channel_id=1, source_target_pairs={{0,1},{1,2},{2,3},{4,5},{5,6},{6,7}} | collective-permute-start | bytes 15335432 | tf_op jit(solution)/shard_map/ppermute | solution.py:375
  442.6 139.3 %collective-permute-start.21 = (bf16[3,13,32,16,128]{4,3,2,1,0:T(8,128)(2,1)}, bf16[3,13,32,16,128]{4,3,2,1,0:T(8,128)(2,1)}, u32[]{:S(2)}, u32[]{:S(2)}) collective-permute-start(bf16[3,13,32,16,128]{4,3,2,1,0:T(8,128)(2,1)} %get-tuple-element.104), channel_id=1, source_target_pairs={{1,0},{2,1},{3,2},{5,4},{6,5},{7,6}} | collective-permute-start | bytes 15335432 | tf_op jit(solution)/shard_map/ppermute | solution.py:376
  446.8 64.0 %collective-permute-start.15 = (bf16[3,3,32,16,128]{4,3,2,1,0:T(8,128)(2,1)}, bf16[3,3,32,16,128]{4,3,2,1,0:T(8,128)(2,1)S(1)}, u32[]{:S(2)}, u32[]{:S(2)}) collective-permute-start(bf16[3,3,32,16,128]{4,3,2,1,0:T(8,128)(2,1)} %get-tuple-element.95), channel_id=1, source_target_pairs={{0,1},{1,2},{2,3},{4,5},{5,6},{6,7}} | collective-permute-start | bytes 3538952 | tf_op jit(solution)/shard_map/ppermute | solution.py:375
  448.7 66.8 %collective-permute-start.16 = (bf16[3,3,32,16,128]{4,3,2,1,0:T(8,128)(2,1)}, bf16[3,3,32,16,128]{4,3,2,1,0:T(8,128)(2,1)S(1)}, u32[]{:S(2)}, u32[]{:S(2)}) collective-permute-start(bf16[3,3,32,16,128]{4,3,2,1,0:T(8,128)(2,1)} %get-tuple-element.96), channel_id=1, source_target_pairs={{1,0},{2,1},{3,2},{5,4},{6,5},{7,6}} | collective-permute-start | bytes 3538952 | tf_op jit(solution)/shard_map/ppermute | solution.py:376
  522.7 92.2 %collective-permute-start.22 = (bf16[8,3,32,16,128]{4,3,2,1,0:T(8,128)(2,1)}, bf16[8,3,32,16,128]{4,3,2,1,0:T(8,128)(2,1)}, u32[]{:S(2)}, u32[]{:S(2)}) collective-permute-start(bf16[8,3,32,16,128]{4,3,2,1,0:T(8,128)(2,1)} %shard_map.56.edge_ref), channel_id=1, source_target_pairs={{0,4},{4,0},{1,5},{5,1},{2,6},{6,2},{3,7},{7,3}} | collective-permute-start | bytes 9437192 | tf_op jit(solution)/shard_map/ppermute | solution.py:404
  574.4 31.2 %collective-permute-start.31 = (bf16[3,3,32,16,128]{4,3,2,1,0:T(8,128)(2,1)}, bf16[3,3,32,16,128]{4,3,2,1,0:T(8,128)(2,1)S(1)}, u32[]{:S(2)}, u32[]{:S(2)}) collective-permute-start(bf16[3,3,32,16,128]{4,3,2,1,0:T(8,128)(2,1)} %get-tuple-element.119), channel_id=1, source_target_pairs={{0,1},{1,2},{2,3},{4,5},{5,6},{6,7}} | collective-permute-start | bytes 3538952 | tf_op jit(solution)/shard_map/ppermute | solution.py:375
  578.8 94.3 %collective-permute-start.23 = (bf16[3,13,32,16,128]{4,3,2,1,0:T(8,128)(2,1)}, bf16[3,13,32,16,128]{4,3,2,1,0:T(8,128)(2,1)}, u32[]{:S(2)}, u32[]{:S(2)}) collective-permute-start(bf16[3,13,32,16,128]{4,3,2,1,0:T(8,128)(2,1)} %get-tuple-element.108), channel_id=1, source_target_pairs={{0,1},{1,2},{2,3},{4,5},{5,6},{6,7}} | collective-permute-start | bytes 15335432 | tf_op jit(solution)/shard_map/ppermute | solution.py:375
  581.9 93.1 %collective-permute-start.24 = (bf16[3,13,32,16,128]{4,3,2,1,0:T(8,128)(2,1)}, bf16[3,13,32,16,128]{4,3,2,1,0:T(8,128)(2,1)}, u32[]{:S(2)}, u32[]{:S(2)}) collective-permute-start(bf16[3,13,32,16,128]{4,3,2,1,0:T(8,128)(2,1)} %get-tuple-element.109), channel_id=1, source_target_pairs={{1,0},{2,1},{3,2},{5,4},{6,5},{7,6}} | collective-permute-start | bytes 15335432 | tf_op jit(solution)/shard_map/ppermute | solution.py:376
  613.7 135.4 %collective-permute-start.33 = (bf16[8,3,32,16,128]{4,3,2,1,0:T(8,128)(2,1)}, bf16[8,3,32,16,128]{4,3,2,1,0:T(8,128)(2,1)}, u32[]{:S(2)}, u32[]{:S(2)}) collective-permute-start(bf16[8,3,32,16,128]{4,3,2,1,0:T(8,128)(2,1)} %shard_map.65.edge_ref), channel_id=1, source_target_pairs={{0,4},{4,0},{1,5},{5,1},{2,6},{6,2},{3,7},{7,3}} | collective-permute-start | bytes 9437192 | tf_op jit(solution)/shard_map/ppermute | solution.py:404
  666.5 121.2 %collective-permute-start.27 = (bf16[3,13,32,16,128]{4,3,2,1,0:T(8,128)(2,1)}, bf16[3,13,32,16,128]{4,3,2,1,0:T(8,128)(2,1)}, u32[]{:S(2)}, u32[]{:S(2)}) collective-permute-start(bf16[3,13,32,16,128]{4,3,2,1,0:T(8,128)(2,1)} %get-tuple-element.113), channel_id=1, source_target_pairs={{0,1},{1,2},{2,3},{4,5},{5,6},{6,7}} | collective-permute-start | bytes 15335432 | tf_op jit(solution)/shard_map/ppermute | solution.py:375
  668.8 118.8 %collective-permute-start.28 = (bf16[3,13,32,16,128]{4,3,2,1,0:T(8,128)(2,1)}, bf16[3,13,32,16,128]{4,3,2,1,0:T(8,128)(2,1)}, u32[]{:S(2)}, u32[]{:S(2)}) collective-permute-start(bf16[3,13,32,16,128]{4,3,2,1,0:T(8,128)(2,1)} %get-tuple-element.114), channel_id=1, source_target_pairs={{1,0},{2,1},{3,2},{5,4},{6,5},{7,6}} | collective-permute-start | bytes 15335432 | tf_op jit(solution)/shard_map/ppermute | solution.py:376
  673.1 64.0 %collective-permute-start.25 = (bf16[3,3,32,16,128]{4,3,2,1,0:T(8,128)(2,1)}, bf16[3,3,32,16,128]{4,3,2,1,0:T(8,128)(2,1)S(1)}, u32[]{:S(2)}, u32[]{:S(2)}) collective-permute-start(bf16[3,3,32,16,128]{4,3,2,1,0:T(8,128)(2,1)} %get-tuple-element.111), channel_id=1, source_target_pairs={{0,1},{1,2},{2,3},{4,5},{5,6},{6,7}} | collective-permute-start | bytes 3538952 | tf_op jit(solution)/shard_map/ppermute | solution.py:375
  675.0 66.6 %collective-permute-start.26 = (bf16[3,3,32,16,128]{4,3,2,1,0:T(8,128)(2,1)}, bf16[3,3,32,16,128]{4,3,2,1,0:T(8,128)(2,1)S(1)}, u32[]{:S(2)}, u32[]{:S(2)}) collective-permute-start(bf16[3,3,32,16,128]{4,3,2,1,0:T(8,128)(2,1)} %get-tuple-element.112), channel_id=1, source_target_pairs={{1,0},{2,1},{3,2},{5,4},{6,5},{7,6}} | collective-permute-start | bytes 3538952 | tf_op jit(solution)/shard_map/ppermute | solution.py:376
  748.8 59.0 %collective-permute-start.29 = (bf16[8,3,32,16,128]{4,3,2,1,0:T(8,128)(2,1)}, bf16[8,3,32,16,128]{4,3,2,1,0:T(8,128)(2,1)S(1)}, u32[]{:S(2)}, u32[]{:S(2)}) collective-permute-start(bf16[8,3,32,16,128]{4,3,2,1,0:T(8,128)(2,1)} %shard_map.62.edge_ref), channel_id=1, source_target_pairs={{0,4},{4,0},{1,5},{5,1},{2,6},{6,2},{3,7},{7,3}} | collective-permute-start | bytes 9437192 | tf_op jit(solution)/shard_map/ppermute | solution.py:404
  787.6 61.0 %collective-permute-start.34 = (bf16[8,8,32,16,128]{4,3,2,1,0:T(8,128)(2,1)}, bf16[8,8,32,16,128]{4,3,2,1,0:T(8,128)(2,1)}, u32[]{:S(2)}, u32[]{:S(2)}) collective-permute-start(bf16[8,8,32,16,128]{4,3,2,1,0:T(8,128)(2,1)} %get-tuple-element.124), channel_id=1, source_target_pairs={{0,1},{1,0},{2,3},{3,2},{4,5},{5,4},{6,7},{7,6}} | collective-permute-start | bytes 25165832 | tf_op jit(solution)/shard_map/ppermute | solution.py:426
  848.1 41.1 %collective-permute-start.30 = (bf16[8,8,32,16,128]{4,3,2,1,0:T(8,128)(2,1)}, bf16[8,8,32,16,128]{4,3,2,1,0:T(8,128)(2,1)}, u32[]{:S(2)}, u32[]{:S(2)}) collective-permute-start(bf16[8,8,32,16,128]{4,3,2,1,0:T(8,128)(2,1)} %get-tuple-element.117), channel_id=1, source_target_pairs={{0,1},{1,0},{2,3},{3,2},{4,5},{5,4},{6,7},{7,6}} | collective-permute-start | bytes 25165832 | tf_op jit(solution)/shard_map/ppermute | solution.py:426
  (17 other events, 166.7 us)

commit v2 on v1

--- a/solution.py
+++ b/solution.py
@@ -91,7 +91,7 @@
             scratch[pl.ds(pl.multiple_of((base + n) * PITCH, 8), j_len), :] = pair
         return 0
 
-    lax.fori_loop(0, side, fill, 0, unroll=8)
+    lax.fori_loop(0, side, fill, 0, unroll=16)
 
     def group(g, _):
         tiles = [scratch[pl.ds(g * SUB + j, lanes, stride=PITCH), :].T.astype(BF) for j in range(SUB)]
@@ -107,7 +107,7 @@
         return 0
 
     groups = j_len // SUB
-    lax.fori_loop(0, groups, group, 0, unroll=4)
+    lax.fori_loop(0, groups, group, 0, unroll=8)
     hg = upn_ref.shape[0]
     upn_ref[...] = filt_ref[groups - hg:, :hg]
     upd_ref[...] = filt_ref[groups - hg:, hg:]
@@ -164,7 +164,7 @@
             scratch[pl.ds(g * SUB + j, lanes, stride=PITCH), :] = tile.T
         return 0
 
-    lax.fori_loop(0, j_len // SUB, group, 0, unroll=4)
+    lax.fori_loop(0, j_len // SUB, group, 0, unroll=8)
 
     def drain(n, _):
         for base, where in ((0, half), (side, 1 - half)):
@@ -174,7 +174,7 @@
             raw_ref[0, 1, n, at] = pair[:, k_len:]
         return 0
 
-    lax.fori_loop(0, side, drain, 0, unroll=8)
+    lax.fori_loop(0, side, drain, 0, unroll=16)
 
 
 def leave(own, other, vol_idx, result, half, perm, full_shape):
@@ -267,7 +267,7 @@
             unit[edge:, 2 * n + m] = tail[:, cut].reshape(-1, ROWS, lanes)
         return 0
 
-    lax.fori_loop(0, chans // 2, channel_pair, 0, unroll=4)
+    lax.fori_loop(0, chans // 2, channel_pair, 0, unroll=chans // 2)
 
     def group_pair(n, _):
         k0, k1 = (n, n + groups // 2) if last else (2 * n, 2 * n + 1)
@@ -287,17 +287,29 @@
             own_ref[0, n] = shaped(jnp.where(is_low, low, high))
             other_ref[0, n] = shaped(jnp.where(is_low, high, low))
         else:
-            iband_ref, new_ref, filt_ref = refs[:3]
+            new_ref = refs[1]
             new_ref[0, k0], new_ref[0, k1] = shaped(new[:, :lanes]), shaped(new[:, lanes:])
-            filt = jnp.dot(new, iband_ref[...], preferred_element_type=F32).astype(BF)
-            filt_ref[0, k0], filt_ref[0, k1] = shaped(filt[:, :lanes]), shaped(filt[:, lanes:])
         return 0
 
     lax.fori_loop(0, groups // 2, group_pair, 0, unroll=4)
 
     if not last:
-        filt_ref, upn_ref, upd_ref, dnn_ref, dnd_ref = refs[2:7]
+        iband_ref, new_ref, filt_ref, upn_ref, upd_ref, dnn_ref, dnd_ref = refs[:7]
         g = pl.program_id(0)
+        many = groups // 2
+
+        def along_i(n, _):
+            first = n * many
+            pairs = [interleave(new_ref[0, first + q].reshape(-1, lanes), new_ref[0, first + many // 2 + q].reshape(-1, lanes))
+                     for q in range(many // 2)]
+            filt = jnp.dot(jnp.concatenate(pairs, axis=0), iband_ref[...], preferred_element_type=F32).astype(BF)
+            side_by_side = (filt[:, :lanes], filt[:, lanes:])
+            for m in range(2):
+                at = pl.ds(first + m * (many // 2), many // 2)
+                filt_ref[0, at] = side_by_side[m].reshape(many // 2, chans, ROWS, lanes)
+            return 0
+
+        lax.fori_loop(0, groups // many, along_i, 0, unroll=2)
 
         @pl.when(g < edge)
         def _():

time: 935 us -> 866 us (0.926)
  Pallas kernels: 613 us -> 540 us
    pallas_call x6, Pallas kernels: 284 us -> 236 us  [finish(): pl.pallas_call(functools.partial(finish_kernel, last), out_shape=out_shap...]
    pallas_call x2, Pallas kernels: 81.3 us -> 65.3 us  [leave(): pl.pallas_call(leave_kernel, out_shape=shape_of(*full_shape), grid_spec=p...]
  transfers between devices with their start and end apart: 35 -> 35, of which waited for: 9 -> 9; matrix products, arithmetic and copies ran while one was open for 2% -> 2% of each run, Pallas kernels for 62% -> 59%
where the time goes in v2:
time: 866 us; the launch traced here: 860 us
  Pallas kernels  540 us (62%)
  waiting for transfers between devices  204 us (24%)
  starting transfers between devices  72.5 us (8%)
  local copies, waits for them, and re-layouts  38.5 us (4%)
    pallas_call x6, Pallas kernels, finish(): pl.pallas_call(functools.partial(finish_kernel, last), out_shape=out_shap...  236 us
    ppermute x12, waiting for transfers between devices, local_layers(): up = lambda a: lax.ppermute(a, ('py', 'px'), upward)  175 us
    pallas_call x12, Pallas kernels, along_j(): pl.pallas_call(along_j_kernel, out_shape=shape_of(jg, count, chans, rows,...  157 us
    pallas_call x3, Pallas kernels, enter(): pl.pallas_call(enter_kernel, out_shape=[shape_of(*s, chans, ROWS, 2 * sid...  76.2 us
    pallas_call x2, Pallas kernels, leave(): pl.pallas_call(leave_kernel, out_shape=shape_of(*full_shape), grid_spec=p...  65.3 us
    ppermute x12, starting transfers between devices, local_layers(): down = lambda a: lax.ppermute(a, ('py', 'px'), downward)  36.6 us
    ppermute x12, starting transfers between devices, local_layers(): up = lambda a: lax.ppermute(a, ('py', 'px'), upward)  30.5 us
    dynamic_slice x2, local copies, waits for them, and re-layouts, local_layers(): lax.dynamic_slice(volumes, (v, p * width, 0, (1 - px) * j_len, 0), (1, wi...  27.2 us
  transfers between devices with their start and end apart: 35, of which 9 were waited for; matrix products, arithmetic and copies ran while one was open for 2% of the time, Pallas kernels for 59%

profile of v2, /device:TPU:1, one launch (start us, length us, event | category | flops | bytes accessed | tf_op | source)
XLA Modules:
  0.0 859.7 jit_solution(16484297218740783937)
XLA Ops:
  0.0 12.2 %constant_dynamic-slice_fusion = (bf16[1,16,64,32,64]{4,3,2,1,0:T(8,128)(2,1)}, bf16[1,16,64,32,64]{4,3,2,1,0:T(8,128)(2,1)}) fusion(bf16[2,32,64,64,64]{4,3,2,1,0:T(8,128)(2,1)} %own_ref.5, s32[]{:T(128)S(6)} %select_n.80), kind=kLoop, calls=%fused_computation.67 | loop fusion | bytes 16777220 | tf_op jit(solution)/shard_map/dynamic_slice | solution.py:396
  12.2 15.0 %constant_dynamic-slice_fusion.2 = bf16[1,32,64,32,64]{4,3,2,1,0:T(8,128)(2,1)} fusion(bf16[2,32,64,64,64]{4,3,2,1,0:T(8,128)(2,1)} %own_ref.5, s32[]{:T(128)S(6)} %select_n.80), kind=kLoop, calls=%fused_computation.69 | loop fusion | bytes 16777220 | tf_op jit(solution)/shard_map/dynamic_slice | solution.py:396
  28.3 5.1 bands.1
  34.7 19.6 %shard_map.47 = (bf16[8,16,32,16,128]{4,3,2,1,0:T(8,128)(2,1)}, bf16[8,16,32,16,128]{4,3,2,1,0:T(8,128)(2,1)}, bf16[3,3,32,16,128]{4,3,2,1,0:T(8,128)(2,1)}, bf1...) custom-call(s32[1]{0:T(128)} %bitcast.half_ref, ...), custom_call_target="tpu_custom_call" | custom-call | flops 16000000000 | bytes 40000000 | tf_op jit(solution)/shard_map/pallas_call | solution.py:125
  54.3 10.5 %collective-permute-done.1.other_ref = bf16[1,16,64,32,64]{4,3,2,1,0:T(8,128)(2,1)} collective-permute-done((bf16[1,16,64,32,64]{4,3,2,1,0:T(8,128)(2,1)}, bf16[1,16,64,32,64]{4,3,2,1,0:T(8,128)(2,1)}, u32[]{:S(2)}, u32[]{:S(2)}) %collective-permute-start.1) | collective-permute-done | bytes 4194336 | tf_op jit(solution)/shard_map/ppermute | solution.py:398
  64.9 19.6 %shard_map.48 = (bf16[8,16,32,16,128]{4,3,2,1,0:T(8,128)(2,1)}, bf16[8,16,32,16,128]{4,3,2,1,0:T(8,128)(2,1)}, bf16[3,3,32,16,128]{4,3,2,1,0:T(8,128)(2,1)}, bf1...) custom-call(s32[1]{0:T(128)} %bitcast.half_ref, ...), custom_call_target="tpu_custom_call", output_to_operand_aliasing={{0}: (5, {}), {1}: (6, {}), {2}: (7, {}), {3}: (8, {}), {4}... | custom-call | flops 16000000000 | bytes 40000000 | tf_op jit(solution)/shard_map/pallas_call | solution.py:125
  99.6 57.6 %collective-permute-done.7.low_ref = bf16[3,3,32,16,128]{4,3,2,1,0:T(8,128)(2,1)} collective-permute-done((bf16[3,3,32,16,128]{4,3,2,1,0:T(8,128)(2,1)}, bf16[3,3,32,16,128]{4,3,2,1,0:T(8,128)(2,1)}, u32[]{:S(2)}, u32[]{:S(2)}) %collective-permute-start.7) | collective-permute-done | bytes 1179680 | tf_op jit(solution)/shard_map/ppermute | solution.py:387
  161.6 6.0 shard_map.51.edge_ref
  168.9 37.0 %shard_map.46 = (bf16[8,16,32,16,128]{4,3,2,1,0:T(8,128)(2,1)}, bf16[8,16,32,16,128]{4,3,2,1,0:T(8,128)(2,1)}, bf16[3,3,32,16,128]{4,3,2,1,0:T(8,128)(2,1)}, bf1...) custom-call(s32[1]{0:T(128)} %bitcast.half_ref, ...), custom_call_target="tpu_custom_call" | custom-call | flops 32000000000 | bytes 80000000 | tf_op jit(solution)/shard_map/pallas_call | solution.py:125
  217.1 20.2 %shard_map.49.rest_ref = bf16[8,13,32,16,128]{4,3,2,1,0:T(8,128)(2,1)} custom-call(bf16[8,16,32,16,128]{4,3,2,1,0:T(8,128)(2,1)} %get-tuple-element.73.field_ref, bf16[3,13,32,16,128]{4,3,2,1,0:T(8,128)(2,1)} %collective-permute-done.3.low_ref, bf16[3,13,32,16,128]{4,3,2,1,0:T(8,128)(2,1)} %collective-permute-done.4.high_ref, ...), custom_call_target="tpu_custom_call" | custom-call | flops 12999999488 | bytes 37700000 | tf_op jit(solution)/shard_map/pallas_call | solution.py:227
  237.2 38.9 %collective-permute-done.5.low_ref = bf16[3,3,32,16,128]{4,3,2,1,0:T(8,128)(2,1)S(1)} collective-permute-done((bf16[3,3,32,16,128]{4,3,2,1,0:T(8,128)(2,1)}, bf16[3,3,32,16,128]{4,3,2,1,0:T(8,128)(2,1)S(1)}, u32[]{:S(2)}, u32[]{:S(2)}) %collective-permute-start.5) | collective-permute-done | bytes 1179680 | tf_op jit(solution)/shard_map/ppermute | solution.py:387
  276.1 4.7 collective-permute-done.6.high_ref
  281.8 6.1 shard_map.50.edge_ref
  289.3 41.3 %shard_map.52 = (bf16[8,16,32,16,128]{4,3,2,1,0:T(8,128)(2,1)}, bf16[8,16,32,16,128]{4,3,2,1,0:T(8,128)(2,1)}, bf16[3,3,32,16,128]{4,3,2,1,0:T(8,128)(2,1)}, bf1...) custom-call(bf16[8,3,32,16,128]{4,3,2,1,0:T(8,128)(2,1)} %shard_map.5, ...), custom_call_target="tpu_custom_call" | custom-call | flops 40000000000 | bytes 75000000 | tf_op jit(solution)/shard_map/pallas_call | solution.py:348
  341.6 20.2 %shard_map.53.rest_ref = bf16[8,13,32,16,128]{4,3,2,1,0:T(8,128)(2,1)} custom-call(bf16[8,16,32,16,128]{4,3,2,1,0:T(8,128)(2,1)} %get-tuple-element.77.field_ref, bf16[3,13,32,16,128]{4,3,2,1,0:T(8,128)(2,1)} %collective-permute-done.10.low_ref, bf16[3,13,32,16,128]{4,3,2,1,0:T(8,128)(2,1)} %collective-permute-done.11.high_ref, ...), custom_call_target="tpu_custom_call" | custom-call | flops 12999999488 | bytes 37700000 | tf_op jit(solution)/shard_map/pallas_call | solution.py:227
  363.8 6.1 shard_map.57.edge_ref
  371.1 41.4 %shard_map.54 = (bf16[8,16,32,16,128]{4,3,2,1,0:T(8,128)(2,1)}, bf16[8,16,32,16,128]{4,3,2,1,0:T(8,128)(2,1)}, bf16[3,3,32,16,128]{4,3,2,1,0:T(8,128)(2,1)}, bf1...) custom-call(bf16[8,3,32,16,128]{4,3,2,1,0:T(8,128)(2,1)} %shard_map.5, ...), custom_call_target="tpu_custom_call" | custom-call | flops 40000000000 | bytes 75000000 | tf_op jit(solution)/shard_map/pallas_call | solution.py:348
  423.4 20.2 %shard_map.55.rest_ref = bf16[8,13,32,16,128]{4,3,2,1,0:T(8,128)(2,1)} custom-call(bf16[8,16,32,16,128]{4,3,2,1,0:T(8,128)(2,1)} %get-tuple-element.97.field_ref, bf16[3,13,32,16,128]{4,3,2,1,0:T(8,128)(2,1)} %collective-permute-done.13.low_ref, bf16[3,13,32,16,128]{4,3,2,1,0:T(8,128)(2,1)} %collective-permute-done.14.high_ref, ...), custom_call_target="tpu_custom_call" | custom-call | flops 12999999488 | bytes 37700000 | tf_op jit(solution)/shard_map/pallas_call | solution.py:227
  443.6 39.4 %collective-permute-done.15.low_ref = bf16[3,3,32,16,128]{4,3,2,1,0:T(8,128)(2,1)S(1)} collective-permute-done((bf16[3,3,32,16,128]{4,3,2,1,0:T(8,128)(2,1)}, bf16[3,3,32,16,128]{4,3,2,1,0:T(8,128)(2,1)S(1)}, u32[]{:S(2)}, u32[]{:S(2)}) %collective-permute-start.15) | collective-permute-done | bytes 1179680 | tf_op jit(solution)/shard_map/ppermute | solution.py:387
  488.8 6.1 shard_map.56.edge_ref
  495.1 41.1 %shard_map.58 = (bf16[8,16,32,16,128]{4,3,2,1,0:T(8,128)(2,1)}, bf16[8,16,32,16,128]{4,3,2,1,0:T(8,128)(2,1)}, bf16[3,3,32,16,128]{4,3,2,1,0:T(8,128)(2,1)}, bf1...) custom-call(bf16[8,3,32,16,128]{4,3,2,1,0:T(8,128)(2,1)} %shard_map.5, ...), custom_call_target="tpu_custom_call" | custom-call | flops 40000000000 | bytes 75000000 | tf_op jit(solution)/shard_map/pallas_call | solution.py:348
  547.5 20.2 %shard_map.59.rest_ref = bf16[8,13,32,16,128]{4,3,2,1,0:T(8,128)(2,1)} custom-call(bf16[8,16,32,16,128]{4,3,2,1,0:T(8,128)(2,1)} %get-tuple-element.94.field_ref, bf16[3,13,32,16,128]{4,3,2,1,0:T(8,128)(2,1)} %collective-permute-done.20.low_ref, bf16[3,13,32,16,128]{4,3,2,1,0:T(8,128)(2,1)} %collective-permute-done.21.high_ref, ...), custom_call_target="tpu_custom_call" | custom-call | flops 12999999488 | bytes 37700000 | tf_op jit(solution)/shard_map/pallas_call | solution.py:227
  569.7 6.1 shard_map.65.edge_ref
  577.0 41.2 %shard_map.60 = (bf16[8,16,32,16,128]{4,3,2,1,0:T(8,128)(2,1)}, bf16[8,16,32,16,128]{4,3,2,1,0:T(8,128)(2,1)}, bf16[3,3,32,16,128]{4,3,2,1,0:T(8,128)(2,1)}, bf1...) custom-call(bf16[8,3,32,16,128]{4,3,2,1,0:T(8,128)(2,1)} %shard_map.5, ...), custom_call_target="tpu_custom_call" | custom-call | flops 40000000000 | bytes 75000000 | tf_op jit(solution)/shard_map/pallas_call | solution.py:348
  629.2 20.2 %shard_map.61.rest_ref = bf16[8,13,32,16,128]{4,3,2,1,0:T(8,128)(2,1)} custom-call(bf16[8,16,32,16,128]{4,3,2,1,0:T(8,128)(2,1)} %get-tuple-element.118.field_ref, bf16[3,13,32,16,128]{4,3,2,1,0:T(8,128)(2,1)} %collective-permute-done.23.low_ref, bf16[3,13,32,16,128]{4,3,2,1,0:T(8,128)(2,1)} %collective-permute-done.24.high_ref, ...), custom_call_target="tpu_custom_call" | custom-call | flops 12999999488 | bytes 37700000 | tf_op jit(solution)/shard_map/pallas_call | solution.py:227
  649.4 39.4 %collective-permute-done.25.low_ref = bf16[3,3,32,16,128]{4,3,2,1,0:T(8,128)(2,1)S(1)} collective-permute-done((bf16[3,3,32,16,128]{4,3,2,1,0:T(8,128)(2,1)}, bf16[3,3,32,16,128]{4,3,2,1,0:T(8,128)(2,1)S(1)}, u32[]{:S(2)}, u32[]{:S(2)}) %collective-permute-start.25) | collective-permute-done | bytes 1179680 | tf_op jit(solution)/shard_map/ppermute | solution.py:387
  694.4 6.1 shard_map.62.edge_ref
  700.8 35.6 %shard_map.66 = (bf16[8,8,32,16,128]{4,3,2,1,0:T(8,128)(2,1)}, bf16[8,8,32,16,128]{4,3,2,1,0:T(8,128)(2,1)}) custom-call(bf16[8,3,32,16,128]{4,3,2,1,0:T(8,128)(2,1)} %shard_map.65.edge_ref, bf16[8,13,32,16,128]{4,3,2,1,0:T(8,128)(2,1)} %shard_map.61.rest_ref, bf16[8,3,32,16,128]{4,3,2,1,0:T(8,128)(2,1)} %collective-permute-done.33.halo_ref, ...), custom_call_target="tpu_custom_call" | custom-call | flops 40000000000 | bytes 75000000 | tf_op jit(solution)/shard_map/pallas_call | solution.py:348
  736.4 20.2 %shard_map.63.rest_ref = bf16[8,13,32,16,128]{4,3,2,1,0:T(8,128)(2,1)} custom-call(bf16[8,16,32,16,128]{4,3,2,1,0:T(8,128)(2,1)} %get-tuple-element.110.field_ref, bf16[3,13,32,16,128]{4,3,2,1,0:T(8,128)(2,1)} %collective-permute-done.27.low_ref, bf16[3,13,32,16,128]{4,3,2,1,0:T(8,128)(2,1)} %collective-permute-done.28.high_ref, ...), custom_call_target="tpu_custom_call" | custom-call | flops 12999999488 | bytes 37700000 | tf_op jit(solution)/shard_map/pallas_call | solution.py:227
  758.2 35.7 %shard_map.64 = (bf16[8,8,32,16,128]{4,3,2,1,0:T(8,128)(2,1)}, bf16[8,8,32,16,128]{4,3,2,1,0:T(8,128)(2,1)}) custom-call(bf16[8,3,32,16,128]{4,3,2,1,0:T(8,128)(2,1)} %shard_map.62.edge_ref, bf16[8,13,32,16,128]{4,3,2,1,0:T(8,128)(2,1)} %shard_map.63.rest_ref, bf16[8,3,32,16,128]{4,3,2,1,0:T(8,128)(2,1)} %copy-done.13, ...), custom_call_target="tpu_custom_call" | custom-call | flops 40000000000 | bytes 75000000 | tf_op jit(solution)/shard_map/pallas_call | solution.py:348
  794.4 32.6 %shard_map.67.refs_0_ = bf16[2,32,64,64,64]{4,3,2,1,0:T(8,128)(2,1)} custom-call(s32[1]{0:T(128)} %bitcast.half_ref, bf16[8,8,32,16,128]{4,3,2,1,0:T(8,128)(2,1)} %get-tuple-element.123.own_ref, bf16[8,8,32,16,128]{4,3,2,1,0:T(8,128)(2,1)} %collective-permute-done.34.other_ref, bf16[256,256]{1,0:T(8,128)(2,1)} %get-tuple-element.127.perm_ref), custom_call_target="tpu_custom_call" | custom-call | flops 30000001024 | bytes 50000000 | tf_op jit(solution)/shard_map/pallas_call | solution.py:191
  827.1 32.6 %shard_map.68 = bf16[2,32,64,64,64]{4,3,2,1,0:T(8,128)(2,1)} custom-call(s32[1]{0:T(128)} %bitcast.half_ref, bf16[8,8,32,16,128]{4,3,2,1,0:T(8,128)(2,1)} %get-tuple-element.116.own_ref, bf16[8,8,32,16,128]{4,3,2,1,0:T(8,128)(2,1)} %collective-permute-done.30.other_ref, ...), custom_call_target="tpu_custom_call", output_to_operand_aliasing={{}: (4, {})} | custom-call | flops 30000001024 | bytes 50000000 | tf_op jit(solution)/shard_map/pallas_call | solution.py:191
  (111 shorter events, 101.1 us)
Async XLA Ops:
  27.2 141.6 %collective-permute-start = (bf16[1,32,64,32,64]{4,3,2,1,0:T(8,128)(2,1)}, bf16[1,32,64,32,64]{4,3,2,1,0:T(8,128)(2,1)}, u32[]{:S(2)}, u32[]{:S(2)}) collective-permute-start(bf16[1,32,64,32,64]{4,3,2,1,0:T(8,128)(2,1)} %constant_dynamic-slice_fusion.2), channel_id=1, source_target_pairs={{0,1},{1,0},{2,3},{3,2},{4,5},{5,4},{6,7},{7,6}} | collective-permute-start | bytes 25165832 | tf_op jit(solution)/shard_map/ppermute | solution.py:398
  27.7 37.1 %collective-permute-start.1 = (bf16[1,16,64,32,64]{4,3,2,1,0:T(8,128)(2,1)}, bf16[1,16,64,32,64]{4,3,2,1,0:T(8,128)(2,1)}, u32[]{:S(2)}, u32[]{:S(2)}) collective-permute-start(bf16[1,16,64,32,64]{4,3,2,1,0:T(8,128)(2,1)} %get-tuple-element.126), channel_id=1, source_target_pairs={{0,1},{1,0},{2,3},{3,2},{4,5},{5,4},{6,7},{7,6}} | collective-permute-start | bytes 12582920 | tf_op jit(solution)/shard_map/ppermute | solution.py:398
  84.5 128.0 %collective-permute-start.3 = (bf16[3,13,32,16,128]{4,3,2,1,0:T(8,128)(2,1)}, bf16[3,13,32,16,128]{4,3,2,1,0:T(8,128)(2,1)}, u32[]{:S(2)}, u32[]{:S(2)}) collective-permute-start(bf16[3,13,32,16,128]{4,3,2,1,0:T(8,128)(2,1)} %get-tuple-element.74), channel_id=1, source_target_pairs={{0,1},{1,2},{2,3},{4,5},{5,6},{6,7}} | collective-permute-start | bytes 15335432 | tf_op jit(solution)/shard_map/ppermute | solution.py:387
  89.0 125.4 %collective-permute-start.4 = (bf16[3,13,32,16,128]{4,3,2,1,0:T(8,128)(2,1)}, bf16[3,13,32,16,128]{4,3,2,1,0:T(8,128)(2,1)}, u32[]{:S(2)}, u32[]{:S(2)}) collective-permute-start(bf16[3,13,32,16,128]{4,3,2,1,0:T(8,128)(2,1)} %get-tuple-element.75), channel_id=1, source_target_pairs={{1,0},{2,1},{3,2},{5,4},{6,5},{7,6}} | collective-permute-start | bytes 15335432 | tf_op jit(solution)/shard_map/ppermute | solution.py:388
  91.1 66.1 %collective-permute-start.7 = (bf16[3,3,32,16,128]{4,3,2,1,0:T(8,128)(2,1)}, bf16[3,3,32,16,128]{4,3,2,1,0:T(8,128)(2,1)}, u32[]{:S(2)}, u32[]{:S(2)}) collective-permute-start(bf16[3,3,32,16,128]{4,3,2,1,0:T(8,128)(2,1)} %get-tuple-element.80), channel_id=1, source_target_pairs={{0,1},{1,2},{2,3},{4,5},{5,6},{6,7}} | collective-permute-start | bytes 3538952 | tf_op jit(solution)/shard_map/ppermute | solution.py:387
  94.6 67.0 %collective-permute-start.8 = (bf16[3,3,32,16,128]{4,3,2,1,0:T(8,128)(2,1)}, bf16[3,3,32,16,128]{4,3,2,1,0:T(8,128)(2,1)}, u32[]{:S(2)}, u32[]{:S(2)}) collective-permute-start(bf16[3,3,32,16,128]{4,3,2,1,0:T(8,128)(2,1)} %get-tuple-element.81), channel_id=1, source_target_pairs={{1,0},{2,1},{3,2},{5,4},{6,5},{7,6}} | collective-permute-start | bytes 3538952 | tf_op jit(solution)/shard_map/ppermute | solution.py:388
  167.6 120.5 %collective-permute-start.9 = (bf16[8,3,32,16,128]{4,3,2,1,0:T(8,128)(2,1)}, bf16[8,3,32,16,128]{4,3,2,1,0:T(8,128)(2,1)}, u32[]{:S(2)}, u32[]{:S(2)}) collective-permute-start(bf16[8,3,32,16,128]{4,3,2,1,0:T(8,128)(2,1)} %shard_map.51.edge_ref), channel_id=1, source_target_pairs={{0,4},{4,0},{1,5},{5,1},{2,6},{6,2},{3,7},{7,3}} | collective-permute-start | bytes 9437192 | tf_op jit(solution)/shard_map/ppermute | solution.py:416
  205.9 129.1 %collective-permute-start.10 = (bf16[3,13,32,16,128]{4,3,2,1,0:T(8,128)(2,1)}, bf16[3,13,32,16,128]{4,3,2,1,0:T(8,128)(2,1)}, u32[]{:S(2)}, u32[]{:S(2)}) collective-permute-start(bf16[3,13,32,16,128]{4,3,2,1,0:T(8,128)(2,1)} %get-tuple-element.87), channel_id=1, source_target_pairs={{0,1},{1,2},{2,3},{4,5},{5,6},{6,7}} | collective-permute-start | bytes 15335432 | tf_op jit(solution)/shard_map/ppermute | solution.py:387
  207.9 130.2 %collective-permute-start.11 = (bf16[3,13,32,16,128]{4,3,2,1,0:T(8,128)(2,1)}, bf16[3,13,32,16,128]{4,3,2,1,0:T(8,128)(2,1)}, u32[]{:S(2)}, u32[]{:S(2)}) collective-permute-start(bf16[3,13,32,16,128]{4,3,2,1,0:T(8,128)(2,1)} %get-tuple-element.88), channel_id=1, source_target_pairs={{1,0},{2,1},{3,2},{5,4},{6,5},{7,6}} | collective-permute-start | bytes 15335432 | tf_op jit(solution)/shard_map/ppermute | solution.py:388
  212.4 63.7 %collective-permute-start.5 = (bf16[3,3,32,16,128]{4,3,2,1,0:T(8,128)(2,1)}, bf16[3,3,32,16,128]{4,3,2,1,0:T(8,128)(2,1)S(1)}, u32[]{:S(2)}, u32[]{:S(2)}) collective-permute-start(bf16[3,3,32,16,128]{4,3,2,1,0:T(8,128)(2,1)} %get-tuple-element.78), channel_id=1, source_target_pairs={{0,1},{1,2},{2,3},{4,5},{5,6},{6,7}} | collective-permute-start | bytes 3538952 | tf_op jit(solution)/shard_map/ppermute | solution.py:387
  214.4 66.4 %collective-permute-start.6 = (bf16[3,3,32,16,128]{4,3,2,1,0:T(8,128)(2,1)}, bf16[3,3,32,16,128]{4,3,2,1,0:T(8,128)(2,1)S(1)}, u32[]{:S(2)}, u32[]{:S(2)}) collective-permute-start(bf16[3,3,32,16,128]{4,3,2,1,0:T(8,128)(2,1)} %get-tuple-element.79), channel_id=1, source_target_pairs={{1,0},{2,1},{3,2},{5,4},{6,5},{7,6}} | collective-permute-start | bytes 3538952 | tf_op jit(solution)/shard_map/ppermute | solution.py:388
  287.9 83.2 %collective-permute-start.12 = (bf16[8,3,32,16,128]{4,3,2,1,0:T(8,128)(2,1)}, bf16[8,3,32,16,128]{4,3,2,1,0:T(8,128)(2,1)}, u32[]{:S(2)}, u32[]{:S(2)}) collective-permute-start(bf16[8,3,32,16,128]{4,3,2,1,0:T(8,128)(2,1)} %shard_map.50.edge_ref), channel_id=1, source_target_pairs={{0,4},{4,0},{1,5},{5,1},{2,6},{6,2},{3,7},{7,3}} | collective-permute-start | bytes 9437192 | tf_op jit(solution)/shard_map/ppermute | solution.py:416
  330.6 31.2 %collective-permute-start.17 = (bf16[3,3,32,16,128]{4,3,2,1,0:T(8,128)(2,1)}, bf16[3,3,32,16,128]{4,3,2,1,0:T(8,128)(2,1)S(1)}, u32[]{:S(2)}, u32[]{:S(2)}) collective-permute-start(bf16[3,3,32,16,128]{4,3,2,1,0:T(8,128)(2,1)} %get-tuple-element.98), channel_id=1, source_target_pairs={{0,1},{1,2},{2,3},{4,5},{5,6},{6,7}} | collective-permute-start | bytes 3538952 | tf_op jit(solution)/shard_map/ppermute | solution.py:387
  335.0 84.0 %collective-permute-start.13 = (bf16[3,13,32,16,128]{4,3,2,1,0:T(8,128)(2,1)}, bf16[3,13,32,16,128]{4,3,2,1,0:T(8,128)(2,1)}, u32[]{:S(2)}, u32[]{:S(2)}) collective-permute-start(bf16[3,13,32,16,128]{4,3,2,1,0:T(8,128)(2,1)} %get-tuple-element.92), channel_id=1, source_target_pairs={{0,1},{1,2},{2,3},{4,5},{5,6},{6,7}} | collective-permute-start | bytes 15335432 | tf_op jit(solution)/shard_map/ppermute | solution.py:387
  338.1 82.8 %collective-permute-start.14 = (bf16[3,13,32,16,128]{4,3,2,1,0:T(8,128)(2,1)}, bf16[3,13,32,16,128]{4,3,2,1,0:T(8,128)(2,1)}, u32[]{:S(2)}, u32[]{:S(2)}) collective-permute-start(bf16[3,13,32,16,128]{4,3,2,1,0:T(8,128)(2,1)} %get-tuple-element.93), channel_id=1, source_target_pairs={{1,0},{2,1},{3,2},{5,4},{6,5},{7,6}} | collective-permute-start | bytes 15335432 | tf_op jit(solution)/shard_map/ppermute | solution.py:388
  369.8 125.3 %collective-permute-start.19 = (bf16[8,3,32,16,128]{4,3,2,1,0:T(8,128)(2,1)}, bf16[8,3,32,16,128]{4,3,2,1,0:T(8,128)(2,1)}, u32[]{:S(2)}, u32[]{:S(2)}) collective-permute-start(bf16[8,3,32,16,128]{4,3,2,1,0:T(8,128)(2,1)} %shard_map.57.edge_ref), channel_id=1, source_target_pairs={{0,4},{4,0},{1,5},{5,1},{2,6},{6,2},{3,7},{7,3}} | collective-permute-start | bytes 9437192 | tf_op jit(solution)/shard_map/ppermute | solution.py:416
  412.4 128.2 %collective-permute-start.20 = (bf16[3,13,32,16,128]{4,3,2,1,0:T(8,128)(2,1)}, bf16[3,13,32,16,128]{4,3,2,1,0:T(8,128)(2,1)}, u32[]{:S(2)}, u32[]{:S(2)}) collective-permute-start(bf16[3,13,32,16,128]{4,3,2,1,0:T(8,128)(2,1)} %get-tuple-element.103), channel_id=1, source_target_pairs={{0,1},{1,2},{2,3},{4,5},{5,6},{6,7}} | collective-permute-start | bytes 15335432 | tf_op jit(solution)/shard_map/ppermute | solution.py:387
  414.8 129.0 %collective-permute-start.21 = (bf16[3,13,32,16,128]{4,3,2,1,0:T(8,128)(2,1)}, bf16[3,13,32,16,128]{4,3,2,1,0:T(8,128)(2,1)}, u32[]{:S(2)}, u32[]{:S(2)}) collective-permute-start(bf16[3,13,32,16,128]{4,3,2,1,0:T(8,128)(2,1)} %get-tuple-element.104), channel_id=1, source_target_pairs={{1,0},{2,1},{3,2},{5,4},{6,5},{7,6}} | collective-permute-start | bytes 15335432 | tf_op jit(solution)/shard_map/ppermute | solution.py:388
  419.0 64.0 %collective-permute-start.15 = (bf16[3,3,32,16,128]{4,3,2,1,0:T(8,128)(2,1)}, bf16[3,3,32,16,128]{4,3,2,1,0:T(8,128)(2,1)S(1)}, u32[]{:S(2)}, u32[]{:S(2)}) collective-permute-start(bf16[3,3,32,16,128]{4,3,2,1,0:T(8,128)(2,1)} %get-tuple-element.95), channel_id=1, source_target_pairs={{0,1},{1,2},{2,3},{4,5},{5,6},{6,7}} | collective-permute-start | bytes 3538952 | tf_op jit(solution)/shard_map/ppermute | solution.py:387
  420.9 66.8 %collective-permute-start.16 = (bf16[3,3,32,16,128]{4,3,2,1,0:T(8,128)(2,1)}, bf16[3,3,32,16,128]{4,3,2,1,0:T(8,128)(2,1)S(1)}, u32[]{:S(2)}, u32[]{:S(2)}) collective-permute-start(bf16[3,3,32,16,128]{4,3,2,1,0:T(8,128)(2,1)} %get-tuple-element.96), channel_id=1, source_target_pairs={{1,0},{2,1},{3,2},{5,4},{6,5},{7,6}} | collective-permute-start | bytes 3538952 | tf_op jit(solution)/shard_map/ppermute | solution.py:388
  494.9 82.1 %collective-permute-start.22 = (bf16[8,3,32,16,128]{4,3,2,1,0:T(8,128)(2,1)}, bf16[8,3,32,16,128]{4,3,2,1,0:T(8,128)(2,1)}, u32[]{:S(2)}, u32[]{:S(2)}) collective-permute-start(bf16[8,3,32,16,128]{4,3,2,1,0:T(8,128)(2,1)} %shard_map.56.edge_ref), channel_id=1, source_target_pairs={{0,4},{4,0},{1,5},{5,1},{2,6},{6,2},{3,7},{7,3}} | collective-permute-start | bytes 9437192 | tf_op jit(solution)/shard_map/ppermute | solution.py:416
  536.2 31.4 %collective-permute-start.31 = (bf16[3,3,32,16,128]{4,3,2,1,0:T(8,128)(2,1)}, bf16[3,3,32,16,128]{4,3,2,1,0:T(8,128)(2,1)S(1)}, u32[]{:S(2)}, u32[]{:S(2)}) collective-permute-start(bf16[3,3,32,16,128]{4,3,2,1,0:T(8,128)(2,1)} %get-tuple-element.119), channel_id=1, source_target_pairs={{0,1},{1,2},{2,3},{4,5},{5,6},{6,7}} | collective-permute-start | bytes 3538952 | tf_op jit(solution)/shard_map/ppermute | solution.py:387
  540.7 84.1 %collective-permute-start.23 = (bf16[3,13,32,16,128]{4,3,2,1,0:T(8,128)(2,1)}, bf16[3,13,32,16,128]{4,3,2,1,0:T(8,128)(2,1)}, u32[]{:S(2)}, u32[]{:S(2)}) collective-permute-start(bf16[3,13,32,16,128]{4,3,2,1,0:T(8,128)(2,1)} %get-tuple-element.108), channel_id=1, source_target_pairs={{0,1},{1,2},{2,3},{4,5},{5,6},{6,7}} | collective-permute-start | bytes 15335432 | tf_op jit(solution)/shard_map/ppermute | solution.py:387
  543.8 82.9 %collective-permute-start.24 = (bf16[3,13,32,16,128]{4,3,2,1,0:T(8,128)(2,1)}, bf16[3,13,32,16,128]{4,3,2,1,0:T(8,128)(2,1)}, u32[]{:S(2)}, u32[]{:S(2)}) collective-permute-start(bf16[3,13,32,16,128]{4,3,2,1,0:T(8,128)(2,1)} %get-tuple-element.109), channel_id=1, source_target_pairs={{1,0},{2,1},{3,2},{5,4},{6,5},{7,6}} | collective-permute-start | bytes 15335432 | tf_op jit(solution)/shard_map/ppermute | solution.py:388
  575.7 125.0 %collective-permute-start.33 = (bf16[8,3,32,16,128]{4,3,2,1,0:T(8,128)(2,1)}, bf16[8,3,32,16,128]{4,3,2,1,0:T(8,128)(2,1)}, u32[]{:S(2)}, u32[]{:S(2)}) collective-permute-start(bf16[8,3,32,16,128]{4,3,2,1,0:T(8,128)(2,1)} %shard_map.65.edge_ref), channel_id=1, source_target_pairs={{0,4},{4,0},{1,5},{5,1},{2,6},{6,2},{3,7},{7,3}} | collective-permute-start | bytes 9437192 | tf_op jit(solution)/shard_map/ppermute | solution.py:416
  618.2 118.2 %collective-permute-start.27 = (bf16[3,13,32,16,128]{4,3,2,1,0:T(8,128)(2,1)}, bf16[3,13,32,16,128]{4,3,2,1,0:T(8,128)(2,1)}, u32[]{:S(2)}, u32[]{:S(2)}) collective-permute-start(bf16[3,13,32,16,128]{4,3,2,1,0:T(8,128)(2,1)} %get-tuple-element.113), channel_id=1, source_target_pairs={{0,1},{1,2},{2,3},{4,5},{5,6},{6,7}} | collective-permute-start | bytes 15335432 | tf_op jit(solution)/shard_map/ppermute | solution.py:387
  620.6 115.8 %collective-permute-start.28 = (bf16[3,13,32,16,128]{4,3,2,1,0:T(8,128)(2,1)}, bf16[3,13,32,16,128]{4,3,2,1,0:T(8,128)(2,1)}, u32[]{:S(2)}, u32[]{:S(2)}) collective-permute-start(bf16[3,13,32,16,128]{4,3,2,1,0:T(8,128)(2,1)} %get-tuple-element.114), channel_id=1, source_target_pairs={{1,0},{2,1},{3,2},{5,4},{6,5},{7,6}} | collective-permute-start | bytes 15335432 | tf_op jit(solution)/shard_map/ppermute | solution.py:388
  624.8 64.0 %collective-permute-start.25 = (bf16[3,3,32,16,128]{4,3,2,1,0:T(8,128)(2,1)}, bf16[3,3,32,16,128]{4,3,2,1,0:T(8,128)(2,1)S(1)}, u32[]{:S(2)}, u32[]{:S(2)}) collective-permute-start(bf16[3,3,32,16,128]{4,3,2,1,0:T(8,128)(2,1)} %get-tuple-element.111), channel_id=1, source_target_pairs={{0,1},{1,2},{2,3},{4,5},{5,6},{6,7}} | collective-permute-start | bytes 3538952 | tf_op jit(solution)/shard_map/ppermute | solution.py:387
  626.7 66.7 %collective-permute-start.26 = (bf16[3,3,32,16,128]{4,3,2,1,0:T(8,128)(2,1)}, bf16[3,3,32,16,128]{4,3,2,1,0:T(8,128)(2,1)S(1)}, u32[]{:S(2)}, u32[]{:S(2)}) collective-permute-start(bf16[3,3,32,16,128]{4,3,2,1,0:T(8,128)(2,1)} %get-tuple-element.112), channel_id=1, source_target_pairs={{1,0},{2,1},{3,2},{5,4},{6,5},{7,6}} | collective-permute-start | bytes 3538952 | tf_op jit(solution)/shard_map/ppermute | solution.py:388
  700.5 56.0 %collective-permute-start.29 = (bf16[8,3,32,16,128]{4,3,2,1,0:T(8,128)(2,1)}, bf16[8,3,32,16,128]{4,3,2,1,0:T(8,128)(2,1)S(1)}, u32[]{:S(2)}, u32[]{:S(2)}) collective-permute-start(bf16[8,3,32,16,128]{4,3,2,1,0:T(8,128)(2,1)} %shard_map.62.edge_ref), channel_id=1, source_target_pairs={{0,4},{4,0},{1,5},{5,1},{2,6},{6,2},{3,7},{7,3}} | collective-permute-start | bytes 9437192 | tf_op jit(solution)/shard_map/ppermute | solution.py:416
  736.4 58.0 %collective-permute-start.34 = (bf16[8,8,32,16,128]{4,3,2,1,0:T(8,128)(2,1)}, bf16[8,8,32,16,128]{4,3,2,1,0:T(8,128)(2,1)}, u32[]{:S(2)}, u32[]{:S(2)}) collective-permute-start(bf16[8,8,32,16,128]{4,3,2,1,0:T(8,128)(2,1)} %get-tuple-element.124), channel_id=1, source_target_pairs={{0,1},{1,0},{2,3},{3,2},{4,5},{5,4},{6,7},{7,6}} | collective-permute-start | bytes 25165832 | tf_op jit(solution)/shard_map/ppermute | solution.py:438
  793.9 33.1 %collective-permute-start.30 = (bf16[8,8,32,16,128]{4,3,2,1,0:T(8,128)(2,1)}, bf16[8,8,32,16,128]{4,3,2,1,0:T(8,128)(2,1)}, u32[]{:S(2)}, u32[]{:S(2)}) collective-permute-start(bf16[8,8,32,16,128]{4,3,2,1,0:T(8,128)(2,1)} %get-tuple-element.117), channel_id=1, source_target_pairs={{0,1},{1,0},{2,3},{3,2},{4,5},{5,4},{6,7},{7,6}} | collective-permute-start | bytes 25165832 | tf_op jit(solution)/shard_map/ppermute | solution.py:438
  (17 other events, 164.3 us)

commit v3 on v2

--- a/solution.py
+++ b/solution.py
@@ -13,6 +13,7 @@
 SUB = 4
 ROWS = SUB * SUB
 PITCH = 40
+CHAN_STEP = 8
 
 
 def shape_of(*dims, dtype=BF):
@@ -79,19 +80,40 @@
     )(taps)
 
 
-def enter_kernel(half_ref, own_ref, other_ref, perm_ref, band_ref, *refs):
-    vol_ref, filt_ref, upn_ref, upd_ref, dnn_ref, dnd_ref, scratch = refs[-7:]
-    side, j_len, k_len = own_ref.shape[2], own_ref.shape[3], own_ref.shape[4]
-    lanes = 2 * side
-    first = half_ref[0] * side
+def enter_kernel(vol_idx, own_ref, raw_ref, perm_ref, band_ref, vol_ref, near_ref, deep_ref, upn_ref, upd_ref, dnn_ref,
+                 dnd_ref, scratch, landing, sent, landed):
+    side, j_all, k_len = own_ref.shape[2], own_ref.shape[3], own_ref.shape[4]
+    j_len, lanes = j_all // 2, 2 * side
+    me = lax.axis_index('px')
+    step, steps = pl.program_id(0), landing.shape[0]
+
+    def to_partner(c):
+        rows = pl.ds(pl.multiple_of((1 - me) * j_len, j_len), j_len)
+        return pltpu.make_async_remote_copy(
+            src_ref=raw_ref.at[vol_idx, pl.ds(2 * c, 2), :, rows, :], dst_ref=landing.at[c],
+            send_sem=sent.at[c], recv_sem=landed.at[c],
+            device_id={'px': 1 - me}, device_id_type=pl.DeviceIdType.MESH)
+
+    @pl.when(step == 0)
+    def _():
+        barrier = pltpu.get_barrier_semaphore()
+        pl.semaphore_signal(barrier, inc=1, device_id={'px': 1 - me}, device_id_type=pl.DeviceIdType.MESH)
+        pl.semaphore_wait(barrier, 1)
+        for c in range(steps):
+            to_partner(c).start()
+
+    to_partner(step).wait_recv()
+    own_rows = pl.ds(pl.multiple_of(me * j_len, j_len), j_len)
 
     def fill(n, _):
-        for base, ref in ((first, own_ref), (side - first, other_ref)):
-            pair = interleave(ref[0, 0, n], ref[0, 1, n]).astype(F32)
-            scratch[pl.ds(pl.multiple_of((base + n) * PITCH, 8), j_len), :] = pair
+        mine = interleave(own_ref[0, 0, n, own_rows], own_ref[0, 1, n, own_rows])
+        theirs = interleave(landing[step, 0, n], landing[step, 1, n])
+        for base, pair in ((me * side, mine), ((1 - me) * side, theirs)):
+            scratch[pl.ds(pl.multiple_of((base + n) * PITCH, 8), j_len), :] = pair.astype(F32)
         return 0
 
     lax.fori_loop(0, side, fill, 0, unroll=16)
+    edge_rows = near_ref.shape[1] * ROWS
 
     def group(g, _):
         tiles = [scratch[pl.ds(g * SUB + j, lanes, stride=PITCH), :].T.astype(BF) for j in range(SUB)]
@@ -102,45 +124,53 @@
         mixed = jnp.dot(perm_ref[...], columns, preferred_element_type=F32).astype(BF)
         filtered = jnp.dot(mixed, band_ref[...], preferred_element_type=F32).astype(BF)
         for m in range(2):
-            vol_ref[g, :, m] = mixed[:, m * lanes:(m + 1) * lanes].reshape(-1, ROWS, lanes)
-            filt_ref[g, :, m] = filtered[:, m * lanes:(m + 1) * lanes].reshape(-1, ROWS, lanes)
+            cut = slice(m * lanes, (m + 1) * lanes)
+            vol_ref[g, :, m] = mixed[:, cut].reshape(-1, ROWS, lanes)
+            near_ref[g, :, m] = filtered[:edge_rows, cut].reshape(-1, ROWS, lanes)
+            deep_ref[g, :, m] = filtered[edge_rows:, cut].reshape(-1, ROWS, lanes)
         return 0
 
     groups = j_len // SUB
     lax.fori_loop(0, groups, group, 0, unroll=8)
     hg = upn_ref.shape[0]
-    upn_ref[...] = filt_ref[groups - hg:, :hg]
-    upd_ref[...] = filt_ref[groups - hg:, hg:]
-    dnn_ref[...] = filt_ref[:hg, :hg]
-    dnd_ref[...] = filt_ref[:hg, hg:]
-
-
-def enter(volumes, vol_idx, other, chan_at, before, half, perm, band, hg):
+    upn_ref[...] = near_ref[groups - hg:]
+    upd_ref[...] = deep_ref[groups - hg:]
+    dnn_ref[...] = near_ref[:hg]
+    dnd_ref[...] = deep_ref[:hg]
+
+    @pl.when(step == steps - 1)
+    def _():
+        for c in range(steps):
+            to_partner(c).wait_send()
+
+
+def enter(volumes, vol_idx, perm, band, hg):
     _, chans, side, j_all, k_len = volumes.shape
     j_len = j_all // 2
     jg, kg = j_len // SUB, k_len // SUB
-    at = chan_at // 2
-    sizes = [(jg, kg), (jg, kg), (hg, hg), (hg, kg - hg), (hg, hg), (hg, kg - hg)]
-    before = before or []
+    steps = chans // 2
+    sizes = [(jg, kg), (jg, hg), (jg, kg - hg), (hg, hg), (hg, kg - hg), (hg, hg), (hg, kg - hg)]
     return pl.pallas_call(
-        enter_kernel,
+        functools.partial(enter_kernel, vol_idx),
         out_shape=[shape_of(*s, chans, ROWS, 2 * side) for s in sizes],
-        grid_spec=pltpu.PrefetchScalarGridSpec(
-            num_scalar_prefetch=1,
-            grid=(other.shape[1] // 2,),
-            in_specs=[
-                pl.BlockSpec((1, 2, side, j_len, k_len), lambda c, h: (vol_idx, c + at, 0, h[0], 0)),
-                pl.BlockSpec((1, 2, side, j_len, k_len), lambda c, h: (0, c, 0, 0, 0)),
-                pl.BlockSpec(perm.shape, lambda c, h: (0, 0)),
-                pl.BlockSpec((None,) + band.shape[1:], lambda c, h: (0, 0, 0)),
-            ] + [pl.BlockSpec(memory_space=pl.ANY)] * len(before),
-            out_specs=[pl.BlockSpec(s + (2, ROWS, 2 * side), lambda c, h: (0, 0, c + at, 0, 0)) for s in sizes],
-            scratch_shapes=[pltpu.VMEM((2 * side * PITCH, 2 * k_len), F32)],
-        ),
-        input_output_aliases={5 + n: n for n in range(len(before))},
-        compiler_params=pltpu.CompilerParams(dimension_semantics=("arbitrary",)),
-        cost_estimate=pl.CostEstimate(flops=other.shape[1] * 1_000_000_000, bytes_accessed=other.shape[1] * 2_500_000, transcendentals=0),
-    )(half, volumes, other, perm, band, *before)
+        grid=(steps,),
+        in_specs=[
+            pl.BlockSpec((1, 2, side, j_all, k_len), lambda c: (vol_idx, c, 0, 0, 0)),
+            pl.BlockSpec(memory_space=pl.ANY),
+            pl.BlockSpec(perm.shape, lambda c: (0, 0)),
+            pl.BlockSpec((None,) + band.shape[1:], lambda c: (0, 0, 0)),
+        ],
+        out_specs=[pl.BlockSpec(s + (2, ROWS, 2 * side), lambda c: (0, 0, c, 0, 0)) for s in sizes],
+        scratch_shapes=[
+            pltpu.VMEM((2 * side * PITCH, 2 * k_len), F32),
+            pltpu.VMEM((steps, 2, side, j_len, k_len), BF),
+            pltpu.SemaphoreType.DMA((steps,)),
+            pltpu.SemaphoreType.DMA((steps,)),
+        ],
+        compiler_params=pltpu.CompilerParams(
+            dimension_semantics=("arbitrary",), collective_id=vol_idx, has_side_effects=True),
+        cost_estimate=pl.CostEstimate(flops=chans * 1_000_000_000, bytes_accessed=chans * 2_500_000, transcendentals=0),
+    )(volumes, volumes, perm, band)
 
 
 def leave_kernel(half_ref, own_ref, other_ref, perm_ref, *refs):
@@ -205,36 +235,30 @@
 
 
 def along_j_kernel(field_ref, low_ref, high_ref, band_ref, out_ref):
-    chans, lanes = field_ref.shape[2], field_ref.shape[4]
-
-    def pair(n, _):
-        halves = []
-        for m in range(2):
-            c = 2 * n + m
-            halves.append(jnp.concatenate(
-                [ref[:, 0, c].reshape(-1, lanes) for ref in (low_ref, field_ref, high_ref)], axis=0))
-        total = jnp.dot(band_ref[...], interleave(*halves), preferred_element_type=F32).astype(BF)
-        for m in range(2):
-            out_ref[:, 0, 2 * n + m] = total[:, m * lanes:(m + 1) * lanes].reshape(-1, ROWS, lanes)
-        return 0
-
-    lax.fori_loop(0, chans // 2, pair, 0, unroll=4)
-
-
-def along_j(field, low, high, band, layer, first):
-    jg, _, chans, rows, lanes = field.shape
-    halo, count = low.shape[:2]
+    count, chans, lanes = field_ref.shape[1], field_ref.shape[2], field_ref.shape[4]
+
+    def group(k, _):
+        for first in range(0, chans, 2):
+            halves = [jnp.concatenate([ref[:, k, c].reshape(-1, lanes) for ref in (low_ref, field_ref, high_ref)], axis=0)
+                      for c in (first, first + 1)]
+            total = jnp.dot(band_ref[...], interleave(*halves), preferred_element_type=F32).astype(BF)
+            for m in range(2):
+                out_ref[:, k, first + m] = total[:, m * lanes:(m + 1) * lanes].reshape(-1, ROWS, lanes)
+        return 0
+
+    lax.fori_loop(0, count, group, 0)
+
+
+def along_j(field, low, high, band, layer):
+    _, count, chans, rows, lanes = field.shape
+    width = CHAN_STEP
+    block = lambda a: pl.BlockSpec((a.shape[0], count, width, rows, lanes), lambda c: (0, 0, c, 0, 0))
     return pl.pallas_call(
         along_j_kernel,
-        out_shape=shape_of(jg, count, chans, rows, lanes),
-        grid=(count,),
-        in_specs=[
-            pl.BlockSpec((jg, 1, chans, rows, lanes), lambda g: (0, g + first, 0, 0, 0)),
-            pl.BlockSpec((halo, 1, chans, rows, lanes), lambda g: (0, g, 0, 0, 0)),
-            pl.BlockSpec((halo, 1, chans, rows, lanes), lambda g: (0, g, 0, 0, 0)),
-            pl.BlockSpec((None,) + band.shape[1:], lambda g: (layer, 0, 0)),
-        ],
-        out_specs=pl.BlockSpec((jg, 1, chans, rows, lanes), lambda g: (0, g, 0, 0, 0)),
+        out_shape=shape_of(*field.shape),
+        grid=(chans // width,),
+        in_specs=[block(field), block(low), block(high), pl.BlockSpec((None,) + band.shape[1:], lambda c: (layer, 0, 0))],
+        out_specs=block(field),
         compiler_params=pltpu.CompilerParams(dimension_semantics=("arbitrary",)),
         cost_estimate=pl.CostEstimate(flops=count * 1_000_000_000, bytes_accessed=count * 2_900_000, transcendentals=0),
     )(field, low, high, band)
@@ -294,32 +318,32 @@
     lax.fori_loop(0, groups // 2, group_pair, 0, unroll=4)
 
     if not last:
-        iband_ref, new_ref, filt_ref, upn_ref, upd_ref, dnn_ref, dnd_ref = refs[:7]
+        iband_ref, new_ref, near_ref, deep_ref, upn_ref, upd_ref, dnn_ref, dnd_ref = refs[:8]
         g = pl.program_id(0)
         many = groups // 2
 
-        def along_i(n, _):
-            first = n * many
+        for first in range(0, groups, many):
             pairs = [interleave(new_ref[0, first + q].reshape(-1, lanes), new_ref[0, first + many // 2 + q].reshape(-1, lanes))
                      for q in range(many // 2)]
             filt = jnp.dot(jnp.concatenate(pairs, axis=0), iband_ref[...], preferred_element_type=F32).astype(BF)
-            side_by_side = (filt[:, :lanes], filt[:, lanes:])
             for m in range(2):
-                at = pl.ds(first + m * (many // 2), many // 2)
-                filt_ref[0, at] = side_by_side[m].reshape(many // 2, chans, ROWS, lanes)
-            return 0
-
-        lax.fori_loop(0, groups // many, along_i, 0, unroll=2)
+                groups_of = filt[:, m * lanes:(m + 1) * lanes].reshape(many // 2, chans, ROWS, lanes)
+                at = first + m * (many // 2)
+                cut = min(max(edge - at, 0), many // 2)
+                if cut > 0:
+                    near_ref[0, at:at + cut] = groups_of[:cut]
+                if cut < many // 2:
+                    deep_ref[0, at + cut - edge:at + many // 2 - edge] = groups_of[cut:]
 
         @pl.when(g < edge)
         def _():
-            dnn_ref[0] = filt_ref[0, :edge]
-            dnd_ref[0] = filt_ref[0, edge:]
+            dnn_ref[0] = near_ref[0]
+            dnd_ref[0] = deep_ref[0]
 
         @pl.when(g >= pl.num_programs(0) - edge)
         def _():
-            upn_ref[0] = filt_ref[0, :edge]
-            upd_ref[0] = filt_ref[0, edge:]
+            upn_ref[0] = near_ref[0]
+            upd_ref[0] = deep_ref[0]
 
 
 def finish(edge, rest, halo, vol, layer, band, halo_band, mix, bias, iband):
@@ -337,8 +361,8 @@
     else:
         operands.append(iband)
         in_specs.append(of_layer(iband, layer + 1))
-        out_shape = [shape_of(*vol.shape)] * 2
-        out_specs = [block(vol)] * 2
+        out_shape = [shape_of(*vol.shape), shape_of(*edge.shape), shape_of(*rest.shape)]
+        out_specs = [block(vol), block(edge), block(rest)]
         up = lambda g: (jnp.maximum(g - (jg - hg), 0), 0, 0, 0, 0)
         down = lambda g: (jnp.minimum(g, hg - 1), 0, 0, 0, 0)
         for index in (up, down):
@@ -389,19 +413,11 @@
 
         states = []
         for v in range(count):
-            pieces = 2 if v == 0 else 1
-            width = chans // pieces
-            outs = None
-            for p in range(pieces):
-                sent = lax.dynamic_slice(
-                    volumes, (v, p * width, 0, (1 - px) * j_len, 0), (1, width, side, j_len, k_len))
-                other = lax.ppermute(sent, 'px', swap)
-                outs = enter(volumes, v, other, p * width, outs, half_idx, perm, iband, hg)
-            states.append(outs)
+            states.append(enter(volumes, v, perm, iband, hg))
         result = None
 
         def send_j(v):
-            _, _, up_near, up_deep, down_near, down_deep = states[v]
+            up_near, up_deep, down_near, down_deep = states[v][3:]
             moved = []
             for move, part in ((up, up_near), (down, down_near),
                                      (up, up_deep), (down, down_deep)):
@@ -412,13 +428,13 @@
             filt = states[v][1]
             if after is not None:
                 filt, after = lax.optimization_barrier((filt, after))
-            edge = along_j(filt, *halos[v][:2], jband, l, 0)
+            edge = along_j(filt, *halos[v][:2], jband, l)
             return edge, lax.ppermute(edge, 'pz', swap), after
 
         halos = [send_j(v) for v in range(count)]
         edges = [edge_of(0, 0, None)] + [None] * (count - 1)
         rests = [None] * count
-        rests[0] = along_j(states[0][1], *halos[0][2:], jband, 0, hg)
+        rests[0] = along_j(states[0][2], *halos[0][2:], jband, 0)
         for step in range(count * layers):
             l, v = divmod(step, count)
             nl, nv = divmod(step + 1, count)
@@ -432,7 +448,7 @@
             if l + 1 < layers:
                 halos[v] = send_j(v)
             if nl < layers:
-                rests[nv] = along_j(states[nv][1], *halos[nv][2:], jband, nl, hg)
+                rests[nv] = along_j(states[nv][2], *halos[nv][2:], jband, nl)
         for v in range(count):
             own, other = states[v]
             other = lax.ppermute(other, 'px', swap)

time: 866 us -> 652 us (0.75)
  waiting for transfers between devices: 204 us -> 25.8 us
  local copies, waits for them, and re-layouts: 38.5 us -> 12.5 us
  Pallas kernels: 540 us -> 530 us
    ppermute x12, waiting for transfers between devices: 175 us -> 4.85 us  [local_layers(): up = lambda a: lax.ppermute(a, ('py', 'px'), upward)]
    dynamic_slice x2 -> x0, local copies, waits for them, and re-layouts: 27.2 us -> none  [local_layers(): lax.dynamic_slice(volumes, (v, p * width, 0, (1 - px) * j_len, 0), (1, wi...]
    ppermute x6, waiting for transfers between devices: 0.02 us -> 14.6 us  [edge_of(): return (edge, lax.ppermute(edge, 'pz', swap), after)]
    ppermute x12, waiting for transfers between devices: 18.4 us -> 6.34 us  [local_layers(): down = lambda a: lax.ppermute(a, ('py', 'px'), downward)]
    pallas_call x15 -> x14, Pallas kernels: 234 us -> 223 us  [the longest x12 141 us: along_j(): pl.pallas_call(along_j_kernel, out_shape=shape_of(*field.shape), grid=(ch...]
    ppermute x3 -> x0, waiting for transfers between devices: 10.5 us -> none  [local_layers(): other = lax.ppermute(sent, 'px', swap)]
  transfers between devices with their start and end apart: 35 -> 32, of which waited for: 9 -> 4; matrix products, arithmetic and copies ran while one was open for 2% -> 1% of each run, Pallas kernels for 59% -> 70%
where the time goes in v3:
time: 652 us; the launch traced here: 648 us
  Pallas kernels  530 us (81%)
  starting transfers between devices  75.7 us (12%)
  waiting for transfers between devices  25.8 us (4%)
  local copies, waits for them, and re-layouts  12.5 us (2%)
    pallas_call x6, Pallas kernels, finish(): pl.pallas_call(functools.partial(finish_kernel, last), out_shape=out_shap...  236 us
    pallas_call x12, Pallas kernels, along_j(): pl.pallas_call(along_j_kernel, out_shape=shape_of(*field.shape), grid=(ch...  141 us
    pallas_call x2, Pallas kernels, enter(): pl.pallas_call(functools.partial(enter_kernel, vol_idx), out_shape=[shape...  82 us
    pallas_call x2, Pallas kernels, leave(): pl.pallas_call(leave_kernel, out_shape=shape_of(*full_shape), grid_spec=p...  65.3 us
    ppermute x12, starting transfers between devices, local_layers(): down = lambda a: lax.ppermute(a, ('py', 'px'), downward)  39.8 us
    ppermute x12, starting transfers between devices, local_layers(): up = lambda a: lax.ppermute(a, ('py', 'px'), upward)  31.1 us
    ppermute x6, waiting for transfers between devices, edge_of(): return (edge, lax.ppermute(edge, 'pz', swap), after)  14.6 us
  transfers between devices with their start and end apart: 32, of which 4 were waited for; matrix products, arithmetic and copies ran while one was open for 1% of the time, Pallas kernels for 70%

profile of v3, /device:TPU:1, one launch (start us, length us, event | category | flops | bytes accessed | tf_op | source)
XLA Modules:
  0.0 648.2 jit_solution(13203989523619151528)
XLA Ops:
  1.3 5.2 bands.1
  7.6 41.0 %shard_map.47 = (bf16[8,16,32,16,128]{4,3,2,1,0:T(8,128)(2,1)}, bf16[8,3,32,16,128]{4,3,2,1,0:T(8,128)(2,1)}, bf16[8,13,32,16,128]{4,3,2,1,0:T(8,128)(2,1)}, bf1...) custom-call(bf16[2,32,64,64,64]{4,3,2,1,0:T(8,128)(2,1)} %raw_ref.3,, ...), custom_call_target="tpu_custom_call" | custom-call | flops 32000000000 | bytes 80000000 | tf_op jit(solution)/shard_map/pallas_call | solution.py:153
  48.7 4.3 collective-permute-start.4
  54.9 3.6 collective-permute-start
  61.6 4.8 collective-permute-done.4.low_ref
  66.4 4.3 collective-permute-done.5.high_ref
  71.8 6.0 shard_map.50.edge_ref
  79.0 40.9 %shard_map.46 = (bf16[8,16,32,16,128]{4,3,2,1,0:T(8,128)(2,1)}, bf16[8,3,32,16,128]{4,3,2,1,0:T(8,128)(2,1)}, bf16[8,13,32,16,128]{4,3,2,1,0:T(8,128)(2,1)}, bf1...) custom-call(bf16[2,32,64,64,64]{4,3,2,1,0:T(8,128)(2,1)} %raw_ref.3,, ...), custom_call_target="tpu_custom_call" | custom-call | flops 32000000000 | bytes 80000000 | tf_op jit(solution)/shard_map/pallas_call | solution.py:153
  130.5 4.5 collective-permute-start.8
  135.0 17.6 %shard_map.48.rest_ref = bf16[8,13,32,16,128]{4,3,2,1,0:T(8,128)(2,1)} custom-call(bf16[8,13,32,16,128]{4,3,2,1,0:T(8,128)(2,1)} %get-tuple-element.67.field_ref, bf16[3,13,32,16,128]{4,3,2,1,0:T(8,128)(2,1)} %collective-permute-done.low_ref, bf16[3,13,32,16,128]{4,3,2,1,0:T(8,128)(2,1)} %collective-permute-done.1.high_ref, ...), custom_call_target="tpu_custom_call" | custom-call | flops 12999999488 | bytes 37700000 | tf_op jit(solution)/shard_map/pallas_call | solution.py:256
  152.6 6.0 shard_map.49.edge_ref
  159.9 41.1 %shard_map.51 = (bf16[8,16,32,16,128]{4,3,2,1,0:T(8,128)(2,1)}, bf16[8,3,32,16,128]{4,3,2,1,0:T(8,128)(2,1)}, bf16[8,13,32,16,128]{4,3,2,1,0:T(8,128)(2,1)}, bf1...) custom-call(bf16[8,3,32,16,128]{4,3,2,1,0:T(8,128)(2,1)} %shard_map., ...), custom_call_target="tpu_custom_call" | custom-call | flops 40000000000 | bytes 75000000 | tf_op jit(solution)/shard_map/pallas_call | solution.py:372
  208.6 4.6 collective-permute-start.11
  213.2 17.5 %shard_map.52.rest_ref = bf16[8,13,32,16,128]{4,3,2,1,0:T(8,128)(2,1)} custom-call(bf16[8,13,32,16,128]{4,3,2,1,0:T(8,128)(2,1)} %get-tuple-element.82.field_ref, bf16[3,13,32,16,128]{4,3,2,1,0:T(8,128)(2,1)} %collective-permute-done.7.low_ref, bf16[3,13,32,16,128]{4,3,2,1,0:T(8,128)(2,1)} %collective-permute-done.8.high_ref, ...), custom_call_target="tpu_custom_call" | custom-call | flops 12999999488 | bytes 37700000 | tf_op jit(solution)/shard_map/pallas_call | solution.py:256
  230.7 6.0 shard_map.56.edge_ref
  239.6 41.4 %shard_map.53 = (bf16[8,16,32,16,128]{4,3,2,1,0:T(8,128)(2,1)}, bf16[8,3,32,16,128]{4,3,2,1,0:T(8,128)(2,1)}, bf16[8,13,32,16,128]{4,3,2,1,0:T(8,128)(2,1)}, bf1...) custom-call(bf16[8,3,32,16,128]{4,3,2,1,0:T(8,128)(2,1)} %shard_map., ...), custom_call_target="tpu_custom_call" | custom-call | flops 40000000000 | bytes 75000000 | tf_op jit(solution)/shard_map/pallas_call | solution.py:372
  292.0 17.5 %shard_map.54.rest_ref = bf16[8,13,32,16,128]{4,3,2,1,0:T(8,128)(2,1)} custom-call(bf16[8,13,32,16,128]{4,3,2,1,0:T(8,128)(2,1)} %get-tuple-element.88.field_ref, bf16[3,13,32,16,128]{4,3,2,1,0:T(8,128)(2,1)} %collective-permute-done.10.low_ref, bf16[3,13,32,16,128]{4,3,2,1,0:T(8,128)(2,1)} %collective-permute-done.11.high_ref, ...), custom_call_target="tpu_custom_call" | custom-call | flops 12999999488 | bytes 37700000 | tf_op jit(solution)/shard_map/pallas_call | solution.py:256
  311.5 5.9 shard_map.55.edge_ref
  317.7 41.3 %shard_map.57 = (bf16[8,16,32,16,128]{4,3,2,1,0:T(8,128)(2,1)}, bf16[8,3,32,16,128]{4,3,2,1,0:T(8,128)(2,1)}, bf16[8,13,32,16,128]{4,3,2,1,0:T(8,128)(2,1)}, bf1...) custom-call(bf16[8,3,32,16,128]{4,3,2,1,0:T(8,128)(2,1)} %shard_map., ...), custom_call_target="tpu_custom_call" | custom-call | flops 40000000000 | bytes 75000000 | tf_op jit(solution)/shard_map/pallas_call | solution.py:372
  367.0 3.9 collective-permute-start.21
  370.9 17.5 %shard_map.58.rest_ref = bf16[8,13,32,16,128]{4,3,2,1,0:T(8,128)(2,1)} custom-call(bf16[8,13,32,16,128]{4,3,2,1,0:T(8,128)(2,1)} %get-tuple-element.100.field_ref, bf16[3,13,32,16,128]{4,3,2,1,0:T(8,128)(2,1)} %collective-permute-done.17.low_ref, bf16[3,13,32,16,128]{4,3,2,1,0:T(8,128)(2,1)} %collective-permute-done.18.high_ref, ...), custom_call_target="tpu_custom_call" | custom-call | flops 12999999488 | bytes 37700000 | tf_op jit(solution)/shard_map/pallas_call | solution.py:256
  388.4 6.0 shard_map.64.edge_ref
  397.2 41.2 %shard_map.59 = (bf16[8,16,32,16,128]{4,3,2,1,0:T(8,128)(2,1)}, bf16[8,3,32,16,128]{4,3,2,1,0:T(8,128)(2,1)}, bf16[8,13,32,16,128]{4,3,2,1,0:T(8,128)(2,1)}, bf1...) custom-call(bf16[8,3,32,16,128]{4,3,2,1,0:T(8,128)(2,1)} %shard_map., ...), custom_call_target="tpu_custom_call" | custom-call | flops 40000000000 | bytes 75000000 | tf_op jit(solution)/shard_map/pallas_call | solution.py:372
  446.0 3.7 collective-permute-start.25
  449.7 17.6 %shard_map.60.rest_ref = bf16[8,13,32,16,128]{4,3,2,1,0:T(8,128)(2,1)} custom-call(bf16[8,13,32,16,128]{4,3,2,1,0:T(8,128)(2,1)} %get-tuple-element.106.field_ref, bf16[3,13,32,16,128]{4,3,2,1,0:T(8,128)(2,1)} %collective-permute-done.20.low_ref, bf16[3,13,32,16,128]{4,3,2,1,0:T(8,128)(2,1)} %collective-permute-done.21.high_ref, ...), custom_call_target="tpu_custom_call" | custom-call | flops 12999999488 | bytes 37700000 | tf_op jit(solution)/shard_map/pallas_call | solution.py:256
  469.3 6.0 shard_map.61.edge_ref
  475.5 35.6 %shard_map.65 = (bf16[8,8,32,16,128]{4,3,2,1,0:T(8,128)(2,1)}, bf16[8,8,32,16,128]{4,3,2,1,0:T(8,128)(2,1)}) custom-call(bf16[8,3,32,16,128]{4,3,2,1,0:T(8,128)(2,1)} %shard_map.64.edge_ref, bf16[8,13,32,16,128]{4,3,2,1,0:T(8,128)(2,1)} %shard_map.60.rest_ref, bf16[8,3,32,16,128]{4,3,2,1,0:T(8,128)(2,1)} %collective-permute-done.30.halo_ref, ...), custom_call_target="tpu_custom_call" | custom-call | flops 40000000000 | bytes 75000000 | tf_op jit(solution)/shard_map/pallas_call | solution.py:372
  513.2 17.5 %shard_map.62.rest_ref = bf16[8,13,32,16,128]{4,3,2,1,0:T(8,128)(2,1)} custom-call(bf16[8,13,32,16,128]{4,3,2,1,0:T(8,128)(2,1)} %get-tuple-element.112.field_ref, bf16[3,13,32,16,128]{4,3,2,1,0:T(8,128)(2,1)} %collective-permute-done.24.low_ref, bf16[3,13,32,16,128]{4,3,2,1,0:T(8,128)(2,1)} %collective-permute-done.25.high_ref, ...), custom_call_target="tpu_custom_call" | custom-call | flops 12999999488 | bytes 37700000 | tf_op jit(solution)/shard_map/pallas_call | solution.py:256
  530.7 14.6 %collective-permute-done.26.halo_ref = bf16[8,3,32,16,128]{4,3,2,1,0:T(8,128)(2,1)S(1)} collective-permute-done((bf16[8,3,32,16,128]{4,3,2,1,0:T(8,128)(2,1)}, bf16[8,3,32,16,128]{4,3,2,1,0:T(8,128)(2,1)S(1)}, u32[]{:S(2)}, u32[]{:S(2)}) %collective-permute-start.26) | collective-permute-done | bytes 3145760 | tf_op jit(solution)/shard_map/ppermute | solution.py:432
  546.9 35.6 %shard_map.63 = (bf16[8,8,32,16,128]{4,3,2,1,0:T(8,128)(2,1)}, bf16[8,8,32,16,128]{4,3,2,1,0:T(8,128)(2,1)}) custom-call(bf16[8,3,32,16,128]{4,3,2,1,0:T(8,128)(2,1)} %shard_map.61.edge_ref, bf16[8,13,32,16,128]{4,3,2,1,0:T(8,128)(2,1)} %shard_map.62.rest_ref, bf16[8,3,32,16,128]{4,3,2,1,0:T(8,128)(2,1)} %copy-done.4, ...), custom_call_target="tpu_custom_call" | custom-call | flops 40000000000 | bytes 75000000 | tf_op jit(solution)/shard_map/pallas_call | solution.py:372
  583.0 32.6 %shard_map.66.refs_0_ = bf16[2,32,64,64,64]{4,3,2,1,0:T(8,128)(2,1)} custom-call(s32[1]{0:T(128)} %bitcast.half_ref, bf16[8,8,32,16,128]{4,3,2,1,0:T(8,128)(2,1)} %get-tuple-element.123.own_ref, bf16[8,8,32,16,128]{4,3,2,1,0:T(8,128)(2,1)} %collective-permute-done.31.other_ref, bf16[256,256]{1,0:T(8,128)(2,1)} %get-tuple-element.125.perm_ref), custom_call_target="tpu_custom_call" | custom-call | flops 30000001024 | bytes 50000000 | tf_op jit(solution)/shard_map/pallas_call | solution.py:221
  615.6 32.6 %shard_map.67 = bf16[2,32,64,64,64]{4,3,2,1,0:T(8,128)(2,1)} custom-call(s32[1]{0:T(128)} %bitcast.half_ref, bf16[8,8,32,16,128]{4,3,2,1,0:T(8,128)(2,1)} %get-tuple-element.116.own_ref, bf16[8,8,32,16,128]{4,3,2,1,0:T(8,128)(2,1)} %collective-permute-done.27.other_ref, ...), custom_call_target="tpu_custom_call", output_to_operand_aliasing={{}: (4, {})} | custom-call | flops 30000001024 | bytes 50000000 | tf_op jit(solution)/shard_map/pallas_call | solution.py:221
  (96 shorter events, 69.8 us)
Async XLA Ops:
  48.7 17.7 %collective-permute-start.4 = (bf16[3,3,32,16,128]{4,3,2,1,0:T(8,128)(2,1)}, bf16[3,3,32,16,128]{4,3,2,1,0:T(8,128)(2,1)S(1)}, u32[]{:S(2)}, u32[]{:S(2)}) collective-permute-start(bf16[3,3,32,16,128]{4,3,2,1,0:T(8,128)(2,1)} %get-tuple-element.75), channel_id=1, source_target_pairs={{0,1},{1,2},{2,3},{4,5},{5,6},{6,7}} | collective-permute-start | bytes 3538952 | tf_op jit(solution)/shard_map/ppermute | solution.py:411
  53.0 17.7 %collective-permute-start.5 = (bf16[3,3,32,16,128]{4,3,2,1,0:T(8,128)(2,1)}, bf16[3,3,32,16,128]{4,3,2,1,0:T(8,128)(2,1)S(1)}, u32[]{:S(2)}, u32[]{:S(2)}) collective-permute-start(bf16[3,3,32,16,128]{4,3,2,1,0:T(8,128)(2,1)} %get-tuple-element.76), channel_id=1, source_target_pairs={{1,0},{2,1},{3,2},{5,4},{6,5},{7,6}} | collective-permute-start | bytes 3538952 | tf_op jit(solution)/shard_map/ppermute | solution.py:412
  54.9 73.4 %collective-permute-start = (bf16[3,13,32,16,128]{4,3,2,1,0:T(8,128)(2,1)}, bf16[3,13,32,16,128]{4,3,2,1,0:T(8,128)(2,1)}, u32[]{:S(2)}, u32[]{:S(2)}) collective-permute-start(bf16[3,13,32,16,128]{4,3,2,1,0:T(8,128)(2,1)} %get-tuple-element.68), channel_id=1, source_target_pairs={{0,1},{1,2},{2,3},{4,5},{5,6},{6,7}} | collective-permute-start | bytes 15335432 | tf_op jit(solution)/shard_map/ppermute | solution.py:411
  58.6 71.9 %collective-permute-start.1 = (bf16[3,13,32,16,128]{4,3,2,1,0:T(8,128)(2,1)}, bf16[3,13,32,16,128]{4,3,2,1,0:T(8,128)(2,1)}, u32[]{:S(2)}, u32[]{:S(2)}) collective-permute-start(bf16[3,13,32,16,128]{4,3,2,1,0:T(8,128)(2,1)} %get-tuple-element.69), channel_id=1, source_target_pairs={{1,0},{2,1},{3,2},{5,4},{6,5},{7,6}} | collective-permute-start | bytes 15335432 | tf_op jit(solution)/shard_map/ppermute | solution.py:412
  77.7 81.0 %collective-permute-start.6 = (bf16[8,3,32,16,128]{4,3,2,1,0:T(8,128)(2,1)}, bf16[8,3,32,16,128]{4,3,2,1,0:T(8,128)(2,1)}, u32[]{:S(2)}, u32[]{:S(2)}) collective-permute-start(bf16[8,3,32,16,128]{4,3,2,1,0:T(8,128)(2,1)} %shard_map.50.edge_ref), channel_id=1, source_target_pairs={{0,4},{4,0},{1,5},{5,1},{2,6},{6,2},{3,7},{7,3}} | collective-permute-start | bytes 9437192 | tf_op jit(solution)/shard_map/ppermute | solution.py:432
  119.9 32.6 %collective-permute-start.2 = (bf16[3,3,32,16,128]{4,3,2,1,0:T(8,128)(2,1)}, bf16[3,3,32,16,128]{4,3,2,1,0:T(8,128)(2,1)}, u32[]{:S(2)}, u32[]{:S(2)}) collective-permute-start(bf16[3,3,32,16,128]{4,3,2,1,0:T(8,128)(2,1)} %get-tuple-element.72), channel_id=1, source_target_pairs={{0,1},{1,2},{2,3},{4,5},{5,6},{6,7}} | collective-permute-start | bytes 3538952 | tf_op jit(solution)/shard_map/ppermute | solution.py:411
  121.9 30.7 %collective-permute-start.3 = (bf16[3,3,32,16,128]{4,3,2,1,0:T(8,128)(2,1)}, bf16[3,3,32,16,128]{4,3,2,1,0:T(8,128)(2,1)}, u32[]{:S(2)}, u32[]{:S(2)}) collective-permute-start(bf16[3,3,32,16,128]{4,3,2,1,0:T(8,128)(2,1)} %get-tuple-element.73), channel_id=1, source_target_pairs={{1,0},{2,1},{3,2},{5,4},{6,5},{7,6}} | collective-permute-start | bytes 3538952 | tf_op jit(solution)/shard_map/ppermute | solution.py:412
  128.3 78.1 %collective-permute-start.7 = (bf16[3,13,32,16,128]{4,3,2,1,0:T(8,128)(2,1)}, bf16[3,13,32,16,128]{4,3,2,1,0:T(8,128)(2,1)}, u32[]{:S(2)}, u32[]{:S(2)}) collective-permute-start(bf16[3,13,32,16,128]{4,3,2,1,0:T(8,128)(2,1)} %get-tuple-element.83), channel_id=1, source_target_pairs={{0,1},{1,2},{2,3},{4,5},{5,6},{6,7}} | collective-permute-start | bytes 15335432 | tf_op jit(solution)/shard_map/ppermute | solution.py:411
  130.5 78.1 %collective-permute-start.8 = (bf16[3,13,32,16,128]{4,3,2,1,0:T(8,128)(2,1)}, bf16[3,13,32,16,128]{4,3,2,1,0:T(8,128)(2,1)}, u32[]{:S(2)}, u32[]{:S(2)}) collective-permute-start(bf16[3,13,32,16,128]{4,3,2,1,0:T(8,128)(2,1)} %get-tuple-element.84), channel_id=1, source_target_pairs={{1,0},{2,1},{3,2},{5,4},{6,5},{7,6}} | collective-permute-start | bytes 15335432 | tf_op jit(solution)/shard_map/ppermute | solution.py:412
  158.5 79.4 %collective-permute-start.9 = (bf16[8,3,32,16,128]{4,3,2,1,0:T(8,128)(2,1)}, bf16[8,3,32,16,128]{4,3,2,1,0:T(8,128)(2,1)S(1)}, u32[]{:S(2)}, u32[]{:S(2)}) collective-permute-start(bf16[8,3,32,16,128]{4,3,2,1,0:T(8,128)(2,1)} %shard_map.49.edge_ref), channel_id=1, source_target_pairs={{0,4},{4,0},{1,5},{5,1},{2,6},{6,2},{3,7},{7,3}} | collective-permute-start | bytes 9437192 | tf_op jit(solution)/shard_map/ppermute | solution.py:432
  201.1 29.6 %collective-permute-start.14 = (bf16[3,3,32,16,128]{4,3,2,1,0:T(8,128)(2,1)}, bf16[3,3,32,16,128]{4,3,2,1,0:T(8,128)(2,1)}, u32[]{:S(2)}, u32[]{:S(2)}) collective-permute-start(bf16[3,3,32,16,128]{4,3,2,1,0:T(8,128)(2,1)} %get-tuple-element.95), channel_id=1, source_target_pairs={{0,1},{1,2},{2,3},{4,5},{5,6},{6,7}} | collective-permute-start | bytes 3538952 | tf_op jit(solution)/shard_map/ppermute | solution.py:411
  203.0 27.7 %collective-permute-start.15 = (bf16[3,3,32,16,128]{4,3,2,1,0:T(8,128)(2,1)}, bf16[3,3,32,16,128]{4,3,2,1,0:T(8,128)(2,1)}, u32[]{:S(2)}, u32[]{:S(2)}) collective-permute-start(bf16[3,3,32,16,128]{4,3,2,1,0:T(8,128)(2,1)} %get-tuple-element.96), channel_id=1, source_target_pairs={{1,0},{2,1},{3,2},{5,4},{6,5},{7,6}} | collective-permute-start | bytes 3538952 | tf_op jit(solution)/shard_map/ppermute | solution.py:412
  206.5 78.9 %collective-permute-start.10 = (bf16[3,13,32,16,128]{4,3,2,1,0:T(8,128)(2,1)}, bf16[3,13,32,16,128]{4,3,2,1,0:T(8,128)(2,1)}, u32[]{:S(2)}, u32[]{:S(2)}) collective-permute-start(bf16[3,13,32,16,128]{4,3,2,1,0:T(8,128)(2,1)} %get-tuple-element.89), channel_id=1, source_target_pairs={{0,1},{1,2},{2,3},{4,5},{5,6},{6,7}} | collective-permute-start | bytes 15335432 | tf_op jit(solution)/shard_map/ppermute | solution.py:411
  208.6 79.9 %collective-permute-start.11 = (bf16[3,13,32,16,128]{4,3,2,1,0:T(8,128)(2,1)}, bf16[3,13,32,16,128]{4,3,2,1,0:T(8,128)(2,1)}, u32[]{:S(2)}, u32[]{:S(2)}) collective-permute-start(bf16[3,13,32,16,128]{4,3,2,1,0:T(8,128)(2,1)} %get-tuple-element.90), channel_id=1, source_target_pairs={{1,0},{2,1},{3,2},{5,4},{6,5},{7,6}} | collective-permute-start | bytes 15335432 | tf_op jit(solution)/shard_map/ppermute | solution.py:412
  236.7 81.0 %collective-permute-start.16 = (bf16[8,3,32,16,128]{4,3,2,1,0:T(8,128)(2,1)}, bf16[8,3,32,16,128]{4,3,2,1,0:T(8,128)(2,1)}, u32[]{:S(2)}, u32[]{:S(2)}) collective-permute-start(bf16[8,3,32,16,128]{4,3,2,1,0:T(8,128)(2,1)} %shard_map.56.edge_ref), channel_id=1, source_target_pairs={{0,4},{4,0},{1,5},{5,1},{2,6},{6,2},{3,7},{7,3}} | collective-permute-start | bytes 9437192 | tf_op jit(solution)/shard_map/ppermute | solution.py:432
  281.0 28.5 %collective-permute-start.12 = (bf16[3,3,32,16,128]{4,3,2,1,0:T(8,128)(2,1)}, bf16[3,3,32,16,128]{4,3,2,1,0:T(8,128)(2,1)S(1)}, u32[]{:S(2)}, u32[]{:S(2)}) collective-permute-start(bf16[3,3,32,16,128]{4,3,2,1,0:T(8,128)(2,1)} %get-tuple-element.92), channel_id=1, source_target_pairs={{0,1},{1,2},{2,3},{4,5},{5,6},{6,7}} | collective-permute-start | bytes 3538952 | tf_op jit(solution)/shard_map/ppermute | solution.py:411
  282.9 26.6 %collective-permute-start.13 = (bf16[3,3,32,16,128]{4,3,2,1,0:T(8,128)(2,1)}, bf16[3,3,32,16,128]{4,3,2,1,0:T(8,128)(2,1)S(1)}, u32[]{:S(2)}, u32[]{:S(2)}) collective-permute-start(bf16[3,3,32,16,128]{4,3,2,1,0:T(8,128)(2,1)} %get-tuple-element.93), channel_id=1, source_target_pairs={{1,0},{2,1},{3,2},{5,4},{6,5},{7,6}} | collective-permute-start | bytes 3538952 | tf_op jit(solution)/shard_map/ppermute | solution.py:412
  285.4 78.9 %collective-permute-start.17 = (bf16[3,13,32,16,128]{4,3,2,1,0:T(8,128)(2,1)}, bf16[3,13,32,16,128]{4,3,2,1,0:T(8,128)(2,1)}, u32[]{:S(2)}, u32[]{:S(2)}) collective-permute-start(bf16[3,13,32,16,128]{4,3,2,1,0:T(8,128)(2,1)} %get-tuple-element.101), channel_id=1, source_target_pairs={{0,1},{1,2},{2,3},{4,5},{5,6},{6,7}} | collective-permute-start | bytes 15335432 | tf_op jit(solution)/shard_map/ppermute | solution.py:411
  288.5 78.5 %collective-permute-start.18 = (bf16[3,13,32,16,128]{4,3,2,1,0:T(8,128)(2,1)}, bf16[3,13,32,16,128]{4,3,2,1,0:T(8,128)(2,1)}, u32[]{:S(2)}, u32[]{:S(2)}) collective-permute-start(bf16[3,13,32,16,128]{4,3,2,1,0:T(8,128)(2,1)} %get-tuple-element.102), channel_id=1, source_target_pairs={{1,0},{2,1},{3,2},{5,4},{6,5},{7,6}} | collective-permute-start | bytes 15335432 | tf_op jit(solution)/shard_map/ppermute | solution.py:412
  317.5 78.1 %collective-permute-start.19 = (bf16[8,3,32,16,128]{4,3,2,1,0:T(8,128)(2,1)}, bf16[8,3,32,16,128]{4,3,2,1,0:T(8,128)(2,1)S(1)}, u32[]{:S(2)}, u32[]{:S(2)}) collective-permute-start(bf16[8,3,32,16,128]{4,3,2,1,0:T(8,128)(2,1)} %shard_map.55.edge_ref), channel_id=1, source_target_pairs={{0,4},{4,0},{1,5},{5,1},{2,6},{6,2},{3,7},{7,3}} | collective-permute-start | bytes 9437192 | tf_op jit(solution)/shard_map/ppermute | solution.py:432
  359.0 29.4 %collective-permute-start.28 = (bf16[3,3,32,16,128]{4,3,2,1,0:T(8,128)(2,1)}, bf16[3,3,32,16,128]{4,3,2,1,0:T(8,128)(2,1)}, u32[]{:S(2)}, u32[]{:S(2)}) collective-permute-start(bf16[3,3,32,16,128]{4,3,2,1,0:T(8,128)(2,1)} %get-tuple-element.119), channel_id=1, source_target_pairs={{0,1},{1,2},{2,3},{4,5},{5,6},{6,7}} | collective-permute-start | bytes 3538952 | tf_op jit(solution)/shard_map/ppermute | solution.py:411
  361.4 27.0 %collective-permute-start.29 = (bf16[3,3,32,16,128]{4,3,2,1,0:T(8,128)(2,1)}, bf16[3,3,32,16,128]{4,3,2,1,0:T(8,128)(2,1)}, u32[]{:S(2)}, u32[]{:S(2)}) collective-permute-start(bf16[3,3,32,16,128]{4,3,2,1,0:T(8,128)(2,1)} %get-tuple-element.120), channel_id=1, source_target_pairs={{1,0},{2,1},{3,2},{5,4},{6,5},{7,6}} | collective-permute-start | bytes 3538952 | tf_op jit(solution)/shard_map/ppermute | solution.py:412
  364.3 78.5 %collective-permute-start.20 = (bf16[3,13,32,16,128]{4,3,2,1,0:T(8,128)(2,1)}, bf16[3,13,32,16,128]{4,3,2,1,0:T(8,128)(2,1)}, u32[]{:S(2)}, u32[]{:S(2)}) collective-permute-start(bf16[3,13,32,16,128]{4,3,2,1,0:T(8,128)(2,1)} %get-tuple-element.107), channel_id=1, source_target_pairs={{0,1},{1,2},{2,3},{4,5},{5,6},{6,7}} | collective-permute-start | bytes 15335432 | tf_op jit(solution)/shard_map/ppermute | solution.py:411
  367.0 79.0 %collective-permute-start.21 = (bf16[3,13,32,16,128]{4,3,2,1,0:T(8,128)(2,1)}, bf16[3,13,32,16,128]{4,3,2,1,0:T(8,128)(2,1)}, u32[]{:S(2)}, u32[]{:S(2)}) collective-permute-start(bf16[3,13,32,16,128]{4,3,2,1,0:T(8,128)(2,1)} %get-tuple-element.108), channel_id=1, source_target_pairs={{1,0},{2,1},{3,2},{5,4},{6,5},{7,6}} | collective-permute-start | bytes 15335432 | tf_op jit(solution)/shard_map/ppermute | solution.py:412
  394.3 81.2 %collective-permute-start.30 = (bf16[8,3,32,16,128]{4,3,2,1,0:T(8,128)(2,1)}, bf16[8,3,32,16,128]{4,3,2,1,0:T(8,128)(2,1)}, u32[]{:S(2)}, u32[]{:S(2)}) collective-permute-start(bf16[8,3,32,16,128]{4,3,2,1,0:T(8,128)(2,1)} %shard_map.64.edge_ref), channel_id=1, source_target_pairs={{0,4},{4,0},{1,5},{5,1},{2,6},{6,2},{3,7},{7,3}} | collective-permute-start | bytes 9437192 | tf_op jit(solution)/shard_map/ppermute | solution.py:432
  438.4 28.8 %collective-permute-start.22 = (bf16[3,3,32,16,128]{4,3,2,1,0:T(8,128)(2,1)}, bf16[3,3,32,16,128]{4,3,2,1,0:T(8,128)(2,1)S(1)}, u32[]{:S(2)}, u32[]{:S(2)}) collective-permute-start(bf16[3,3,32,16,128]{4,3,2,1,0:T(8,128)(2,1)} %get-tuple-element.110), channel_id=1, source_target_pairs={{0,1},{1,2},{2,3},{4,5},{5,6},{6,7}} | collective-permute-start | bytes 3538952 | tf_op jit(solution)/shard_map/ppermute | solution.py:411
  440.4 26.9 %collective-permute-start.23 = (bf16[3,3,32,16,128]{4,3,2,1,0:T(8,128)(2,1)}, bf16[3,3,32,16,128]{4,3,2,1,0:T(8,128)(2,1)S(1)}, u32[]{:S(2)}, u32[]{:S(2)}) collective-permute-start(bf16[3,3,32,16,128]{4,3,2,1,0:T(8,128)(2,1)} %get-tuple-element.111), channel_id=1, source_target_pairs={{1,0},{2,1},{3,2},{5,4},{6,5},{7,6}} | collective-permute-start | bytes 3538952 | tf_op jit(solution)/shard_map/ppermute | solution.py:412
  442.9 68.3 %collective-permute-start.24 = (bf16[3,13,32,16,128]{4,3,2,1,0:T(8,128)(2,1)}, bf16[3,13,32,16,128]{4,3,2,1,0:T(8,128)(2,1)}, u32[]{:S(2)}, u32[]{:S(2)}) collective-permute-start(bf16[3,13,32,16,128]{4,3,2,1,0:T(8,128)(2,1)} %get-tuple-element.113), channel_id=1, source_target_pairs={{0,1},{1,2},{2,3},{4,5},{5,6},{6,7}} | collective-permute-start | bytes 15335432 | tf_op jit(solution)/shard_map/ppermute | solution.py:411
  446.0 67.2 %collective-permute-start.25 = (bf16[3,13,32,16,128]{4,3,2,1,0:T(8,128)(2,1)}, bf16[3,13,32,16,128]{4,3,2,1,0:T(8,128)(2,1)}, u32[]{:S(2)}, u32[]{:S(2)}) collective-permute-start(bf16[3,13,32,16,128]{4,3,2,1,0:T(8,128)(2,1)} %get-tuple-element.114), channel_id=1, source_target_pairs={{1,0},{2,1},{3,2},{5,4},{6,5},{7,6}} | collective-permute-start | bytes 15335432 | tf_op jit(solution)/shard_map/ppermute | solution.py:412
  475.3 70.0 %collective-permute-start.26 = (bf16[8,3,32,16,128]{4,3,2,1,0:T(8,128)(2,1)}, bf16[8,3,32,16,128]{4,3,2,1,0:T(8,128)(2,1)S(1)}, u32[]{:S(2)}, u32[]{:S(2)}) collective-permute-start(bf16[8,3,32,16,128]{4,3,2,1,0:T(8,128)(2,1)} %shard_map.61.edge_ref), channel_id=1, source_target_pairs={{0,4},{4,0},{1,5},{5,1},{2,6},{6,2},{3,7},{7,3}} | collective-permute-start | bytes 9437192 | tf_op jit(solution)/shard_map/ppermute | solution.py:432
  511.1 71.8 %collective-permute-start.31 = (bf16[8,8,32,16,128]{4,3,2,1,0:T(8,128)(2,1)}, bf16[8,8,32,16,128]{4,3,2,1,0:T(8,128)(2,1)}, u32[]{:S(2)}, u32[]{:S(2)}) collective-permute-start(bf16[8,8,32,16,128]{4,3,2,1,0:T(8,128)(2,1)} %get-tuple-element.124), channel_id=1, source_target_pairs={{0,1},{1,0},{2,3},{3,2},{4,5},{5,4},{6,7},{7,6}} | collective-permute-start | bytes 25165832 | tf_op jit(solution)/shard_map/ppermute | solution.py:454
  582.5 33.0 %collective-permute-start.27 = (bf16[8,8,32,16,128]{4,3,2,1,0:T(8,128)(2,1)}, bf16[8,8,32,16,128]{4,3,2,1,0:T(8,128)(2,1)}, u32[]{:S(2)}, u32[]{:S(2)}) collective-permute-start(bf16[8,8,32,16,128]{4,3,2,1,0:T(8,128)(2,1)} %get-tuple-element.117), channel_id=1, source_target_pairs={{0,1},{1,0},{2,3},{3,2},{4,5},{5,4},{6,7},{7,6}} | collective-permute-start | bytes 25165832 | tf_op jit(solution)/shard_map/ppermute | solution.py:454
  (11 other events, 109.5 us)

commit v4 on v3

--- a/solution.py
+++ b/solution.py
@@ -82,8 +82,8 @@
 
 def enter_kernel(vol_idx, own_ref, raw_ref, perm_ref, band_ref, vol_ref, near_ref, deep_ref, upn_ref, upd_ref, dnn_ref,
                  dnd_ref, scratch, landing, sent, landed):
-    side, j_all, k_len = own_ref.shape[2], own_ref.shape[3], own_ref.shape[4]
-    j_len, lanes = j_all // 2, 2 * side
+    side, j_len, k_len = own_ref.shape[2], own_ref.shape[3], own_ref.shape[4]
+    lanes = 2 * side
     me = lax.axis_index('px')
     step, steps = pl.program_id(0), landing.shape[0]
 
@@ -103,10 +103,9 @@
             to_partner(c).start()
 
     to_partner(step).wait_recv()
-    own_rows = pl.ds(pl.multiple_of(me * j_len, j_len), j_len)
 
     def fill(n, _):
-        mine = interleave(own_ref[0, 0, n, own_rows], own_ref[0, 1, n, own_rows])
+        mine = interleave(own_ref[0, 0, n], own_ref[0, 1, n])
         theirs = interleave(landing[step, 0, n], landing[step, 1, n])
         for base, pair in ((me * side, mine), ((1 - me) * side, theirs)):
             scratch[pl.ds(pl.multiple_of((base + n) * PITCH, 8), j_len), :] = pair.astype(F32)
@@ -155,7 +154,7 @@
         out_shape=[shape_of(*s, chans, ROWS, 2 * side) for s in sizes],
         grid=(steps,),
         in_specs=[
-            pl.BlockSpec((1, 2, side, j_all, k_len), lambda c: (vol_idx, c, 0, 0, 0)),
+            pl.BlockSpec((1, 2, side, j_len, k_len), lambda c: (vol_idx, c, 0, lax.axis_index('px'), 0)),
             pl.BlockSpec(memory_space=pl.ANY),
             pl.BlockSpec(perm.shape, lambda c: (0, 0)),
             pl.BlockSpec((None,) + band.shape[1:], lambda c: (0, 0, 0)),
@@ -204,7 +203,7 @@
             raw_ref[0, 1, n, at] = pair[:, k_len:]
         return 0
 
-    lax.fori_loop(0, side, drain, 0, unroll=16)
+    lax.fori_loop(0, side, drain, 0, unroll=32)
 
 
 def leave(own, other, vol_idx, result, half, perm, full_shape):
@@ -246,7 +245,7 @@
                 out_ref[:, k, first + m] = total[:, m * lanes:(m + 1) * lanes].reshape(-1, ROWS, lanes)
         return 0
 
-    lax.fori_loop(0, count, group, 0)
+    lax.fori_loop(0, count, group, 0, unroll=count if count > low_ref.shape[0] else 1)
 
 
 def along_j(field, low, high, band, layer):
@@ -315,7 +314,7 @@
             new_ref[0, k0], new_ref[0, k1] = shaped(new[:, :lanes]), shaped(new[:, lanes:])
         return 0
 
-    lax.fori_loop(0, groups // 2, group_pair, 0, unroll=4)
+    lax.fori_loop(0, groups // 2, group_pair, 0, unroll=8)
 
     if not last:
         iband_ref, new_ref, near_ref, deep_ref, upn_ref, upd_ref, dnn_ref, dnd_ref = refs[:8]

time: 652 us -> 627 us (0.962)
  the two profiles are of different devices: /device:TPU:1 before, /device:TPU:0 now
where the time goes in v4:
time: 627 us; the launch traced here: 615 us
  Pallas kernels  486 us (78%)
  starting transfers between devices  86.6 us (14%)
  waiting for transfers between devices  24.6 us (4%)
  local copies, waits for them, and re-layouts  12.8 us (2%)
    pallas_call x6, Pallas kernels, finish(): pl.pallas_call(functools.partial(finish_kernel, last), out_shape=out_shap...  219 us
    pallas_call x12, Pallas kernels, along_j(): pl.pallas_call(along_j_kernel, out_shape=shape_of(*field.shape), grid=(ch...  116 us
    pallas_call x2, Pallas kernels, enter(): pl.pallas_call(functools.partial(enter_kernel, vol_idx), out_shape=[shape...  81.9 us
    ppermute x12, starting transfers between devices, local_layers(): up = lambda a: lax.ppermute(a, ('py', 'px'), upward)  64 us
    pallas_call x2, Pallas kernels, leave(): pl.pallas_call(leave_kernel, out_shape=shape_of(*full_shape), grid_spec=p...  63 us
    ppermute x6, waiting for transfers between devices, edge_of(): return (edge, lax.ppermute(edge, 'pz', swap), after)  24.6 us
    ppermute x12, starting transfers between devices, local_layers(): down = lambda a: lax.ppermute(a, ('py', 'px'), downward)  15.6 us
  transfers between devices with their start and end apart: 32, of which 1 were waited for; matrix products, arithmetic and copies ran while one was open for 1% of the time, Pallas kernels for 67%

profile of v4, /device:TPU:0, one launch (start us, length us, event | category | flops | bytes accessed | tf_op | source)
XLA Modules:
  0.0 614.7 jit_solution(833475680280068177)
XLA Ops:
  1.3 5.2 bands.1
  7.6 36.7 %shard_map.47 = (bf16[8,16,32,16,128]{4,3,2,1,0:T(8,128)(2,1)}, bf16[8,3,32,16,128]{4,3,2,1,0:T(8,128)(2,1)}, bf16[8,13,32,16,128]{4,3,2,1,0:T(8,128)(2,1)}, bf1...) custom-call(bf16[2,32,64,64,64]{4,3,2,1,0:T(8,128)(2,1)} %raw_ref.3,, ...), custom_call_target="tpu_custom_call" | custom-call | flops 32000000000 | bytes 80000000 | tf_op jit(solution)/shard_map/pallas_call | solution.py:152
  48.1 7.4 %collective-permute-start = (bf16[3,13,32,16,128]{4,3,2,1,0:T(8,128)(2,1)}, bf16[3,13,32,16,128]{4,3,2,1,0:T(8,128)(2,1)}, u32[]{:S(2)}, u32[]{:S(2)}) collective-permute-start(bf16[3,13,32,16,128]{4,3,2,1,0:T(8,128)(2,1)} %get-tuple-element.68), channel_id=1, source_target_pairs={{0,1},{1,2},{2,3},{4,5},{5,6},{6,7}} | collective-permute-start | bytes 15335432 | tf_op jit(solution)/shard_map/ppermute | solution.py:410
  58.3 6.0 shard_map.50.edge_ref
  65.7 45.3 %shard_map.46 = (bf16[8,16,32,16,128]{4,3,2,1,0:T(8,128)(2,1)}, bf16[8,3,32,16,128]{4,3,2,1,0:T(8,128)(2,1)}, bf16[8,13,32,16,128]{4,3,2,1,0:T(8,128)(2,1)}, bf1...) custom-call(bf16[2,32,64,64,64]{4,3,2,1,0:T(8,128)(2,1)} %raw_ref.3,, ...), custom_call_target="tpu_custom_call" | custom-call | flops 32000000000 | bytes 80000000 | tf_op jit(solution)/shard_map/pallas_call | solution.py:152
  118.8 5.4 collective-permute-start.7
  125.5 13.4 %shard_map.48.rest_ref = bf16[8,13,32,16,128]{4,3,2,1,0:T(8,128)(2,1)} custom-call(bf16[8,13,32,16,128]{4,3,2,1,0:T(8,128)(2,1)} %get-tuple-element.67.field_ref, bf16[3,13,32,16,128]{4,3,2,1,0:T(8,128)(2,1)} %collective-permute-done.low_ref, bf16[3,13,32,16,128]{4,3,2,1,0:T(8,128)(2,1)} %collective-permute-done.1.high_ref, ...), custom_call_target="tpu_custom_call" | custom-call | flops 12999999488 | bytes 37700000 | tf_op jit(solution)/shard_map/pallas_call | solution.py:255
  138.9 6.0 shard_map.49.edge_ref
  146.6 38.9 %shard_map.51 = (bf16[8,16,32,16,128]{4,3,2,1,0:T(8,128)(2,1)}, bf16[8,3,32,16,128]{4,3,2,1,0:T(8,128)(2,1)}, bf16[8,13,32,16,128]{4,3,2,1,0:T(8,128)(2,1)}, bf1...) custom-call(bf16[8,3,32,16,128]{4,3,2,1,0:T(8,128)(2,1)} %shard_map., ...), custom_call_target="tpu_custom_call" | custom-call | flops 40000000000 | bytes 75000000 | tf_op jit(solution)/shard_map/pallas_call | solution.py:371
  185.5 3.8 collective-permute-start.14
  190.6 16.2 %collective-permute-start.10 = (bf16[3,13,32,16,128]{4,3,2,1,0:T(8,128)(2,1)}, bf16[3,13,32,16,128]{4,3,2,1,0:T(8,128)(2,1)}, u32[]{:S(2)}, u32[]{:S(2)}) collective-permute-start(bf16[3,13,32,16,128]{4,3,2,1,0:T(8,128)(2,1)} %get-tuple-element.89), channel_id=1, source_target_pairs={{0,1},{1,2},{2,3},{4,5},{5,6},{6,7}} | collective-permute-start | bytes 15335432 | tf_op jit(solution)/shard_map/ppermute | solution.py:410
  208.1 13.4 %shard_map.52.rest_ref = bf16[8,13,32,16,128]{4,3,2,1,0:T(8,128)(2,1)} custom-call(bf16[8,13,32,16,128]{4,3,2,1,0:T(8,128)(2,1)} %get-tuple-element.82.field_ref, bf16[3,13,32,16,128]{4,3,2,1,0:T(8,128)(2,1)} %collective-permute-done.7.low_ref, bf16[3,13,32,16,128]{4,3,2,1,0:T(8,128)(2,1)} %collective-permute-done.8.high_ref, ...), custom_call_target="tpu_custom_call" | custom-call | flops 12999999488 | bytes 37700000 | tf_op jit(solution)/shard_map/pallas_call | solution.py:255
  221.5 6.0 shard_map.56.edge_ref
  230.6 39.1 %shard_map.53 = (bf16[8,16,32,16,128]{4,3,2,1,0:T(8,128)(2,1)}, bf16[8,3,32,16,128]{4,3,2,1,0:T(8,128)(2,1)}, bf16[8,13,32,16,128]{4,3,2,1,0:T(8,128)(2,1)}, bf1...) custom-call(bf16[8,3,32,16,128]{4,3,2,1,0:T(8,128)(2,1)} %shard_map., ...), custom_call_target="tpu_custom_call" | custom-call | flops 40000000000 | bytes 75000000 | tf_op jit(solution)/shard_map/pallas_call | solution.py:371
  273.9 5.3 collective-permute-start.17
  280.4 13.4 %shard_map.54.rest_ref = bf16[8,13,32,16,128]{4,3,2,1,0:T(8,128)(2,1)} custom-call(bf16[8,13,32,16,128]{4,3,2,1,0:T(8,128)(2,1)} %get-tuple-element.88.field_ref, bf16[3,13,32,16,128]{4,3,2,1,0:T(8,128)(2,1)} %collective-permute-done.10.low_ref, bf16[3,13,32,16,128]{4,3,2,1,0:T(8,128)(2,1)} %collective-permute-done.11.high_ref, ...), custom_call_target="tpu_custom_call" | custom-call | flops 12999999488 | bytes 37700000 | tf_op jit(solution)/shard_map/pallas_call | solution.py:255
  295.9 5.9 shard_map.55.edge_ref
  302.4 39.0 %shard_map.57 = (bf16[8,16,32,16,128]{4,3,2,1,0:T(8,128)(2,1)}, bf16[8,3,32,16,128]{4,3,2,1,0:T(8,128)(2,1)}, bf16[8,13,32,16,128]{4,3,2,1,0:T(8,128)(2,1)}, bf1...) custom-call(bf16[8,3,32,16,128]{4,3,2,1,0:T(8,128)(2,1)} %shard_map., ...), custom_call_target="tpu_custom_call" | custom-call | flops 40000000000 | bytes 75000000 | tf_op jit(solution)/shard_map/pallas_call | solution.py:371
  341.3 3.8 collective-permute-start.28
  346.4 5.3 collective-permute-start.20
  353.0 13.4 %shard_map.58.rest_ref = bf16[8,13,32,16,128]{4,3,2,1,0:T(8,128)(2,1)} custom-call(bf16[8,13,32,16,128]{4,3,2,1,0:T(8,128)(2,1)} %get-tuple-element.100.field_ref, bf16[3,13,32,16,128]{4,3,2,1,0:T(8,128)(2,1)} %collective-permute-done.17.low_ref, bf16[3,13,32,16,128]{4,3,2,1,0:T(8,128)(2,1)} %collective-permute-done.18.high_ref, ...), custom_call_target="tpu_custom_call" | custom-call | flops 12999999488 | bytes 37700000 | tf_op jit(solution)/shard_map/pallas_call | solution.py:255
  366.4 6.0 shard_map.64.edge_ref
  375.5 38.9 %shard_map.59 = (bf16[8,16,32,16,128]{4,3,2,1,0:T(8,128)(2,1)}, bf16[8,3,32,16,128]{4,3,2,1,0:T(8,128)(2,1)}, bf16[8,13,32,16,128]{4,3,2,1,0:T(8,128)(2,1)}, bf1...) custom-call(bf16[8,3,32,16,128]{4,3,2,1,0:T(8,128)(2,1)} %shard_map., ...), custom_call_target="tpu_custom_call" | custom-call | flops 40000000000 | bytes 75000000 | tf_op jit(solution)/shard_map/pallas_call | solution.py:371
  418.5 5.3 collective-permute-start.24
  425.3 13.5 %shard_map.60.rest_ref = bf16[8,13,32,16,128]{4,3,2,1,0:T(8,128)(2,1)} custom-call(bf16[8,13,32,16,128]{4,3,2,1,0:T(8,128)(2,1)} %get-tuple-element.106.field_ref, bf16[3,13,32,16,128]{4,3,2,1,0:T(8,128)(2,1)} %collective-permute-done.20.low_ref, bf16[3,13,32,16,128]{4,3,2,1,0:T(8,128)(2,1)} %collective-permute-done.21.high_ref, ...), custom_call_target="tpu_custom_call" | custom-call | flops 12999999488 | bytes 37700000 | tf_op jit(solution)/shard_map/pallas_call | solution.py:255
  440.8 6.0 shard_map.61.edge_ref
  447.3 31.7 %shard_map.65 = (bf16[8,8,32,16,128]{4,3,2,1,0:T(8,128)(2,1)}, bf16[8,8,32,16,128]{4,3,2,1,0:T(8,128)(2,1)}) custom-call(bf16[8,3,32,16,128]{4,3,2,1,0:T(8,128)(2,1)} %shard_map.64.edge_ref, bf16[8,13,32,16,128]{4,3,2,1,0:T(8,128)(2,1)} %shard_map.60.rest_ref, bf16[8,3,32,16,128]{4,3,2,1,0:T(8,128)(2,1)} %collective-permute-done.30.halo_ref, ...), custom_call_target="tpu_custom_call" | custom-call | flops 40000000000 | bytes 75000000 | tf_op jit(solution)/shard_map/pallas_call | solution.py:371
  479.9 13.4 %shard_map.62.rest_ref = bf16[8,13,32,16,128]{4,3,2,1,0:T(8,128)(2,1)} custom-call(bf16[8,13,32,16,128]{4,3,2,1,0:T(8,128)(2,1)} %get-tuple-element.112.field_ref, bf16[3,13,32,16,128]{4,3,2,1,0:T(8,128)(2,1)} %collective-permute-done.24.low_ref, bf16[3,13,32,16,128]{4,3,2,1,0:T(8,128)(2,1)} %collective-permute-done.25.high_ref, ...), custom_call_target="tpu_custom_call" | custom-call | flops 12999999488 | bytes 37700000 | tf_op jit(solution)/shard_map/pallas_call | solution.py:255
  493.3 24.5 %collective-permute-done.26.halo_ref = bf16[8,3,32,16,128]{4,3,2,1,0:T(8,128)(2,1)S(1)} collective-permute-done((bf16[8,3,32,16,128]{4,3,2,1,0:T(8,128)(2,1)}, bf16[8,3,32,16,128]{4,3,2,1,0:T(8,128)(2,1)S(1)}, u32[]{:S(2)}, u32[]{:S(2)}) %collective-permute-start.26) | collective-permute-done | bytes 3145760 | tf_op jit(solution)/shard_map/ppermute | solution.py:431
  519.5 31.7 %shard_map.63 = (bf16[8,8,32,16,128]{4,3,2,1,0:T(8,128)(2,1)}, bf16[8,8,32,16,128]{4,3,2,1,0:T(8,128)(2,1)}) custom-call(bf16[8,3,32,16,128]{4,3,2,1,0:T(8,128)(2,1)} %shard_map.61.edge_ref, bf16[8,13,32,16,128]{4,3,2,1,0:T(8,128)(2,1)} %shard_map.62.rest_ref, bf16[8,3,32,16,128]{4,3,2,1,0:T(8,128)(2,1)} %copy-done.4, ...), custom_call_target="tpu_custom_call" | custom-call | flops 40000000000 | bytes 75000000 | tf_op jit(solution)/shard_map/pallas_call | solution.py:371
  551.3 31.5 %shard_map.66.refs_0_ = bf16[2,32,64,64,64]{4,3,2,1,0:T(8,128)(2,1)} custom-call(s32[1]{0:T(128)} %bitcast.half_ref, bf16[8,8,32,16,128]{4,3,2,1,0:T(8,128)(2,1)} %get-tuple-element.123.own_ref, bf16[8,8,32,16,128]{4,3,2,1,0:T(8,128)(2,1)} %collective-permute-done.31.other_ref, bf16[256,256]{1,0:T(8,128)(2,1)} %get-tuple-element.125.perm_ref), custom_call_target="tpu_custom_call" | custom-call | flops 30000001024 | bytes 50000000 | tf_op jit(solution)/shard_map/pallas_call | solution.py:220
  582.8 31.5 %shard_map.67 = bf16[2,32,64,64,64]{4,3,2,1,0:T(8,128)(2,1)} custom-call(s32[1]{0:T(128)} %bitcast.half_ref, bf16[8,8,32,16,128]{4,3,2,1,0:T(8,128)(2,1)} %get-tuple-element.116.own_ref, bf16[8,8,32,16,128]{4,3,2,1,0:T(8,128)(2,1)} %collective-permute-done.27.other_ref, ...), custom_call_target="tpu_custom_call", output_to_operand_aliasing={{}: (4, {})} | custom-call | flops 30000001024 | bytes 50000000 | tf_op jit(solution)/shard_map/pallas_call | solution.py:220
  (96 shorter events, 51.2 us)
Async XLA Ops:
  44.3 12.5 %collective-permute-start.4 = (bf16[3,3,32,16,128]{4,3,2,1,0:T(8,128)(2,1)}, bf16[3,3,32,16,128]{4,3,2,1,0:T(8,128)(2,1)S(1)}, u32[]{:S(2)}, u32[]{:S(2)}) collective-permute-start(bf16[3,3,32,16,128]{4,3,2,1,0:T(8,128)(2,1)} %get-tuple-element.75), channel_id=1, source_target_pairs={{0,1},{1,2},{2,3},{4,5},{5,6},{6,7}} | collective-permute-start | bytes 3538952 | tf_op jit(solution)/shard_map/ppermute | solution.py:410
  46.8 10.0 %collective-permute-start.5 = (bf16[3,3,32,16,128]{4,3,2,1,0:T(8,128)(2,1)}, bf16[3,3,32,16,128]{4,3,2,1,0:T(8,128)(2,1)S(1)}, u32[]{:S(2)}, u32[]{:S(2)}) collective-permute-start(bf16[3,3,32,16,128]{4,3,2,1,0:T(8,128)(2,1)} %get-tuple-element.76), channel_id=1, source_target_pairs={{1,0},{2,1},{3,2},{5,4},{6,5},{7,6}} | collective-permute-start | bytes 3538952 | tf_op jit(solution)/shard_map/ppermute | solution.py:411
  48.1 70.7 %collective-permute-start = (bf16[3,13,32,16,128]{4,3,2,1,0:T(8,128)(2,1)}, bf16[3,13,32,16,128]{4,3,2,1,0:T(8,128)(2,1)}, u32[]{:S(2)}, u32[]{:S(2)}) collective-permute-start(bf16[3,13,32,16,128]{4,3,2,1,0:T(8,128)(2,1)} %get-tuple-element.68), channel_id=1, source_target_pairs={{0,1},{1,2},{2,3},{4,5},{5,6},{6,7}} | collective-permute-start | bytes 15335432 | tf_op jit(solution)/shard_map/ppermute | solution.py:410
  55.5 68.7 %collective-permute-start.1 = (bf16[3,13,32,16,128]{4,3,2,1,0:T(8,128)(2,1)}, bf16[3,13,32,16,128]{4,3,2,1,0:T(8,128)(2,1)}, u32[]{:S(2)}, u32[]{:S(2)}) collective-permute-start(bf16[3,13,32,16,128]{4,3,2,1,0:T(8,128)(2,1)} %get-tuple-element.69), channel_id=1, source_target_pairs={{1,0},{2,1},{3,2},{5,4},{6,5},{7,6}} | collective-permute-start | bytes 15335432 | tf_op jit(solution)/shard_map/ppermute | solution.py:411
  64.2 81.2 %collective-permute-start.6 = (bf16[8,3,32,16,128]{4,3,2,1,0:T(8,128)(2,1)}, bf16[8,3,32,16,128]{4,3,2,1,0:T(8,128)(2,1)}, u32[]{:S(2)}, u32[]{:S(2)}) collective-permute-start(bf16[8,3,32,16,128]{4,3,2,1,0:T(8,128)(2,1)} %shard_map.50.edge_ref), channel_id=1, source_target_pairs={{0,4},{4,0},{1,5},{5,1},{2,6},{6,2},{3,7},{7,3}} | collective-permute-start | bytes 9437192 | tf_op jit(solution)/shard_map/ppermute | solution.py:431
  111.0 27.9 %collective-permute-start.2 = (bf16[3,3,32,16,128]{4,3,2,1,0:T(8,128)(2,1)}, bf16[3,3,32,16,128]{4,3,2,1,0:T(8,128)(2,1)}, u32[]{:S(2)}, u32[]{:S(2)}) collective-permute-start(bf16[3,3,32,16,128]{4,3,2,1,0:T(8,128)(2,1)} %get-tuple-element.72), channel_id=1, source_target_pairs={{0,1},{1,2},{2,3},{4,5},{5,6},{6,7}} | collective-permute-start | bytes 3538952 | tf_op jit(solution)/shard_map/ppermute | solution.py:410
  114.5 24.5 %collective-permute-start.3 = (bf16[3,3,32,16,128]{4,3,2,1,0:T(8,128)(2,1)}, bf16[3,3,32,16,128]{4,3,2,1,0:T(8,128)(2,1)}, u32[]{:S(2)}, u32[]{:S(2)}) collective-permute-start(bf16[3,3,32,16,128]{4,3,2,1,0:T(8,128)(2,1)} %get-tuple-element.73), channel_id=1, source_target_pairs={{1,0},{2,1},{3,2},{5,4},{6,5},{7,6}} | collective-permute-start | bytes 3538952 | tf_op jit(solution)/shard_map/ppermute | solution.py:411
  118.8 71.7 %collective-permute-start.7 = (bf16[3,13,32,16,128]{4,3,2,1,0:T(8,128)(2,1)}, bf16[3,13,32,16,128]{4,3,2,1,0:T(8,128)(2,1)}, u32[]{:S(2)}, u32[]{:S(2)}) collective-permute-start(bf16[3,13,32,16,128]{4,3,2,1,0:T(8,128)(2,1)} %get-tuple-element.83), channel_id=1, source_target_pairs={{0,1},{1,2},{2,3},{4,5},{5,6},{6,7}} | collective-permute-start | bytes 15335432 | tf_op jit(solution)/shard_map/ppermute | solution.py:410
  124.2 82.6 %collective-permute-start.8 = (bf16[3,13,32,16,128]{4,3,2,1,0:T(8,128)(2,1)}, bf16[3,13,32,16,128]{4,3,2,1,0:T(8,128)(2,1)}, u32[]{:S(2)}, u32[]{:S(2)}) collective-permute-start(bf16[3,13,32,16,128]{4,3,2,1,0:T(8,128)(2,1)} %get-tuple-element.84), channel_id=1, source_target_pairs={{1,0},{2,1},{3,2},{5,4},{6,5},{7,6}} | collective-permute-start | bytes 15335432 | tf_op jit(solution)/shard_map/ppermute | solution.py:411
  144.9 84.0 %collective-permute-start.9 = (bf16[8,3,32,16,128]{4,3,2,1,0:T(8,128)(2,1)}, bf16[8,3,32,16,128]{4,3,2,1,0:T(8,128)(2,1)S(1)}, u32[]{:S(2)}, u32[]{:S(2)}) collective-permute-start(bf16[8,3,32,16,128]{4,3,2,1,0:T(8,128)(2,1)} %shard_map.49.edge_ref), channel_id=1, source_target_pairs={{0,4},{4,0},{1,5},{5,1},{2,6},{6,2},{3,7},{7,3}} | collective-permute-start | bytes 9437192 | tf_op jit(solution)/shard_map/ppermute | solution.py:431
  185.5 36.0 %collective-permute-start.14 = (bf16[3,3,32,16,128]{4,3,2,1,0:T(8,128)(2,1)}, bf16[3,3,32,16,128]{4,3,2,1,0:T(8,128)(2,1)}, u32[]{:S(2)}, u32[]{:S(2)}) collective-permute-start(bf16[3,3,32,16,128]{4,3,2,1,0:T(8,128)(2,1)} %get-tuple-element.95), channel_id=1, source_target_pairs={{0,1},{1,2},{2,3},{4,5},{5,6},{6,7}} | collective-permute-start | bytes 3538952 | tf_op jit(solution)/shard_map/ppermute | solution.py:410
  189.3 32.2 %collective-permute-start.15 = (bf16[3,3,32,16,128]{4,3,2,1,0:T(8,128)(2,1)}, bf16[3,3,32,16,128]{4,3,2,1,0:T(8,128)(2,1)}, u32[]{:S(2)}, u32[]{:S(2)}) collective-permute-start(bf16[3,3,32,16,128]{4,3,2,1,0:T(8,128)(2,1)} %get-tuple-element.96), channel_id=1, source_target_pairs={{1,0},{2,1},{3,2},{5,4},{6,5},{7,6}} | collective-permute-start | bytes 3538952 | tf_op jit(solution)/shard_map/ppermute | solution.py:411
  190.6 83.3 %collective-permute-start.10 = (bf16[3,13,32,16,128]{4,3,2,1,0:T(8,128)(2,1)}, bf16[3,13,32,16,128]{4,3,2,1,0:T(8,128)(2,1)}, u32[]{:S(2)}, u32[]{:S(2)}) collective-permute-start(bf16[3,13,32,16,128]{4,3,2,1,0:T(8,128)(2,1)} %get-tuple-element.89), channel_id=1, source_target_pairs={{0,1},{1,2},{2,3},{4,5},{5,6},{6,7}} | collective-permute-start | bytes 15335432 | tf_op jit(solution)/shard_map/ppermute | solution.py:410
  206.8 72.4 %collective-permute-start.11 = (bf16[3,13,32,16,128]{4,3,2,1,0:T(8,128)(2,1)}, bf16[3,13,32,16,128]{4,3,2,1,0:T(8,128)(2,1)}, u32[]{:S(2)}, u32[]{:S(2)}) collective-permute-start(bf16[3,13,32,16,128]{4,3,2,1,0:T(8,128)(2,1)} %get-tuple-element.90), channel_id=1, source_target_pairs={{1,0},{2,1},{3,2},{5,4},{6,5},{7,6}} | collective-permute-start | bytes 15335432 | tf_op jit(solution)/shard_map/ppermute | solution.py:411
  227.5 74.9 %collective-permute-start.16 = (bf16[8,3,32,16,128]{4,3,2,1,0:T(8,128)(2,1)}, bf16[8,3,32,16,128]{4,3,2,1,0:T(8,128)(2,1)}, u32[]{:S(2)}, u32[]{:S(2)}) collective-permute-start(bf16[8,3,32,16,128]{4,3,2,1,0:T(8,128)(2,1)} %shard_map.56.edge_ref), channel_id=1, source_target_pairs={{0,4},{4,0},{1,5},{5,1},{2,6},{6,2},{3,7},{7,3}} | collective-permute-start | bytes 9437192 | tf_op jit(solution)/shard_map/ppermute | solution.py:431
  269.7 24.1 %collective-permute-start.12 = (bf16[3,3,32,16,128]{4,3,2,1,0:T(8,128)(2,1)}, bf16[3,3,32,16,128]{4,3,2,1,0:T(8,128)(2,1)S(1)}, u32[]{:S(2)}, u32[]{:S(2)}) collective-permute-start(bf16[3,3,32,16,128]{4,3,2,1,0:T(8,128)(2,1)} %get-tuple-element.92), channel_id=1, source_target_pairs={{0,1},{1,2},{2,3},{4,5},{5,6},{6,7}} | collective-permute-start | bytes 3538952 | tf_op jit(solution)/shard_map/ppermute | solution.py:410
  272.6 21.3 %collective-permute-start.13 = (bf16[3,3,32,16,128]{4,3,2,1,0:T(8,128)(2,1)}, bf16[3,3,32,16,128]{4,3,2,1,0:T(8,128)(2,1)S(1)}, u32[]{:S(2)}, u32[]{:S(2)}) collective-permute-start(bf16[3,3,32,16,128]{4,3,2,1,0:T(8,128)(2,1)} %get-tuple-element.93), channel_id=1, source_target_pairs={{1,0},{2,1},{3,2},{5,4},{6,5},{7,6}} | collective-permute-start | bytes 3538952 | tf_op jit(solution)/shard_map/ppermute | solution.py:411
  273.9 72.5 %collective-permute-start.17 = (bf16[3,13,32,16,128]{4,3,2,1,0:T(8,128)(2,1)}, bf16[3,13,32,16,128]{4,3,2,1,0:T(8,128)(2,1)}, u32[]{:S(2)}, u32[]{:S(2)}) collective-permute-start(bf16[3,13,32,16,128]{4,3,2,1,0:T(8,128)(2,1)} %get-tuple-element.101), channel_id=1, source_target_pairs={{0,1},{1,2},{2,3},{4,5},{5,6},{6,7}} | collective-permute-start | bytes 15335432 | tf_op jit(solution)/shard_map/ppermute | solution.py:410
  279.1 72.5 %collective-permute-start.18 = (bf16[3,13,32,16,128]{4,3,2,1,0:T(8,128)(2,1)}, bf16[3,13,32,16,128]{4,3,2,1,0:T(8,128)(2,1)}, u32[]{:S(2)}, u32[]{:S(2)}) collective-permute-start(bf16[3,13,32,16,128]{4,3,2,1,0:T(8,128)(2,1)} %get-tuple-element.102), channel_id=1, source_target_pairs={{1,0},{2,1},{3,2},{5,4},{6,5},{7,6}} | collective-permute-start | bytes 15335432 | tf_op jit(solution)/shard_map/ppermute | solution.py:411
  301.8 72.0 %collective-permute-start.19 = (bf16[8,3,32,16,128]{4,3,2,1,0:T(8,128)(2,1)}, bf16[8,3,32,16,128]{4,3,2,1,0:T(8,128)(2,1)S(1)}, u32[]{:S(2)}, u32[]{:S(2)}) collective-permute-start(bf16[8,3,32,16,128]{4,3,2,1,0:T(8,128)(2,1)} %shard_map.55.edge_ref), channel_id=1, source_target_pairs={{0,4},{4,0},{1,5},{5,1},{2,6},{6,2},{3,7},{7,3}} | collective-permute-start | bytes 9437192 | tf_op jit(solution)/shard_map/ppermute | solution.py:431
  341.3 25.0 %collective-permute-start.28 = (bf16[3,3,32,16,128]{4,3,2,1,0:T(8,128)(2,1)}, bf16[3,3,32,16,128]{4,3,2,1,0:T(8,128)(2,1)}, u32[]{:S(2)}, u32[]{:S(2)}) collective-permute-start(bf16[3,3,32,16,128]{4,3,2,1,0:T(8,128)(2,1)} %get-tuple-element.119), channel_id=1, source_target_pairs={{0,1},{1,2},{2,3},{4,5},{5,6},{6,7}} | collective-permute-start | bytes 3538952 | tf_op jit(solution)/shard_map/ppermute | solution.py:410
  345.1 21.3 %collective-permute-start.29 = (bf16[3,3,32,16,128]{4,3,2,1,0:T(8,128)(2,1)}, bf16[3,3,32,16,128]{4,3,2,1,0:T(8,128)(2,1)}, u32[]{:S(2)}, u32[]{:S(2)}) collective-permute-start(bf16[3,3,32,16,128]{4,3,2,1,0:T(8,128)(2,1)} %get-tuple-element.120), channel_id=1, source_target_pairs={{1,0},{2,1},{3,2},{5,4},{6,5},{7,6}} | collective-permute-start | bytes 3538952 | tf_op jit(solution)/shard_map/ppermute | solution.py:411
  346.4 72.1 %collective-permute-start.20 = (bf16[3,13,32,16,128]{4,3,2,1,0:T(8,128)(2,1)}, bf16[3,13,32,16,128]{4,3,2,1,0:T(8,128)(2,1)}, u32[]{:S(2)}, u32[]{:S(2)}) collective-permute-start(bf16[3,13,32,16,128]{4,3,2,1,0:T(8,128)(2,1)} %get-tuple-element.107), channel_id=1, source_target_pairs={{0,1},{1,2},{2,3},{4,5},{5,6},{6,7}} | collective-permute-start | bytes 15335432 | tf_op jit(solution)/shard_map/ppermute | solution.py:410
  351.7 72.1 %collective-permute-start.21 = (bf16[3,13,32,16,128]{4,3,2,1,0:T(8,128)(2,1)}, bf16[3,13,32,16,128]{4,3,2,1,0:T(8,128)(2,1)}, u32[]{:S(2)}, u32[]{:S(2)}) collective-permute-start(bf16[3,13,32,16,128]{4,3,2,1,0:T(8,128)(2,1)} %get-tuple-element.108), channel_id=1, source_target_pairs={{1,0},{2,1},{3,2},{5,4},{6,5},{7,6}} | collective-permute-start | bytes 15335432 | tf_op jit(solution)/shard_map/ppermute | solution.py:411
  372.3 75.0 %collective-permute-start.30 = (bf16[8,3,32,16,128]{4,3,2,1,0:T(8,128)(2,1)}, bf16[8,3,32,16,128]{4,3,2,1,0:T(8,128)(2,1)}, u32[]{:S(2)}, u32[]{:S(2)}) collective-permute-start(bf16[8,3,32,16,128]{4,3,2,1,0:T(8,128)(2,1)} %shard_map.64.edge_ref), channel_id=1, source_target_pairs={{0,4},{4,0},{1,5},{5,1},{2,6},{6,2},{3,7},{7,3}} | collective-permute-start | bytes 9437192 | tf_op jit(solution)/shard_map/ppermute | solution.py:431
  414.4 24.4 %collective-permute-start.22 = (bf16[3,3,32,16,128]{4,3,2,1,0:T(8,128)(2,1)}, bf16[3,3,32,16,128]{4,3,2,1,0:T(8,128)(2,1)S(1)}, u32[]{:S(2)}, u32[]{:S(2)}) collective-permute-start(bf16[3,3,32,16,128]{4,3,2,1,0:T(8,128)(2,1)} %get-tuple-element.110), channel_id=1, source_target_pairs={{0,1},{1,2},{2,3},{4,5},{5,6},{6,7}} | collective-permute-start | bytes 3538952 | tf_op jit(solution)/shard_map/ppermute | solution.py:410
  417.2 21.6 %collective-permute-start.23 = (bf16[3,3,32,16,128]{4,3,2,1,0:T(8,128)(2,1)}, bf16[3,3,32,16,128]{4,3,2,1,0:T(8,128)(2,1)S(1)}, u32[]{:S(2)}, u32[]{:S(2)}) collective-permute-start(bf16[3,3,32,16,128]{4,3,2,1,0:T(8,128)(2,1)} %get-tuple-element.111), channel_id=1, source_target_pairs={{1,0},{2,1},{3,2},{5,4},{6,5},{7,6}} | collective-permute-start | bytes 3538952 | tf_op jit(solution)/shard_map/ppermute | solution.py:411
  418.5 61.3 %collective-permute-start.24 = (bf16[3,13,32,16,128]{4,3,2,1,0:T(8,128)(2,1)}, bf16[3,13,32,16,128]{4,3,2,1,0:T(8,128)(2,1)}, u32[]{:S(2)}, u32[]{:S(2)}) collective-permute-start(bf16[3,13,32,16,128]{4,3,2,1,0:T(8,128)(2,1)} %get-tuple-element.113), channel_id=1, source_target_pairs={{0,1},{1,2},{2,3},{4,5},{5,6},{6,7}} | collective-permute-start | bytes 15335432 | tf_op jit(solution)/shard_map/ppermute | solution.py:410
  423.8 56.0 %collective-permute-start.25 = (bf16[3,13,32,16,128]{4,3,2,1,0:T(8,128)(2,1)}, bf16[3,13,32,16,128]{4,3,2,1,0:T(8,128)(2,1)}, u32[]{:S(2)}, u32[]{:S(2)}) collective-permute-start(bf16[3,13,32,16,128]{4,3,2,1,0:T(8,128)(2,1)} %get-tuple-element.114), channel_id=1, source_target_pairs={{1,0},{2,1},{3,2},{5,4},{6,5},{7,6}} | collective-permute-start | bytes 15335432 | tf_op jit(solution)/shard_map/ppermute | solution.py:411
  446.8 71.1 %collective-permute-start.26 = (bf16[8,3,32,16,128]{4,3,2,1,0:T(8,128)(2,1)}, bf16[8,3,32,16,128]{4,3,2,1,0:T(8,128)(2,1)S(1)}, u32[]{:S(2)}, u32[]{:S(2)}) collective-permute-start(bf16[8,3,32,16,128]{4,3,2,1,0:T(8,128)(2,1)} %shard_map.61.edge_ref), channel_id=1, source_target_pairs={{0,4},{4,0},{1,5},{5,1},{2,6},{6,2},{3,7},{7,3}} | collective-permute-start | bytes 9437192 | tf_op jit(solution)/shard_map/ppermute | solution.py:431
  479.0 72.3 %collective-permute-start.31 = (bf16[8,8,32,16,128]{4,3,2,1,0:T(8,128)(2,1)}, bf16[8,8,32,16,128]{4,3,2,1,0:T(8,128)(2,1)}, u32[]{:S(2)}, u32[]{:S(2)}) collective-permute-start(bf16[8,8,32,16,128]{4,3,2,1,0:T(8,128)(2,1)} %get-tuple-element.124), channel_id=1, source_target_pairs={{0,1},{1,0},{2,3},{3,2},{4,5},{5,4},{6,7},{7,6}} | collective-permute-start | bytes 25165832 | tf_op jit(solution)/shard_map/ppermute | solution.py:453
  551.2 31.6 %collective-permute-start.27 = (bf16[8,8,32,16,128]{4,3,2,1,0:T(8,128)(2,1)}, bf16[8,8,32,16,128]{4,3,2,1,0:T(8,128)(2,1)}, u32[]{:S(2)}, u32[]{:S(2)}) collective-permute-start(bf16[8,8,32,16,128]{4,3,2,1,0:T(8,128)(2,1)} %get-tuple-element.117), channel_id=1, source_target_pairs={{0,1},{1,0},{2,3},{3,2},{4,5},{5,4},{6,7},{7,6}} | collective-permute-start | bytes 25165832 | tf_op jit(solution)/shard_map/ppermute | solution.py:453
  (11 other events, 114.6 us)
